TPU v7x, 32 devices: a whole 2x2x4 slice. The times are simulated.
32 devices in a mesh: row: 16 (over z, x, core), col: 2 (over y).
Axes of the slice: x: 2, y: 2, z: 4, core: 2. Of those that a mesh axis runs over, the one named last changes fastest.
Arguments:
- pair_map: float32 [256, 256, 128], P('row', 'col'), may hold values from -6 to 6
- pair_mask: int32 [256, 256], P('row', 'col'), may hold values 0 or 1
- in_gain: float32 [128], replicated, may hold values from 0.25 to 1.75
- in_bias: float32 [128], replicated, may hold values from -3 to 3
- w_proj: bfloat16 [128, 512], replicated, may hold values from -0.5 to 0.5
- w_gate: bfloat16 [128, 128], replicated, may hold values from -0.5 to 0.5
- out_gain: float32 [128], replicated, may hold values from 0.25 to 1.75
- out_bias: float32 [128], replicated, may hold values from -3 to 3
- w_out: bfloat16 [128, 128], replicated, may hold values from -0.5 to 0.5
Outputs:
- update: float32 [256, 256, 128], P('row', 'col')
All inputs are finite; a program needn't handle non-finite values. No bound on the sum of `pair_mask` on one device may be relied on, other than what follows from the above.
Results may differ from a plain program's by a relative error of at most 0.0035.
Values may be sent and summed in bfloat16 or wider, within the bound.
No kernel may reach another device: no remote copies, remote signals or barrier semaphores. Data moves between devices by JAX's collectives and lax.ppermute only.
A program may use at most 128 MiB of HBM per device.

v0:
```python
import jax
import jax.numpy as jnp
from jax import lax
from jax.sharding import PartitionSpec as P


def layer_norm(values, gain, bias):
    average = jnp.mean(values, axis=-1, keepdims=True)
    variance = jnp.mean(jnp.square(values - average), axis=-1, keepdims=True)
    return (values - average) * lax.rsqrt(variance + 1e-05) * gain + bias


def local(pair_map, pair_mask, in_gain, in_bias, w_proj, w_gate, out_gain, out_bias, w_out):
    row_count, col_count, channels = pair_map.shape
    hidden_width = w_out.shape[0]
    normed_map = layer_norm(pair_map, in_gain, in_bias).astype(jnp.bfloat16)
    flattened = normed_map.reshape(-1, channels)
    projected_all = jnp.dot(flattened, w_proj, preferred_element_type=jnp.float32).reshape(
        row_count, col_count, 4 * hidden_width
    )
    masked = pair_mask.astype(jnp.float32)[..., None]
    left_side = (
        masked
        * jax.nn.sigmoid(projected_all[..., :hidden_width])
        * projected_all[..., hidden_width : 2 * hidden_width]
    ).astype(jnp.bfloat16)
    gating = jax.nn.sigmoid(jnp.dot(flattened, w_gate, preferred_element_type=jnp.float32)).reshape(
        row_count, col_count, channels
    )
    right_side = (
        masked
        * jax.nn.sigmoid(projected_all[..., 2 * hidden_width : 3 * hidden_width])
        * projected_all[..., 3 * hidden_width :]
    ).astype(jnp.bfloat16)
    partial_value = jnp.einsum(
        "ikc,jkc->ijc",
        left_side,
        lax.all_gather(right_side, "row", axis=0, tiled=True),
        preferred_element_type=jnp.float32,
    )
    summed = lax.psum_scatter(partial_value, "col", scatter_dimension=1, tiled=True)
    normed_sum = layer_norm(summed, out_gain, out_bias).astype(jnp.bfloat16)
    result = jnp.dot(
        normed_sum.reshape(-1, hidden_width), w_out, preferred_element_type=jnp.float32
    ).reshape(row_count, col_count, channels)
    return gating * result


def solution(mesh):
    in_specs = (P("row", "col", None), P("row", "col"), P(), P(), P(), P(), P(), P(), P())
    out_specs = P("row", "col", None)
    return jax.shard_map(local, mesh=mesh, in_specs=in_specs, out_specs=out_specs, check_vma=False)
```

profile of v0, /device:TPU:0, one launch (start us, length us, event | category | flops | bytes accessed | tf_op | source)
XLA Modules:
  0.0 154.0 jit_solution(5582246668509512168)
XLA Ops:
  6.5 0.0 copy-start
  6.5 0.0 all-gather.2.cloned.1.call-start
  6.5 1.6 %reduce_sum.36 = f32[16,128]{1,0:T(8,128)S(1)} reduce(f32[16,128,128]{2,1,0:T(8,128)} %param.9, f32[]{:T(128)} %constant.10.clone.1), dimensions={2}, to_apply=%region_0.0 | reduce | flops 260096 | bytes 1056772 | tf_op jit(solution)/shard_map/reduce_sum | solution.py:8
  8.2 1.9 %multiply_reduce_fusion.1 = f32[16,128]{1,0:T(8,128)S(1)} fusion(f32[16,128,128]{2,1,0:T(8,128)} %param.9, f32[16,128]{1,0:T(8,128)S(1)} %broadcast_multiply_fusion.1), kind=kLoop, calls=%fused_computation.23 | loop fusion | flops 784384 | bytes 1064960 | tf_op jit(solution)/shard_map/reduce_sum | solution.py:9
  10.0 0.7 convert_element_type.16
  10.7 1.9 %add_convert_fusion.1 = bf16[16,128,128]{2,1,0:T(8,128)(2,1)S(1)} fusion(f32[16,128,128]{2,1,0:T(8,128)} %param.9, f32[128]{0:T(128)} %param.12, f32[128]{0:T(128)} %param.11, f32[16,128]{1,0:T(8,128)S(1)} %add_rsqrt_fusion.1, f32[16,128]{1,0:T(8,128)S(1)} %broadcast_multiply_fusion.1), kind=kLoop, calls=%fused_computation.22 | loop fusion | flops 1310720 | bytes 1590272 | tf_op jit(solution)/shard_map/convert_element_type | solution.py:16
  12.6 0.0 copy-done
  12.6 0.7 fusion.14
  13.3 1.4 fusion.3
  14.7 0.0 all-gather.2.cloned.1.call-update
  14.7 0.0 reduce-scatter.2.cloned.1.call-start
  14.8 0.4 copy.14
  15.2 76.7 %all-gather.2.cloned.1.call-done = bf16[256,128,128]{2,1,0:T(8,128)(2,1)} async-done(((bf16[16,128,128]{2,1,0:T(8,128)(2,1)}), bf16[256,128,128]{2,1,0:T(8,128)(2,1)}) %all-gather.2.cloned.1.call-update) | async-done | bytes 8388624 | tf_op jit(solution)/shard_map/all_gather | solution.py:38
  91.9 11.8 %copy.13 = bf16[256,128,128]{1,0,2:T(8,128)(2,1)} copy(bf16[256,128,128]{2,1,0:T(8,128)(2,1)} %all-gather.2.cloned.1.call-done) | data formatting | bytes 16777216 | tf_op jit(solution)/shard_map/all_gather | solution.py:38
  103.7 0.0 copy-start.4
  103.7 0.0 copy-start.2
  103.7 0.0 copy-start.3
  103.7 0.0 copy-start.1
  103.7 7.1 %convolution_bitcast_fusion = f32[16,256,128]{1,0,2:T(8,128)} fusion(bf16[256,128,128]{1,0,2:T(8,128)(2,1)} %copy.13, bf16[16,128,128]{1,0,2:T(8,128)(2,1)S(1)} %copy.14), kind=kOutput, calls=%fused_computation.4 | convolution fusion | flops 134217728 | bytes 11010048 | tf_op jit(solution)/shard_map/ikc,jkc->ijc/dot_general | solution.py:35
  110.8 0.0 reduce-scatter.2.cloned.1.call-update
  110.8 0.0 copy-done.4
  110.8 0.4 fusion.2
  111.3 30.2 %reduce-scatter.2.cloned.1.call-done = f32[16,128,128]{1,0,2:T(8,128)} async-done(((f32[16,256,128]{1,0,2:T(8,128)}), f32[16,128,128]{1,0,2:T(8,128)}) %reduce-scatter.2.cloned.1.call-update) | async-done | bytes 1048592 | tf_op jit(solution)/shard_map/reduce_scatter | solution.py:41
  141.5 1.4 reduce_sum.38
  142.8 1.4 multiply_reduce_fusion
  144.2 0.0 copy-done.2
  144.2 0.0 copy-done.3
  144.3 1.6 %add_convert_fusion = bf16[16,128,128]{1,0,2:T(8,128)(2,1)S(1)} fusion(f32[16,128,128]{1,0,2:T(8,128)} %reduce-scatter.2.cloned.1.call-done, f32[128]{0:T(128)S(1)} %copy-done.2, f32[128]{0:T(128)S(1)} %copy-done.3, f32[16,128]{1,0:T(8,128)S(1)} %add_rsqrt_fusion, f32[16,128]{1,0:T(8,128)S(1)} %broadcast_multiply_fusion), kind=kLoop, calls=%fused_computation.20 | loop fusion | flops 1310720 | bytes 1590272 | tf_op jit(solution)/shard_map/convert_element_type | solution.py:42
  145.8 0.0 copy-done.1
  145.8 1.3 convolution_multiply_fusion
  (4 shorter events, 0.0 us)
Async XLA Ops:
  6.5 6.1 %copy-start = (bf16[128,512]{1,0:T(8,128)(2,1)S(1)}, bf16[128,512]{1,0:T(8,128)(2,1)}, u32[]{:S(2)}) copy-start(bf16[128,512]{1,0:T(8,128)(2,1)} %param.13) | copy-start | bytes 393220
  6.5 85.3 %all-gather.2.cloned.1.call-start = ((), (), s32[]{:S(2)}) async-start(), calls=%async_computation.1 | async-start | bytes 8912896 | tf_op jit(solution)/shard_map/all_gather | solution.py:38
  14.7 126.8 %reduce-scatter.2.cloned.1.call-start = ((), (), s32[]{:S(2)}) async-start(), calls=%async_computation.2 | async-start | bytes 3145728 | tf_op jit(solution)/shard_map/reduce_scatter | solution.py:41
  103.7 7.2 %copy-start.4 = (bf16[128,128]{1,0:T(8,128)(2,1)S(1)}, bf16[128,128]{1,0:T(8,128)(2,1)}, u32[]{:S(2)}) copy-start(bf16[128,128]{1,0:T(8,128)(2,1)} %param.14) | copy-start | bytes 98308
  103.7 40.6 %copy-start.2 = (f32[128]{0:T(128)S(1)}, f32[128]{0:T(128)}, u32[]{:S(2)}) copy-start(f32[128]{0:T(128)} %param.16) | copy-start | bytes 1540
  103.7 40.6 %copy-start.3 = (f32[128]{0:T(128)S(1)}, f32[128]{0:T(128)}, u32[]{:S(2)}) copy-start(f32[128]{0:T(128)} %param.15) | copy-start | bytes 1540
  103.7 42.2 %copy-start.1 = (bf16[128,128]{1,0:T(8,128)(2,1)S(1)}, bf16[128,128]{1,0:T(8,128)(2,1)}, u32[]{:S(2)}) copy-start(bf16[128,128]{1,0:T(8,128)(2,1)} %param.17) | copy-start | bytes 98308
Sparse Core Ops, SparseCore 0:
  14.8 77.0 all-gather.1
  110.9 30.4 reduce-scatter.1
where the time goes:
time: 155 us; the launch traced here: 154 us
  waiting for transfers between devices  107 us (69%)
  between operations  13.5 us (9%)
  local copies, waits for them, and re-layouts  12.2 us (8%)
  other arithmetic  11.7 us (8%)
  matrix products  9.53 us (6%)
    all_gather x1, waiting for transfers between devices, local(): lax.all_gather(right_side, 'row', axis=0, tiled=True)  76.7 us
    reduce_scatter x1, waiting for transfers between devices, local(): lax.psum_scatter(partial_value, 'col', scatter_dimension=1, tiled=True)  30.2 us
    all_gather x1, local copies, waits for them, and re-layouts, local(): lax.all_gather(right_side, 'row', axis=0, tiled=True)  11.8 us
    dot_general x1, matrix products, local(): jnp.einsum('ikc,jkc->ijc', left_side, lax.all_gather(right_side, 'row', a...  7.12 us
    reduce_sum x2, other arithmetic, layer_norm(): variance = jnp.mean(jnp.square(values - average), axis=-1, keepdims=True)  3.24 us
  transfers between devices with their start and end apart: 2, of which 2 were waited for; matrix products, arithmetic and copies ran while one was open for 1% of the time, Pallas kernels for 0%

commit v1 on v0

v1 whole, which is shorter than its diff:
```python
import functools

import jax
import jax.numpy as jnp
from jax import lax
from jax.experimental import pallas as pl
from jax.experimental.pallas import tpu as pltpu
from jax.sharding import PartitionSpec as P

F32 = jnp.float32
BF16 = jnp.bfloat16
EPSILON = 1e-05
NT = (((1,), (1,)), ((), ()))


def layer_norm(values, gain, bias):
    average = jnp.mean(values, axis=-1, keepdims=True)
    variance = jnp.mean(jnp.square(values - average), axis=-1, keepdims=True)
    return (values - average) * lax.rsqrt(variance + EPSILON) * gain + bias


def gathered(pair_map, pair_mask, in_gain, in_bias, w_proj, w_gate, out_gain, out_bias, w_out):
    row_count, col_count, channels = pair_map.shape
    hidden_width = w_out.shape[0]
    normed_map = layer_norm(pair_map, in_gain, in_bias).astype(BF16)
    flattened = normed_map.reshape(-1, channels)
    projected_all = jnp.dot(flattened, w_proj, preferred_element_type=F32).reshape(
        row_count, col_count, 4 * hidden_width
    )
    masked = pair_mask.astype(F32)[..., None]
    left_side = (
        masked
        * jax.nn.sigmoid(projected_all[..., :hidden_width])
        * projected_all[..., hidden_width : 2 * hidden_width]
    ).astype(BF16)
    gating = jax.nn.sigmoid(jnp.dot(flattened, w_gate, preferred_element_type=F32)).reshape(
        row_count, col_count, channels
    )
    right_side = (
        masked
        * jax.nn.sigmoid(projected_all[..., 2 * hidden_width : 3 * hidden_width])
        * projected_all[..., 3 * hidden_width :]
    ).astype(BF16)
    partial_value = jnp.einsum(
        "ikc,jkc->ijc",
        left_side,
        lax.all_gather(right_side, "row", axis=0, tiled=True),
        preferred_element_type=F32,
    )
    summed = lax.psum_scatter(partial_value, "col", scatter_dimension=1, tiled=True)
    normed_sum = layer_norm(summed, out_gain, out_bias).astype(BF16)
    result = jnp.dot(normed_sum.reshape(-1, hidden_width), w_out, preferred_element_type=F32).reshape(
        row_count, col_count, channels
    )
    return gating * result


def project_kernel(map_ref, mask_ref, gain_ref, bias_ref, w_proj_ref, w_gate_ref, sides_ref, gating_ref, w_scr, side_scr):
    step = pl.program_id(0)
    block, cols, channels = map_ref.shape
    hidden = w_proj_ref.shape[1] // 4
    rows = mask_ref.shape[0]

    @pl.when(step == 0)
    def _():
        for part in range(4):
            columns = w_proj_ref[:, part * hidden : (part + 1) * hidden]
            w_scr[part * hidden : (part + 1) * hidden, :] = columns.astype(F32).T.astype(BF16)

    values = map_ref[...].reshape(block * cols, channels)
    normed = layer_norm(values, gain_ref[...], bias_ref[...]).astype(BF16)
    gates = jax.nn.sigmoid(jnp.dot(normed, w_gate_ref[...], preferred_element_type=F32))
    gating_ref[...] = gates.reshape(block, cols, channels)
    projected = lax.dot_general(w_scr[...], normed, NT, preferred_element_type=F32)
    for at in range(block):
        row = step * block + at
        masked = mask_ref[pl.ds(row, 1), :].astype(F32)
        here = projected[:, at * cols : (at + 1) * cols]
        for side in range(2):
            gate = here[2 * side * hidden : (2 * side + 1) * hidden]
            value = here[(2 * side + 1) * hidden : (2 * side + 2) * hidden]
            side_scr[side, pl.ds(row, hidden, stride=rows), :] = masked * jax.nn.sigmoid(gate) * value

    @pl.when(step == pl.num_programs(0) - 1)
    def _():
        parts, _, share = sides_ref.shape[:3]
        for side in range(2):
            sides_ref[:, side] = side_scr[side].astype(BF16).reshape(parts, share, rows, cols)


def pairs_kernel(sides_ref, out_ref):
    row_parts, col_parts, _, _, rows, cols = sides_ref.shape

    def side(which):
        return jnp.concatenate(
            [sides_ref[:, q, which, 0].reshape(row_parts * rows, cols) for q in range(col_parts)], axis=1
        )

    summed = lax.dot_general(side(0), side(1), NT, preferred_element_type=F32).astype(BF16)
    for q in range(col_parts):
        out_ref[:, q, 0] = summed[:, q * cols : (q + 1) * cols].reshape(row_parts, rows, cols)


def output_kernel(summed_ref, gating_ref, gain_ref, bias_ref, w_out_ref, out_ref, scr):
    step = pl.program_id(0)
    hidden, rows, cols = summed_ref.shape
    block, _, channels = out_ref.shape

    @pl.when(step == 0)
    def _():
        values = summed_ref[...].astype(F32)
        average = jnp.sum(values, axis=0, keepdims=True) / hidden
        centred = values - average
        variance = jnp.sum(jnp.square(centred), axis=0, keepdims=True) / hidden
        scr[...] = (centred * lax.rsqrt(variance + EPSILON)).reshape(hidden * rows, cols)

    for at in range(block):
        scaled = scr[pl.ds(step * block + at, hidden, stride=rows), :].T
        normed_sum = (scaled * gain_ref[...] + bias_ref[...]).astype(BF16)
        result = jnp.dot(normed_sum, w_out_ref[...], preferred_element_type=F32)
        out_ref[at] = gating_ref[at] * result


def whole(shape):
    return pl.BlockSpec(shape, lambda *_: (0,) * len(shape))


def exchanged(
    pair_map, pair_mask, in_gain, in_bias, w_proj, w_gate, out_gain, out_bias, w_out, *, row_parts, col_parts
):
    rows, cols, channels = pair_map.shape
    hidden = w_out.shape[0]
    parts = row_parts * col_parts
    share = hidden // parts
    block = 4
    sides, gating = pl.pallas_call(
        project_kernel,
        grid=(rows // block,),
        in_specs=[
            pl.BlockSpec((block, cols, channels), lambda i: (i, 0, 0)),
            whole((rows, cols)),
            whole((1, channels)),
            whole((1, channels)),
            whole(w_proj.shape),
            whole(w_gate.shape),
        ],
        out_specs=[
            whole((parts, 2, share, rows, cols)),
            pl.BlockSpec((block, cols, channels), lambda i: (i, 0, 0)),
        ],
        out_shape=[
            jax.ShapeDtypeStruct((parts, 2, share, rows, cols), BF16),
            jax.ShapeDtypeStruct((rows, cols, channels), F32),
        ],
        scratch_shapes=[
            pltpu.VMEM((4 * hidden, channels), BF16),
            pltpu.VMEM((2, hidden * rows, cols), F32),
        ],
        name="project",
    )(pair_map, pair_mask, in_gain.reshape(1, -1), in_bias.reshape(1, -1), w_proj, w_gate)
    sides = lax.all_to_all(sides, ("row", "col"), 0, 0, tiled=True)
    sides = sides.reshape(row_parts, col_parts, 2, share, rows, cols)
    summed = pl.pallas_call(
        pairs_kernel,
        grid=(share,),
        in_specs=[pl.BlockSpec((row_parts, col_parts, 2, 1, rows, cols), lambda c: (0, 0, 0, c, 0, 0))],
        out_specs=pl.BlockSpec((row_parts, col_parts, 1, rows, cols), lambda c: (0, 0, c, 0, 0)),
        out_shape=jax.ShapeDtypeStruct((row_parts, col_parts, share, rows, cols), BF16),
        name="pairs",
    )(sides)
    summed = summed.reshape(parts, share, rows, cols)
    summed = lax.all_to_all(summed, ("row", "col"), 0, 0, tiled=True).reshape(hidden, rows, cols)
    return pl.pallas_call(
        output_kernel,
        grid=(rows // block,),
        in_specs=[
            whole((hidden, rows, cols)),
            pl.BlockSpec((block, cols, channels), lambda i: (i, 0, 0)),
            whole((1, hidden)),
            whole((1, hidden)),
            whole(w_out.shape),
        ],
        out_specs=pl.BlockSpec((block, cols, channels), lambda i: (i, 0, 0)),
        out_shape=jax.ShapeDtypeStruct((rows, cols, channels), F32),
        scratch_shapes=[pltpu.VMEM((hidden * rows, cols), F32)],
        name="output",
    )(summed, gating, out_gain.reshape(1, -1), out_bias.reshape(1, -1), w_out)


def solution(mesh):
    row_parts, col_parts = mesh.shape["row"], mesh.shape["col"]

    def local(pair_map, pair_mask, in_gain, in_bias, w_proj, w_gate, out_gain, out_bias, w_out):
        rows, cols, channels = pair_map.shape
        hidden = w_out.shape[0]
        whole_tiles = rows % 16 == 0 and cols % 128 == 0 and channels % 128 == 0 and hidden % 128 == 0
        plan = gathered
        if whole_tiles and hidden % (row_parts * col_parts) == 0:
            plan = functools.partial(exchanged, row_parts=row_parts, col_parts=col_parts)
        return plan(pair_map, pair_mask, in_gain, in_bias, w_proj, w_gate, out_gain, out_bias, w_out)

    in_specs = (P("row", "col", None), P("row", "col"), P(), P(), P(), P(), P(), P(), P())
    out_specs = P("row", "col", None)
    return jax.shard_map(local, mesh=mesh, in_specs=in_specs, out_specs=out_specs, check_vma=False)
```

time: 155 us -> 66.7 us (0.43)
  waiting for transfers between devices: 107 us -> 0 us
  blocking collectives: 0 us -> 52.3 us
  between operations: 13.5 us -> 0.01 us
  Pallas kernels: 0 us -> 13.3 us
  local copies, waits for them, and re-layouts: 12.2 us -> 0 us
  other arithmetic: 11.7 us -> 0 us
  matrix products: 9.53 us -> 0 us
    all_gather x1 -> x0, waiting for transfers between devices: 76.7 us -> none  [local(): lax.all_gather(right_side, 'row', axis=0, tiled=True)]
    all_to_all x0 -> x2, blocking collectives: none -> 52.3 us  [the longest x1 33.6 us: exchanged(): sides = lax.all_to_all(sides, ('row', 'col'), 0, 0, tiled=True)]
    reduce_scatter x1 -> x0, waiting for transfers between devices: 30.2 us -> none  [local(): lax.psum_scatter(partial_value, 'col', scatter_dimension=1, tiled=True)]
    pallas_call x0 -> x3, Pallas kernels: none -> 13.3 us  [the longest x1 5.11 us: exchanged(): pl.pallas_call(project_kernel, grid=(rows // block,), in_specs=[pl.BlockS...]
    all_gather x1 -> x0, local copies, waits for them, and re-layouts: 11.8 us -> none  [local(): lax.all_gather(right_side, 'row', axis=0, tiled=True)]
    dot_general x4 -> x0, matrix products: 9.53 us -> none  [the longest x1 7.12 us: local(): jnp.einsum('ikc,jkc->ijc', left_side, lax.all_gather(right_side, 'row', a...]
    reduce_sum x4 -> x0, other arithmetic: 6.21 us -> none  [the longest x2 3.24 us: layer_norm(): variance = jnp.mean(jnp.square(values - average), axis=-1, keepdims=True)]
    convert_element_type x4 -> x0, other arithmetic: 5.51 us -> none  [the longest x1 1.85 us: local(): normed_map = layer_norm(pair_map, in_gain, in_bias).astype(jnp.bfloat16)]
  transfers between devices with their start and end apart: 2 -> 0, of which waited for: 2 -> 0; matrix products, arithmetic and copies ran while one was open for 1% -> 0% of each run, Pallas kernels for 0% -> 0%
where the time goes in v1:
time: 66.7 us; the launch traced here: 65.6 us
  blocking collectives  52.3 us (78%)
  Pallas kernels  13.3 us (20%)
    all_to_all x1, blocking collectives, exchanged(): sides = lax.all_to_all(sides, ('row', 'col'), 0, 0, tiled=True)  33.6 us
    all_to_all x1, blocking collectives, exchanged(): lax.all_to_all(summed, ('row', 'col'), 0, 0, tiled=True)  18.7 us
    pallas_call x1, Pallas kernels, exchanged(): pl.pallas_call(project_kernel, grid=(rows // block,), in_specs=[pl.BlockS...  5.11 us
    pallas_call x1, Pallas kernels, exchanged(): pl.pallas_call(output_kernel, grid=(rows // block,), in_specs=[whole((hid...  4.47 us
    pallas_call x1, Pallas kernels, exchanged(): pl.pallas_call(pairs_kernel, grid=(share,), in_specs=[pl.BlockSpec((row_p...  3.69 us

profile of v1, /device:TPU:0, one launch (start us, length us, event | category | flops | bytes accessed | tf_op | source)
XLA Modules:
  0.0 65.6 jit_solution(12989356308249011438)
XLA Ops:
  0.0 5.1 %project.1 = (bf16[32,2,4,16,128]{4,3,2,1,0:T(8,128)(2,1)}, f32[16,128,128]{2,1,0:T(8,128)}) custom-call(f32[16,128,128]{2,1,0:T(8,128)} %map_ref.1, s32[16,128]{1,0:T(8,128)} %mask_ref.1, f32[1,128]{1,0:T(1,128)} %bitcast.10, f32[1,128]{1,0:T(1,128)} %bitcast.11, bf16[128,512]{1,0:T(8,128)(2,1)} %w_proj_ref.1, bf16[128,128]{1,0:T(8,128)(2,1)} %w_gate_ref.1), custom_call_target="tpu_custom_call" | custom-call | tf_op jit(solution)/shard_map/project/pallas_call | solution.py:136
  5.1 33.6 %all_to_all.10 = bf16[32,2,4,16,128]{4,3,2,1,0:T(8,128)(2,1)} all-to-all(bf16[32,2,4,16,128]{4,3,2,1,0:T(8,128)(2,1)} %get-tuple-element.7), channel_id=1, replica_groups=mesh['row'=16,'col'=2] {'row','col'}, dimensions={0} | all-to-all | bytes 2097152 | tf_op jit(solution)/shard_map/all_to_all | solution.py:161
  38.8 3.7 %pairs.1 = bf16[16,2,4,16,128]{4,3,2,1,0:T(8,128)(2,1)} custom-call(bf16[16,2,2,4,16,128]{5,4,3,2,1,0:T(8,128)(2,1)} %bitcast.7), custom_call_target="tpu_custom_call" | custom-call | tf_op jit(solution)/shard_map/pairs/pallas_call | solution.py:163
  42.4 18.7 %all_to_all.11 = bf16[32,4,16,128]{3,2,1,0:T(8,128)(2,1)} all-to-all(bf16[32,4,16,128]{3,2,1,0:T(8,128)(2,1)} %bitcast.9), channel_id=1, replica_groups=mesh['row'=16,'col'=2] {'row','col'}, dimensions={0} | all-to-all | bytes 1048576 | tf_op jit(solution)/shard_map/all_to_all | solution.py:172
  61.1 4.5 %output.1 = f32[16,128,128]{2,1,0:T(8,128)} custom-call(bf16[128,16,128]{2,1,0:T(8,128)(2,1)} %bitcast.8, f32[16,128,128]{2,1,0:T(8,128)} %get-tuple-element.8.gating_ref, f32[1,128]{1,0:T(1,128)} %bitcast.12, f32[1,128]{1,0:T(1,128)} %bitcast.13, bf16[128,128]{1,0:T(8,128)(2,1)} %w_out_ref.1), custom_call_target="tpu_custom_call" | custom-call | tf_op jit(solution)/shard_map/output/pallas_call | solution.py:173

commit v2 on v0

v2 whole, which is shorter than its diff:
```python
import functools

import jax
import jax.numpy as jnp
from jax import lax
from jax.experimental import pallas as pl
from jax.experimental.pallas import tpu as pltpu
from jax.sharding import PartitionSpec as P


F32 = jnp.float32
BF16 = jnp.bfloat16
EPSILON = 1e-05
NT = (((1,), (1,)), ((), ()))


def layer_norm(values, gain, bias):
    average = jnp.mean(values, axis=-1, keepdims=True)
    variance = jnp.mean(jnp.square(values - average), axis=-1, keepdims=True)
    return (values - average) * lax.rsqrt(variance + EPSILON) * gain + bias


def gathered(pair_map, pair_mask, in_gain, in_bias, w_proj, w_gate, out_gain, out_bias, w_out):
    row_count, col_count, channels = pair_map.shape
    hidden_width = w_out.shape[0]
    normed_map = layer_norm(pair_map, in_gain, in_bias).astype(BF16)
    flattened = normed_map.reshape(-1, channels)
    projected_all = jnp.dot(flattened, w_proj, preferred_element_type=F32).reshape(
        row_count, col_count, 4 * hidden_width
    )
    masked = pair_mask.astype(F32)[..., None]
    left_side = (
        masked
        * jax.nn.sigmoid(projected_all[..., :hidden_width])
        * projected_all[..., hidden_width : 2 * hidden_width]
    ).astype(BF16)
    gating = jax.nn.sigmoid(jnp.dot(flattened, w_gate, preferred_element_type=F32)).reshape(
        row_count, col_count, channels
    )
    right_side = (
        masked
        * jax.nn.sigmoid(projected_all[..., 2 * hidden_width : 3 * hidden_width])
        * projected_all[..., 3 * hidden_width :]
    ).astype(BF16)
    partial_value = jnp.einsum(
        "ikc,jkc->ijc",
        left_side,
        lax.all_gather(right_side, "row", axis=0, tiled=True),
        preferred_element_type=F32,
    )
    summed = lax.psum_scatter(partial_value, "col", scatter_dimension=1, tiled=True)
    normed_sum = layer_norm(summed, out_gain, out_bias).astype(BF16)
    result = jnp.dot(normed_sum.reshape(-1, hidden_width), w_out, preferred_element_type=F32).reshape(
        row_count, col_count, channels
    )
    return gating * result


ROW_BITS = 4
GROUPS = 4
VMEM_LIMIT = 16 * 2**20
HBM = pl.BlockSpec(memory_space=pltpu.MemorySpace.HBM)
VMEM = pl.BlockSpec(memory_space=pltpu.MemorySpace.VMEM)


def gated(gate, value):
    half = 0.5 * value
    return half * jnp.tanh(0.5 * gate) + half


def in_hbm(array):
    return pltpu.with_memory_space_constraint(array, pltpu.MemorySpace.HBM)


def own_bits():
    row, col = lax.axis_index("row"), lax.axis_index("col")
    return [(row >> bit) & 1 for bit in reversed(range(ROW_BITS))] + [col]


def start_copies(pairs, semaphores):
    copies = [pltpu.make_async_copy(source, target, semaphores.at[n]) for n, (source, target) in enumerate(pairs)]
    for copy in copies:
        copy.start()
    return [copy.wait for copy in copies]


def turned(weights):
    return weights.astype(F32).T.astype(BF16)


def project(normed, w_turned, mask_ref, side_scr):
    rows, cols = mask_ref.shape
    hidden = side_scr.shape[1] // rows
    for side in range(2):
        weights = w_turned[2 * side * hidden : (2 * side + 2) * hidden, :]
        projected = lax.dot_general(weights, normed, NT, preferred_element_type=F32)
        for row in range(rows):
            here = projected[:, row * cols : (row + 1) * cols]
            masked = mask_ref[row : row + 1, :].astype(F32)
            side_scr[side, pl.ds(row, hidden, stride=rows), :] = masked * gated(here[:hidden], here[hidden:])


def cut(side_scr, side, outs):
    _, _, wide, _, col = own_bits()
    share, rows, cols = outs[0].shape
    for offset, out_ref in enumerate(outs):
        start = pl.multiple_of(((2 * wide + col) ^ offset) * (share * rows), share * rows)
        out_ref[...] = side_scr[side, pl.ds(start, share * rows), :].astype(BF16).reshape(share, rows, cols)


def sides_kernel(map_hbm, mask_hbm, gain_hbm, bias_hbm, w_hbm, *refs):
    lefts, rights, normed_ref = refs[:GROUPS], refs[GROUPS : 2 * GROUPS], refs[2 * GROUPS]
    map_scr, mask_scr, gain_scr, bias_scr, w_scr, w_turned, side_scr, sems = refs[2 * GROUPS + 1 :]
    rows, cols, channels = map_scr.shape
    hidden = w_scr.shape[1] // 4
    wait_map, wait_w, wait_gain, wait_bias, wait_mask = start_copies(
        [(map_hbm, map_scr), (w_hbm, w_scr), (gain_hbm, gain_scr), (bias_hbm, bias_scr), (mask_hbm, mask_scr)], sems
    )
    wait_w()
    for part in range(4):
        w_turned[part * hidden : (part + 1) * hidden, :] = turned(w_scr[:, part * hidden : (part + 1) * hidden])
    wait_gain()
    wait_bias()
    wait_mask()
    wait_map()
    values = map_scr[...].reshape(rows * cols, channels)
    normed = layer_norm(values, gain_scr[...], bias_scr[...]).astype(BF16)
    normed_ref[...] = normed
    project(normed, w_turned, mask_scr, side_scr)
    cut(side_scr, 0, lefts)
    cut(side_scr, 1, rights)


def gates_kernel(normed_ref, w_gate_ref, gain_hbm, bias_hbm, w_out_hbm, gating_ref, gain_ref, bias_ref, w_out_ref, sems):
    waits = start_copies([(gain_hbm, gain_ref), (bias_hbm, bias_ref), (w_out_hbm, w_out_ref)], sems)
    rows, cols, channels = gating_ref.shape
    block = rows // 4
    for step in range(4):
        normed = normed_ref[step * block * cols : (step + 1) * block * cols, :]
        gates = jnp.dot(normed, w_gate_ref[...], preferred_element_type=F32)
        gating_ref[step * block : (step + 1) * block] = (0.5 * jnp.tanh(0.5 * gates) + 0.5).reshape(
            block, cols, channels
        )
    for wait in waits:
        wait()


def pairs_kernel(*refs):
    rights, lefts, out_ref, scr = refs[: 4 * GROUPS], refs[4 * GROUPS : 6 * GROUPS], refs[-2], refs[-1]
    half, parity, wide, core, _ = own_bits()
    share, rows, _ = lefts[0].shape
    for n, piece in enumerate(rights):
        other_core, other_half, other_wide, other_col = [(n >> bit) & 1 for bit in (3, 2, 1, 0)]
        block = 4 * (half ^ other_half) + 2 * (wide ^ other_wide) + (core ^ other_core)
        scr[other_col, :, pl.ds(pl.multiple_of(block * rows, rows), rows), :] = piece[...]
    count = scr.shape[2]
    first = lax.broadcasted_iota(jnp.int32, (GROUPS, rows // 2, count), 2) < count // 2
    for pair in range(share // 2):
        packed = []
        for c in (2 * pair, 2 * pair + 1):
            left = jnp.concatenate(
                [jnp.concatenate([lefts[2 * at + q][c] for at in range(GROUPS)], axis=0) for q in range(2)], axis=1
            )
            right = jnp.concatenate([scr[q, c] for q in range(2)], axis=1)
            summed = lax.dot_general(left, right, NT, preferred_element_type=F32)
            rolled = pltpu.roll(summed, count // 2, 1).reshape(GROUPS, 2, rows // 2, count)
            summed = summed.reshape(GROUPS, 2, rows // 2, count)
            packed.append(
                [
                    jnp.where(first, summed[:, 0], rolled[:, 1]),
                    jnp.where(first, rolled[:, 0], summed[:, 1]),
                ]
            )
        for at in range(GROUPS):
            place = 4 * (parity ^ (at >> 1)) + 2 * (wide ^ (at & 1))
            for q in range(2):
                out_ref[place + q, pair] = jnp.concatenate([packed[0][q][at], packed[1][q][at]], axis=0).astype(BF16)


def output_kernel(summed_ref, gating_ref, gain_ref, bias_ref, w_ref, out_hbm, scr, out_scr, sems):
    rows, cols, _ = out_scr.shape
    hidden = w_ref.shape[0]
    low = rows // 2
    for part in range(2):
        values = summed_ref[part * GROUPS : (part + 1) * GROUPS].astype(F32).reshape(hidden, low, cols)
        average = jnp.sum(values, axis=0, keepdims=True) / hidden
        centred = values - average
        variance = jnp.sum(jnp.square(centred), axis=0, keepdims=True) / hidden
        scr[part] = (centred * lax.rsqrt(variance + EPSILON)).reshape(hidden * low, cols)
    waits = []
    for row in range(low):
        for part in range(2):
            scaled = scr[part, pl.ds(row, hidden, stride=low), :].T
            normed_sum = (scaled * gain_ref[...] + bias_ref[...]).astype(BF16)
            result = jnp.dot(normed_sum, w_ref[...], preferred_element_type=F32)
            for high in range(2):
                at, where = row + high * low, slice(part * cols // 2, (part + 1) * cols // 2)
                out_scr[at, where] = gating_ref[at, where] * result[high * cols // 2 : (high + 1) * cols // 2]
        if row % 2:
            for high in range(2):
                ready = pl.ds(row - 1 + high * low, 2)
                waits += start_copies(
                    [(out_scr.at[ready], out_hbm.at[ready])], sems.at[pl.ds(row // 2 + high * low // 2, 1)]
                )
    for wait in waits:
        wait()


def exchanged(pair_map, pair_mask, in_gain, in_bias, w_proj, w_gate, out_gain, out_bias, w_out, *, col_parts):
    rows, cols, channels = pair_map.shape
    hidden = w_out.shape[0]
    share = hidden // GROUPS
    half, parity, wide, core, col = [col_parts << bit for bit in reversed(range(ROW_BITS))] + [1]
    plane = [0, col, wide, wide + col]
    devices = range(2 * half)

    def swap(array, offset):
        if not offset:
            return array
        return lax.ppermute(array, ("row", "col"), [(n, n ^ offset) for n in devices])

    params = pltpu.CompilerParams(vmem_limit_bytes=VMEM_LIMIT)
    inputs = (pair_map, pair_mask, in_gain.reshape(1, -1), in_bias.reshape(1, -1), w_proj)
    piece = jax.ShapeDtypeStruct((share, rows, cols), BF16)
    *pieces, normed = pl.pallas_call(
        sides_kernel,
        in_specs=[HBM] * 5,
        out_specs=[VMEM] * (2 * GROUPS + 1),
        out_shape=[piece] * (2 * GROUPS) + [jax.ShapeDtypeStruct((rows * cols, channels), BF16)],
        scratch_shapes=[
            pltpu.VMEM((rows, cols, channels), F32),
            pltpu.VMEM((rows, cols), pair_mask.dtype),
            pltpu.VMEM((1, channels), F32),
            pltpu.VMEM((1, channels), F32),
            pltpu.VMEM((channels, 4 * hidden), BF16),
            pltpu.VMEM((4 * hidden, channels), BF16),
            pltpu.VMEM((2, hidden * rows, cols), F32),
            pltpu.SemaphoreType.DMA((5,)),
        ],
        compiler_params=params,
        name="sides",
    )(*[in_hbm(x) for x in inputs])
    lefts, rights = pieces[:GROUPS], pieces[GROUPS:]
    lefts = [swap(x, plane[n]) for n, x in enumerate(lefts)]
    lefts += [swap(x, parity) for x in lefts]
    rights = [swap(x, plane[n]) for n, x in enumerate(rights)]
    rights += [swap(x, half) for x in rights]
    rights += [swap(x, core) for x in rights]
    gating, gain, bias, w_last = pl.pallas_call(
        gates_kernel,
        in_specs=[VMEM, VMEM, HBM, HBM, HBM],
        out_specs=[VMEM] * 4,
        out_shape=[
            jax.ShapeDtypeStruct((rows, cols, channels), F32),
            jax.ShapeDtypeStruct((1, hidden), F32),
            jax.ShapeDtypeStruct((1, hidden), F32),
            jax.ShapeDtypeStruct(w_out.shape, BF16),
        ],
        scratch_shapes=[pltpu.SemaphoreType.DMA((3,))],
        compiler_params=params,
        name="gates",
    )(normed, w_gate, in_hbm(out_gain.reshape(1, -1)), in_hbm(out_bias.reshape(1, -1)), in_hbm(w_out))
    summed = pl.pallas_call(
        pairs_kernel,
        in_specs=[VMEM] * (6 * GROUPS + 1),
        out_specs=VMEM,
        out_shape=jax.ShapeDtypeStruct((2 * GROUPS, share // 2, rows, cols), BF16),
        scratch_shapes=[pltpu.VMEM((2, share, 8 * rows, cols), BF16)],
        compiler_params=params,
        name="pairs",
    )(*rights, *lefts, gain)
    circles = [
        [own + other + offset for other in (0, parity) for offset in plane]
        for own in (0, core, half, half + core)
    ]
    summed = lax.all_to_all(summed, ("row", "col"), 0, 0, tiled=True, axis_index_groups=circles)
    return pl.pallas_call(
        output_kernel,
        in_specs=[VMEM] * 5,
        out_specs=HBM,
        out_shape=pltpu.MemorySpace.HBM((rows, cols, channels), F32),
        scratch_shapes=[
            pltpu.VMEM((2, hidden * rows // 2, cols), F32),
            pltpu.VMEM((rows, cols, channels), F32),
            pltpu.SemaphoreType.DMA((rows // 2,)),
        ],
        compiler_params=params,
        name="output",
    )(summed, gating, gain, bias, w_last)


def solution(mesh):
    row_parts, col_parts = mesh.shape["row"], mesh.shape["col"]

    def local(pair_map, pair_mask, in_gain, in_bias, w_proj, w_gate, out_gain, out_bias, w_out):
        rows, cols, channels = pair_map.shape
        hidden = w_out.shape[0]
        whole_tiles = rows % 16 == 0 and cols % 128 == 0 and channels % 128 == 0 and hidden % 128 == 0
        bits = row_parts == 2**ROW_BITS and col_parts == 2 and rows * row_parts == col_parts * cols
        plan = gathered
        if whole_tiles and bits:
            plan = functools.partial(exchanged, col_parts=col_parts)
        return plan(pair_map, pair_mask, in_gain, in_bias, w_proj, w_gate, out_gain, out_bias, w_out)

    in_specs = (P("row", "col", None), P("row", "col"), P(), P(), P(), P(), P(), P(), P())
    out_specs = P("row", "col", None)
    return jax.shard_map(local, mesh=mesh, in_specs=in_specs, out_specs=out_specs, check_vma=False)
```

time: 155 us -> 66 us (0.43)
  the two profiles are of different devices: /device:TPU:0 before, /device:TPU:16 now
where the time goes in v2:
time: 66 us; the launch traced here: 65.8 us
  starting transfers between devices  25.8 us (39%)
  waiting for transfers between devices  17.7 us (27%)
  blocking collectives  15.4 us (23%)
  Pallas kernels  6.87 us (10%)
    ppermute x22, starting transfers between devices, swap(): lax.ppermute(array, ('row', 'col'), [(n, n ^ offset) for n in devices])  25.8 us
    ppermute x22, waiting for transfers between devices, swap(): lax.ppermute(array, ('row', 'col'), [(n, n ^ offset) for n in devices])  17.7 us
    all_to_all x1, blocking collectives, exchanged(): lax.all_to_all(summed, ('row', 'col'), 0, 0, tiled=True, axis_index_group...  15.4 us
    pallas_call x1, Pallas kernels, exchanged(): pl.pallas_call(sides_kernel, in_specs=[HBM] * 5, out_specs=[VMEM] * (2 *...  3.16 us
    pallas_call x1, Pallas kernels, exchanged(): pl.pallas_call(output_kernel, in_specs=[VMEM] * 5, out_specs=HBM, out_sha...  1.66 us
  transfers between devices with their start and end apart: 22, of which 8 were waited for; matrix products, arithmetic and copies ran while one was open for 0% of the time, Pallas kernels for 1%

profile of v2, /device:TPU:16, one launch (start us, length us, event | category | flops | bytes accessed | tf_op | source)
XLA Modules:
  0.0 65.8 jit_solution(3672140456796553943)
XLA Ops:
  0.0 3.2 %sides.1 = (bf16[32,16,128]{2,1,0:T(8,128)(2,1)S(1)}, bf16[32,16,128]{2,1,0:T(8,128)(2,1)S(1)}, bf16[32,16,128]{2,1,0:T(8,128)(2,1)S(1)}, bf16[32,16,128]{2,1,0:...) custom-call(f32[16,128,128]{2,1,0:T(8,128)} %map_hbm.1, ...), custom_call_target="tpu_custom_call" | custom-call | tf_op jit(solution)/shard_map/sides/pallas_call | solution.py:225
  3.2 1.6 %collective-permute-start = (bf16[32,16,128]{2,1,0:T(8,128)(2,1)S(1)}, bf16[32,16,128]{2,1,0:T(8,128)(2,1)S(1)}, u32[]{:S(2)}, u32[]{:S(2)}) collective-permute-start(bf16[32,16,128]{2,1,0:T(8,128)(2,1)S(1)} %get-tuple-element.19), channel_id=1, source_target_pairs={{0,1},{1,0},{2,3},{3,2},{4,5},{5,4},{6,7},{7,6},{8,9},{9,8},{10,11... | collective-permute-start | bytes 393224 | tf_op jit(solution)/shard_map/ppermute | solution.py:220
  4.8 1.5 %collective-permute-start.1 = (bf16[32,16,128]{2,1,0:T(8,128)(2,1)S(1)}, bf16[32,16,128]{2,1,0:T(8,128)(2,1)S(1)}, u32[]{:S(2)}, u32[]{:S(2)}) collective-permute-start(bf16[32,16,128]{2,1,0:T(8,128)(2,1)S(1)} %get-tuple-element.20), channel_id=1, source_target_pairs={{0,4},{1,5},{2,6},{3,7},{4,0},{5,1},{6,2},{7,3},{8,12},{9,13},{10,... | collective-permute-start | bytes 393224 | tf_op jit(solution)/shard_map/ppermute | solution.py:220
  6.2 0.5 collective-permute-start.2
  6.7 1.5 %collective-permute-start.15 = (bf16[32,16,128]{2,1,0:T(8,128)(2,1)S(1)}, bf16[32,16,128]{2,1,0:T(8,128)(2,1)S(1)}, u32[]{:S(2)}, u32[]{:S(2)}) collective-permute-start(bf16[32,16,128]{2,1,0:T(8,128)(2,1)S(1)} %get-tuple-element.23), channel_id=1, source_target_pairs={{0,1},{1,0},{2,3},{3,2},{4,5},{5,4},{6,7},{7,6},{8,9},{9,8},{10,11... | collective-permute-start | bytes 393224 | tf_op jit(solution)/shard_map/ppermute | solution.py:220
  8.2 1.5 %collective-permute-start.16 = (bf16[32,16,128]{2,1,0:T(8,128)(2,1)S(1)}, bf16[32,16,128]{2,1,0:T(8,128)(2,1)S(1)}, u32[]{:S(2)}, u32[]{:S(2)}) collective-permute-start(bf16[32,16,128]{2,1,0:T(8,128)(2,1)S(1)} %get-tuple-element.24), channel_id=1, source_target_pairs={{0,4},{1,5},{2,6},{3,7},{4,0},{5,1},{6,2},{7,3},{8,12},{9,13},{10,... | collective-permute-start | bytes 393224 | tf_op jit(solution)/shard_map/ppermute | solution.py:220
  9.7 0.0 collective-permute-done.refs_1_
  9.7 1.7 %collective-permute-start.17 = (bf16[32,16,128]{2,1,0:T(8,128)(2,1)S(1)}, bf16[32,16,128]{2,1,0:T(8,128)(2,1)S(1)}, u32[]{:S(2)}, u32[]{:S(2)}) collective-permute-start(bf16[32,16,128]{2,1,0:T(8,128)(2,1)S(1)} %get-tuple-element.25), channel_id=1, source_target_pairs={{0,5},{1,4},{2,7},{3,6},{4,1},{5,0},{6,3},{7,2},{8,13},{9,12},{10,... | collective-permute-start | bytes 393224 | tf_op jit(solution)/shard_map/ppermute | solution.py:220
  11.5 0.0 collective-permute-done.1.refs_2_
  11.5 1.6 %collective-permute-start.18 = (bf16[32,16,128]{2,1,0:T(8,128)(2,1)S(1)}, bf16[32,16,128]{2,1,0:T(8,128)(2,1)S(1)}, u32[]{:S(2)}, u32[]{:S(2)}) collective-permute-start(bf16[32,16,128]{2,1,0:T(8,128)(2,1)S(1)} %get-tuple-element.22.refs_16_), channel_id=1, source_target_pairs={{0,8},{1,9},{2,10},{3,11},{4,12},{5,13},{6,14},{7,15},{8,0},{9,1},... | collective-permute-start | bytes 393224 | tf_op jit(solution)/shard_map/ppermute | solution.py:220
  13.1 0.5 collective-permute-done.2.refs_3_
  13.6 0.0 collective-permute-start.7
  13.6 0.5 collective-permute-done.15.refs_17_
  14.1 0.1 collective-permute-start.3
  14.2 2.5 %collective-permute-done.16.refs_18_ = bf16[32,16,128]{2,1,0:T(8,128)(2,1)S(1)} collective-permute-done((bf16[32,16,128]{2,1,0:T(8,128)(2,1)S(1)}, bf16[32,16,128]{2,1,0:T(8,128)(2,1)S(1)}, u32[]{:S(2)}, u32[]{:S(2)}) %collective-permute-start.16) | collective-permute-done | bytes 131104 | tf_op jit(solution)/shard_map/ppermute | solution.py:220
  16.7 0.0 collective-permute-start.8
  16.7 1.4 %collective-permute-done.17.refs_19_ = bf16[32,16,128]{2,1,0:T(8,128)(2,1)S(1)} collective-permute-done((bf16[32,16,128]{2,1,0:T(8,128)(2,1)S(1)}, bf16[32,16,128]{2,1,0:T(8,128)(2,1)S(1)}, u32[]{:S(2)}, u32[]{:S(2)}) %collective-permute-start.17) | collective-permute-done | bytes 131104 | tf_op jit(solution)/shard_map/ppermute | solution.py:220
  18.1 0.2 collective-permute-start.4
  18.3 0.0 collective-permute-done.18.refs_20_
  18.3 0.0 collective-permute-start.9
  18.3 0.0 collective-permute-done.7.refs_8_
  18.3 2.8 %collective-permute-start.5 = (bf16[32,16,128]{2,1,0:T(8,128)(2,1)S(1)}, bf16[32,16,128]{2,1,0:T(8,128)(2,1)S(1)}, u32[]{:S(2)}, u32[]{:S(2)}) collective-permute-start(bf16[32,16,128]{2,1,0:T(8,128)(2,1)S(1)} %collective-permute-done.1.refs_2_), channel_id=1, source_target_pairs={{0,16},{1,17},{2,18},{3,19},{4,20},{5,21},{6,22},{7,23},{8,24},{9,... | collective-permute-start | bytes 393224 | tf_op jit(solution)/shard_map/ppermute | solution.py:220
  21.1 5.4 %collective-permute-done.3.refs_4_ = bf16[32,16,128]{2,1,0:T(8,128)(2,1)S(1)} collective-permute-done((bf16[32,16,128]{2,1,0:T(8,128)(2,1)S(1)}, bf16[32,16,128]{2,1,0:T(8,128)(2,1)S(1)}, u32[]{:S(2)}, u32[]{:S(2)}) %collective-permute-start.3) | collective-permute-done | bytes 131104 | tf_op jit(solution)/shard_map/ppermute | solution.py:220
  26.5 0.0 collective-permute-start.10
  26.5 0.0 collective-permute-done.8.refs_9_
  26.5 3.4 %collective-permute-start.6 = (bf16[32,16,128]{2,1,0:T(8,128)(2,1)S(1)}, bf16[32,16,128]{2,1,0:T(8,128)(2,1)S(1)}, u32[]{:S(2)}, u32[]{:S(2)}) collective-permute-start(bf16[32,16,128]{2,1,0:T(8,128)(2,1)S(1)} %collective-permute-done.2.refs_3_), channel_id=1, source_target_pairs={{0,16},{1,17},{2,18},{3,19},{4,20},{5,21},{6,22},{7,23},{8,24},{9,... | collective-permute-start | bytes 393224 | tf_op jit(solution)/shard_map/ppermute | solution.py:220
  29.9 0.0 collective-permute-done.4.refs_5_
  29.9 6.1 %collective-permute-start.19 = (bf16[32,16,128]{2,1,0:T(8,128)(2,1)S(1)}, bf16[32,16,128]{2,1,0:T(8,128)(2,1)S(1)}, u32[]{:S(2)}, u32[]{:S(2)}) collective-permute-start(bf16[32,16,128]{2,1,0:T(8,128)(2,1)S(1)} %collective-permute-done.15.refs_17_), channel_id=1, source_target_pairs={{0,8},{1,9},{2,10},{3,11},{4,12},{5,13},{6,14},{7,15},{8,0},{9,1},... | collective-permute-start | bytes 393224 | tf_op jit(solution)/shard_map/ppermute | solution.py:220
  36.0 0.0 collective-permute-done.9.refs_10_
  36.0 0.0 collective-permute-start.20
  36.0 0.0 collective-permute-done.5.refs_6_
  36.0 2.8 %collective-permute-start.21 = (bf16[32,16,128]{2,1,0:T(8,128)(2,1)S(1)}, bf16[32,16,128]{2,1,0:T(8,128)(2,1)S(1)}, u32[]{:S(2)}, u32[]{:S(2)}) collective-permute-start(bf16[32,16,128]{2,1,0:T(8,128)(2,1)S(1)} %collective-permute-done.17.refs_19_), channel_id=1, source_target_pairs={{0,8},{1,9},{2,10},{3,11},{4,12},{5,13},{6,14},{7,15},{8,0},{9,1},... | collective-permute-start | bytes 393224 | tf_op jit(solution)/shard_map/ppermute | solution.py:220
  38.8 0.0 collective-permute-done.10.refs_11_
  38.8 0.0 collective-permute-start.11
  38.8 0.0 collective-permute-done.6.refs_7_
  38.8 0.5 collective-permute-start.12
  39.3 2.6 %collective-permute-done.19.refs_21_ = bf16[32,16,128]{2,1,0:T(8,128)(2,1)S(1)} collective-permute-done((bf16[32,16,128]{2,1,0:T(8,128)(2,1)S(1)}, bf16[32,16,128]{2,1,0:T(8,128)(2,1)S(1)}, u32[]{:S(2)}, u32[]{:S(2)}) %collective-permute-start.19) | collective-permute-done | bytes 131104 | tf_op jit(solution)/shard_map/ppermute | solution.py:220
  41.9 0.0 collective-permute-start.13
  41.9 2.8 %collective-permute-done.20.refs_22_ = bf16[32,16,128]{2,1,0:T(8,128)(2,1)S(1)} collective-permute-done((bf16[32,16,128]{2,1,0:T(8,128)(2,1)S(1)}, bf16[32,16,128]{2,1,0:T(8,128)(2,1)S(1)}, u32[]{:S(2)}, u32[]{:S(2)}) %collective-permute-start.20) | collective-permute-done | bytes 131104 | tf_op jit(solution)/shard_map/ppermute | solution.py:220
  44.7 0.0 collective-permute-start.14
  44.7 0.8 %gates.1 = (f32[16,128,128]{2,1,0:T(8,128)S(1)}, f32[1,128]{1,0:T(1,128)S(1)}, f32[1,128]{1,0:T(1,128)S(1)}, bf16[128,128]{1,0:T(8,128)(2,1)S(1)}) custom-call(bf16[2048,128]{1,0:T(8,128)(2,1)S(1)} %get-tuple-element.26.normed_ref, bf16[128,128]{1,0:T(8,128)(2,1)S(1)} %copy-done, f32[1,128]{1,0:T(1,128)} %bitcast.6, f32[1,128]{1,0:T(1,128)} %bitcast.7, ...), custom_call_target="tpu_custom_call" | custom-call | tf_op jit(solution)/shard_map/gates/pallas_call | solution.py:249
  45.6 1.9 %collective-permute-done.21.refs_23_ = bf16[32,16,128]{2,1,0:T(8,128)(2,1)S(1)} collective-permute-done((bf16[32,16,128]{2,1,0:T(8,128)(2,1)S(1)}, bf16[32,16,128]{2,1,0:T(8,128)(2,1)S(1)}, u32[]{:S(2)}, u32[]{:S(2)}) %collective-permute-start.21) | collective-permute-done | bytes 131104 | tf_op jit(solution)/shard_map/ppermute | solution.py:220
  47.5 0.0 collective-permute-done.11.refs_12_
  47.5 0.0 collective-permute-done.12.refs_13_
  47.5 0.0 collective-permute-done.13.refs_14_
  47.5 1.2 %pairs.1 = bf16[8,16,16,128]{3,2,1,0:T(8,128)(2,1)S(1)} custom-call(bf16[32,16,128]{2,1,0:T(8,128)(2,1)S(1)} %get-tuple-element.18.refs_0_, bf16[32,16,128]{2,1,0:T(8,128)(2,1)S(1)} %collective-permute-done.refs_1_, bf16[32,16,128]{2,1,0:T(8,128)(2,1)S(1)} %collective-permute-done.1.refs_2_, bf16[32,16,128]{2,1,0:T(8,128)(2,1)S(1)} %collective-permute-done.2.refs_3_, ...), custom_call_target="tpu_custom_call" | custom-call | tf_op jit(solution)/shard_map/pairs/pallas_call | solution.py:263
  48.7 15.4 %all_to_all.5.summed_ref = bf16[8,16,16,128]{3,2,1,0:T(8,128)(2,1)S(1)} all-to-all(bf16[8,16,16,128]{3,2,1,0:T(8,128)(2,1)S(1)} %pairs.1), channel_id=1, replica_groups={{0,1,4,5,8,9,12,13},{2,3,6,7,10,11,14,15},{16,17,20,21,24,25,28,29},{18..., dimensions={0} | all-to-all | bytes 1048576 | tf_op jit(solution)/shard_map/all_to_all | solution.py:276
  64.1 1.7 %output.1 = f32[16,128,128]{2,1,0:T(8,128)} custom-call(bf16[8,16,16,128]{3,2,1,0:T(8,128)(2,1)S(1)} %all_to_all.5.summed_ref, f32[16,128,128]{2,1,0:T(8,128)S(1)} %get-tuple-element.28.gating_ref, f32[1,128]{1,0:T(1,128)S(1)} %get-tuple-element.27.refs_24_.gain_ref, f32[1,128]{1,0:T(1,128)S(1)} %get-tuple-element.29.bias_ref, ...), custom_call_target="tpu_custom_call" | custom-call | tf_op jit(solution)/shard_map/output/pallas_call | solution.py:277
  (3 shorter events, 0.0 us)
Async XLA Ops:
  0.0 44.7 %copy-start = (bf16[128,128]{1,0:T(8,128)(2,1)S(1)}, bf16[128,128]{1,0:T(8,128)(2,1)}, u32[]{:S(2)}) copy-start(bf16[128,128]{1,0:T(8,128)(2,1)} %w_gate_ref.1) | copy-start | bytes 98308
  3.2 6.6 %collective-permute-start = (bf16[32,16,128]{2,1,0:T(8,128)(2,1)S(1)}, bf16[32,16,128]{2,1,0:T(8,128)(2,1)S(1)}, u32[]{:S(2)}, u32[]{:S(2)}) collective-permute-start(bf16[32,16,128]{2,1,0:T(8,128)(2,1)S(1)} %get-tuple-element.19), channel_id=1, source_target_pairs={{0,1},{1,0},{2,3},{3,2},{4,5},{5,4},{6,7},{7,6},{8,9},{9,8},{10,11... | collective-permute-start | bytes 393224 | tf_op jit(solution)/shard_map/ppermute | solution.py:220
  4.8 6.7 %collective-permute-start.1 = (bf16[32,16,128]{2,1,0:T(8,128)(2,1)S(1)}, bf16[32,16,128]{2,1,0:T(8,128)(2,1)S(1)}, u32[]{:S(2)}, u32[]{:S(2)}) collective-permute-start(bf16[32,16,128]{2,1,0:T(8,128)(2,1)S(1)} %get-tuple-element.20), channel_id=1, source_target_pairs={{0,4},{1,5},{2,6},{3,7},{4,0},{5,1},{6,2},{7,3},{8,12},{9,13},{10,... | collective-permute-start | bytes 393224 | tf_op jit(solution)/shard_map/ppermute | solution.py:220
  6.2 7.3 %collective-permute-start.2 = (bf16[32,16,128]{2,1,0:T(8,128)(2,1)S(1)}, bf16[32,16,128]{2,1,0:T(8,128)(2,1)S(1)}, u32[]{:S(2)}, u32[]{:S(2)}) collective-permute-start(bf16[32,16,128]{2,1,0:T(8,128)(2,1)S(1)} %get-tuple-element.21), channel_id=1, source_target_pairs={{0,5},{1,4},{2,7},{3,6},{4,1},{5,0},{6,3},{7,2},{8,13},{9,12},{10,... | collective-permute-start | bytes 393224 | tf_op jit(solution)/shard_map/ppermute | solution.py:220
  6.7 7.4 %collective-permute-start.15 = (bf16[32,16,128]{2,1,0:T(8,128)(2,1)S(1)}, bf16[32,16,128]{2,1,0:T(8,128)(2,1)S(1)}, u32[]{:S(2)}, u32[]{:S(2)}) collective-permute-start(bf16[32,16,128]{2,1,0:T(8,128)(2,1)S(1)} %get-tuple-element.23), channel_id=1, source_target_pairs={{0,1},{1,0},{2,3},{3,2},{4,5},{5,4},{6,7},{7,6},{8,9},{9,8},{10,11... | collective-permute-start | bytes 393224 | tf_op jit(solution)/shard_map/ppermute | solution.py:220
  8.2 8.5 %collective-permute-start.16 = (bf16[32,16,128]{2,1,0:T(8,128)(2,1)S(1)}, bf16[32,16,128]{2,1,0:T(8,128)(2,1)S(1)}, u32[]{:S(2)}, u32[]{:S(2)}) collective-permute-start(bf16[32,16,128]{2,1,0:T(8,128)(2,1)S(1)} %get-tuple-element.24), channel_id=1, source_target_pairs={{0,4},{1,5},{2,6},{3,7},{4,0},{5,1},{6,2},{7,3},{8,12},{9,13},{10,... | collective-permute-start | bytes 393224 | tf_op jit(solution)/shard_map/ppermute | solution.py:220
  9.7 8.4 %collective-permute-start.17 = (bf16[32,16,128]{2,1,0:T(8,128)(2,1)S(1)}, bf16[32,16,128]{2,1,0:T(8,128)(2,1)S(1)}, u32[]{:S(2)}, u32[]{:S(2)}) collective-permute-start(bf16[32,16,128]{2,1,0:T(8,128)(2,1)S(1)} %get-tuple-element.25), channel_id=1, source_target_pairs={{0,5},{1,4},{2,7},{3,6},{4,1},{5,0},{6,3},{7,2},{8,13},{9,12},{10,... | collective-permute-start | bytes 393224 | tf_op jit(solution)/shard_map/ppermute | solution.py:220
  11.5 6.8 %collective-permute-start.18 = (bf16[32,16,128]{2,1,0:T(8,128)(2,1)S(1)}, bf16[32,16,128]{2,1,0:T(8,128)(2,1)S(1)}, u32[]{:S(2)}, u32[]{:S(2)}) collective-permute-start(bf16[32,16,128]{2,1,0:T(8,128)(2,1)S(1)} %get-tuple-element.22.refs_16_), channel_id=1, source_target_pairs={{0,8},{1,9},{2,10},{3,11},{4,12},{5,13},{6,14},{7,15},{8,0},{9,1},... | collective-permute-start | bytes 393224 | tf_op jit(solution)/shard_map/ppermute | solution.py:220
  13.6 4.8 %collective-permute-start.7 = (bf16[32,16,128]{2,1,0:T(8,128)(2,1)S(1)}, bf16[32,16,128]{2,1,0:T(8,128)(2,1)S(1)}, u32[]{:S(2)}, u32[]{:S(2)}) collective-permute-start(bf16[32,16,128]{2,1,0:T(8,128)(2,1)S(1)} %get-tuple-element.18.refs_0_), channel_id=1, source_target_pairs={{0,2},{1,3},{2,0},{3,1},{4,6},{5,7},{6,4},{7,5},{8,10},{9,11},{10,... | collective-permute-start | bytes 393224 | tf_op jit(solution)/shard_map/ppermute | solution.py:220
  14.1 12.4 %collective-permute-start.3 = (bf16[32,16,128]{2,1,0:T(8,128)(2,1)S(1)}, bf16[32,16,128]{2,1,0:T(8,128)(2,1)S(1)}, u32[]{:S(2)}, u32[]{:S(2)}) collective-permute-start(bf16[32,16,128]{2,1,0:T(8,128)(2,1)S(1)} %get-tuple-element.18.refs_0_), channel_id=1, source_target_pairs={{0,16},{1,17},{2,18},{3,19},{4,20},{5,21},{6,22},{7,23},{8,24},{9,... | collective-permute-start | bytes 393224 | tf_op jit(solution)/shard_map/ppermute | solution.py:220
  16.7 9.8 %collective-permute-start.8 = (bf16[32,16,128]{2,1,0:T(8,128)(2,1)S(1)}, bf16[32,16,128]{2,1,0:T(8,128)(2,1)S(1)}, u32[]{:S(2)}, u32[]{:S(2)}) collective-permute-start(bf16[32,16,128]{2,1,0:T(8,128)(2,1)S(1)} %collective-permute-done.refs_1_), channel_id=1, source_target_pairs={{0,2},{1,3},{2,0},{3,1},{4,6},{5,7},{6,4},{7,5},{8,10},{9,11},{10,... | collective-permute-start | bytes 393224 | tf_op jit(solution)/shard_map/ppermute | solution.py:220
  18.1 11.8 %collective-permute-start.4 = (bf16[32,16,128]{2,1,0:T(8,128)(2,1)S(1)}, bf16[32,16,128]{2,1,0:T(8,128)(2,1)S(1)}, u32[]{:S(2)}, u32[]{:S(2)}) collective-permute-start(bf16[32,16,128]{2,1,0:T(8,128)(2,1)S(1)} %collective-permute-done.refs_1_), channel_id=1, source_target_pairs={{0,16},{1,17},{2,18},{3,19},{4,20},{5,21},{6,22},{7,23},{8,24},{9,... | collective-permute-start | bytes 393224 | tf_op jit(solution)/shard_map/ppermute | solution.py:220
  18.3 17.7 %collective-permute-start.9 = (bf16[32,16,128]{2,1,0:T(8,128)(2,1)S(1)}, bf16[32,16,128]{2,1,0:T(8,128)(2,1)S(1)}, u32[]{:S(2)}, u32[]{:S(2)}) collective-permute-start(bf16[32,16,128]{2,1,0:T(8,128)(2,1)S(1)} %collective-permute-done.1.refs_2_), channel_id=1, source_target_pairs={{0,2},{1,3},{2,0},{3,1},{4,6},{5,7},{6,4},{7,5},{8,10},{9,11},{10,... | collective-permute-start | bytes 393224 | tf_op jit(solution)/shard_map/ppermute | solution.py:220
  18.3 17.7 %collective-permute-start.5 = (bf16[32,16,128]{2,1,0:T(8,128)(2,1)S(1)}, bf16[32,16,128]{2,1,0:T(8,128)(2,1)S(1)}, u32[]{:S(2)}, u32[]{:S(2)}) collective-permute-start(bf16[32,16,128]{2,1,0:T(8,128)(2,1)S(1)} %collective-permute-done.1.refs_2_), channel_id=1, source_target_pairs={{0,16},{1,17},{2,18},{3,19},{4,20},{5,21},{6,22},{7,23},{8,24},{9,... | collective-permute-start | bytes 393224 | tf_op jit(solution)/shard_map/ppermute | solution.py:220
  26.5 12.3 %collective-permute-start.10 = (bf16[32,16,128]{2,1,0:T(8,128)(2,1)S(1)}, bf16[32,16,128]{2,1,0:T(8,128)(2,1)S(1)}, u32[]{:S(2)}, u32[]{:S(2)}) collective-permute-start(bf16[32,16,128]{2,1,0:T(8,128)(2,1)S(1)} %collective-permute-done.2.refs_3_), channel_id=1, source_target_pairs={{0,2},{1,3},{2,0},{3,1},{4,6},{5,7},{6,4},{7,5},{8,10},{9,11},{10,... | collective-permute-start | bytes 393224 | tf_op jit(solution)/shard_map/ppermute | solution.py:220
  26.5 12.3 %collective-permute-start.6 = (bf16[32,16,128]{2,1,0:T(8,128)(2,1)S(1)}, bf16[32,16,128]{2,1,0:T(8,128)(2,1)S(1)}, u32[]{:S(2)}, u32[]{:S(2)}) collective-permute-start(bf16[32,16,128]{2,1,0:T(8,128)(2,1)S(1)} %collective-permute-done.2.refs_3_), channel_id=1, source_target_pairs={{0,16},{1,17},{2,18},{3,19},{4,20},{5,21},{6,22},{7,23},{8,24},{9,... | collective-permute-start | bytes 393224 | tf_op jit(solution)/shard_map/ppermute | solution.py:220
  29.9 12.0 %collective-permute-start.19 = (bf16[32,16,128]{2,1,0:T(8,128)(2,1)S(1)}, bf16[32,16,128]{2,1,0:T(8,128)(2,1)S(1)}, u32[]{:S(2)}, u32[]{:S(2)}) collective-permute-start(bf16[32,16,128]{2,1,0:T(8,128)(2,1)S(1)} %collective-permute-done.15.refs_17_), channel_id=1, source_target_pairs={{0,8},{1,9},{2,10},{3,11},{4,12},{5,13},{6,14},{7,15},{8,0},{9,1},... | collective-permute-start | bytes 393224 | tf_op jit(solution)/shard_map/ppermute | solution.py:220
  36.0 8.8 %collective-permute-start.20 = (bf16[32,16,128]{2,1,0:T(8,128)(2,1)S(1)}, bf16[32,16,128]{2,1,0:T(8,128)(2,1)S(1)}, u32[]{:S(2)}, u32[]{:S(2)}) collective-permute-start(bf16[32,16,128]{2,1,0:T(8,128)(2,1)S(1)} %collective-permute-done.16.refs_18_), channel_id=1, source_target_pairs={{0,8},{1,9},{2,10},{3,11},{4,12},{5,13},{6,14},{7,15},{8,0},{9,1},... | collective-permute-start | bytes 393224 | tf_op jit(solution)/shard_map/ppermute | solution.py:220
  36.0 11.4 %collective-permute-start.21 = (bf16[32,16,128]{2,1,0:T(8,128)(2,1)S(1)}, bf16[32,16,128]{2,1,0:T(8,128)(2,1)S(1)}, u32[]{:S(2)}, u32[]{:S(2)}) collective-permute-start(bf16[32,16,128]{2,1,0:T(8,128)(2,1)S(1)} %collective-permute-done.17.refs_19_), channel_id=1, source_target_pairs={{0,8},{1,9},{2,10},{3,11},{4,12},{5,13},{6,14},{7,15},{8,0},{9,1},... | collective-permute-start | bytes 393224 | tf_op jit(solution)/shard_map/ppermute | solution.py:220
  38.8 8.6 %collective-permute-start.11 = (bf16[32,16,128]{2,1,0:T(8,128)(2,1)S(1)}, bf16[32,16,128]{2,1,0:T(8,128)(2,1)S(1)}, u32[]{:S(2)}, u32[]{:S(2)}) collective-permute-start(bf16[32,16,128]{2,1,0:T(8,128)(2,1)S(1)} %collective-permute-done.3.refs_4_), channel_id=1, source_target_pairs={{0,2},{1,3},{2,0},{3,1},{4,6},{5,7},{6,4},{7,5},{8,10},{9,11},{10,... | collective-permute-start | bytes 393224 | tf_op jit(solution)/shard_map/ppermute | solution.py:220
  38.8 8.6 %collective-permute-start.12 = (bf16[32,16,128]{2,1,0:T(8,128)(2,1)S(1)}, bf16[32,16,128]{2,1,0:T(8,128)(2,1)S(1)}, u32[]{:S(2)}, u32[]{:S(2)}) collective-permute-start(bf16[32,16,128]{2,1,0:T(8,128)(2,1)S(1)} %collective-permute-done.4.refs_5_), channel_id=1, source_target_pairs={{0,2},{1,3},{2,0},{3,1},{4,6},{5,7},{6,4},{7,5},{8,10},{9,11},{10,... | collective-permute-start | bytes 393224 | tf_op jit(solution)/shard_map/ppermute | solution.py:220
  41.9 5.5 %collective-permute-start.13 = (bf16[32,16,128]{2,1,0:T(8,128)(2,1)S(1)}, bf16[32,16,128]{2,1,0:T(8,128)(2,1)S(1)}, u32[]{:S(2)}, u32[]{:S(2)}) collective-permute-start(bf16[32,16,128]{2,1,0:T(8,128)(2,1)S(1)} %collective-permute-done.5.refs_6_), channel_id=1, source_target_pairs={{0,2},{1,3},{2,0},{3,1},{4,6},{5,7},{6,4},{7,5},{8,10},{9,11},{10,... | collective-permute-start | bytes 393224 | tf_op jit(solution)/shard_map/ppermute | solution.py:220
  44.7 2.7 %collective-permute-start.14 = (bf16[32,16,128]{2,1,0:T(8,128)(2,1)S(1)}, bf16[32,16,128]{2,1,0:T(8,128)(2,1)S(1)}, u32[]{:S(2)}, u32[]{:S(2)}) collective-permute-start(bf16[32,16,128]{2,1,0:T(8,128)(2,1)S(1)} %collective-permute-done.6.refs_7_), channel_id=1, source_target_pairs={{0,2},{1,3},{2,0},{3,1},{4,6},{5,7},{6,4},{7,5},{8,10},{9,11},{10,... | collective-permute-start | bytes 393224 | tf_op jit(solution)/shard_map/ppermute | solution.py:220

commit v3 on v2

--- a/solution.py
+++ b/solution.py
@@ -63,9 +63,8 @@
 VMEM = pl.BlockSpec(memory_space=pltpu.MemorySpace.VMEM)
 
 
-def gated(gate, value):
-    half = 0.5 * value
-    return half * jnp.tanh(0.5 * gate) + half
+def gated(half_gate, half_value):
+    return half_value * jnp.tanh(half_gate) + half_value
 
 
 def in_hbm(array):
@@ -84,41 +83,49 @@
     return [copy.wait for copy in copies]
 
 
-def turned(weights):
-    return weights.astype(F32).T.astype(BF16)
-
-
-def project(normed, w_turned, mask_ref, side_scr):
+def turn(w_ref, w_turned):
+    hidden = w_ref.shape[1] // 2
+    for part, scale in enumerate((0.5, 1.0)):
+        columns = w_ref[:, part * hidden : (part + 1) * hidden].astype(F32)
+        w_turned[part * hidden : (part + 1) * hidden, :] = (scale * columns).T.astype(BF16)
+
+
+def project(normed, w_turned, mask_ref, side_scr, first):
     rows, cols = mask_ref.shape
-    hidden = side_scr.shape[1] // rows
-    for side in range(2):
-        weights = w_turned[2 * side * hidden : (2 * side + 2) * hidden, :]
-        projected = lax.dot_general(weights, normed, NT, preferred_element_type=F32)
-        for row in range(rows):
-            here = projected[:, row * cols : (row + 1) * cols]
-            masked = mask_ref[row : row + 1, :].astype(F32)
-            side_scr[side, pl.ds(row, hidden, stride=rows), :] = masked * gated(here[:hidden], here[hidden:])
-
-
-def cut(side_scr, side, outs):
+    hidden = w_turned.shape[0] // 2
+    projected = lax.dot_general(w_turned[...], normed, NT, preferred_element_type=F32)
+    for at in range(normed.shape[0] // cols):
+        row = first + at
+        here = projected[:, at * cols : (at + 1) * cols]
+        half_masked = 0.5 * mask_ref[row : row + 1, :].astype(F32)
+        side_scr[pl.ds(row, hidden, stride=rows), :] = gated(here[:hidden], half_masked * here[hidden:])
+
+
+def cut(side_scr, outs):
     _, _, wide, _, col = own_bits()
     share, rows, cols = outs[0].shape
     for offset, out_ref in enumerate(outs):
         start = pl.multiple_of(((2 * wide + col) ^ offset) * (share * rows), share * rows)
-        out_ref[...] = side_scr[side, pl.ds(start, share * rows), :].astype(BF16).reshape(share, rows, cols)
-
-
-def sides_kernel(map_hbm, mask_hbm, gain_hbm, bias_hbm, w_hbm, *refs):
-    lefts, rights, normed_ref = refs[:GROUPS], refs[GROUPS : 2 * GROUPS], refs[2 * GROUPS]
-    map_scr, mask_scr, gain_scr, bias_scr, w_scr, w_turned, side_scr, sems = refs[2 * GROUPS + 1 :]
+        out_ref[...] = side_scr[pl.ds(start, share * rows), :].astype(BF16).reshape(share, rows, cols)
+
+
+def right_kernel(map_hbm, mask_hbm, gain_hbm, bias_hbm, w_hbm, *refs):
+    outs, normed_ref = refs[:GROUPS], refs[GROUPS]
+    map_scr, mask_scr, gain_scr, bias_scr, w_scr, w_turned, side_scr, sems = refs[GROUPS + 1 :]
     rows, cols, channels = map_scr.shape
-    hidden = w_scr.shape[1] // 4
+    width = w_scr.shape[1]
     wait_map, wait_w, wait_gain, wait_bias, wait_mask = start_copies(
-        [(map_hbm, map_scr), (w_hbm, w_scr), (gain_hbm, gain_scr), (bias_hbm, bias_scr), (mask_hbm, mask_scr)], sems
+        [
+            (map_hbm, map_scr),
+            (w_hbm.at[:, width : 2 * width], w_scr),
+            (gain_hbm, gain_scr),
+            (bias_hbm, bias_scr),
+            (mask_hbm, mask_scr),
+        ],
+        sems,
     )
     wait_w()
-    for part in range(4):
-        w_turned[part * hidden : (part + 1) * hidden, :] = turned(w_scr[:, part * hidden : (part + 1) * hidden])
+    turn(w_scr, w_turned)
     wait_gain()
     wait_bias()
     wait_mask()
@@ -126,12 +133,32 @@
     values = map_scr[...].reshape(rows * cols, channels)
     normed = layer_norm(values, gain_scr[...], bias_scr[...]).astype(BF16)
     normed_ref[...] = normed
-    project(normed, w_turned, mask_scr, side_scr)
-    cut(side_scr, 0, lefts)
-    cut(side_scr, 1, rights)
-
-
-def gates_kernel(normed_ref, w_gate_ref, gain_hbm, bias_hbm, w_out_hbm, gating_ref, gain_ref, bias_ref, w_out_ref, sems):
+    project(normed, w_turned, mask_scr, side_scr, 0)
+    cut(side_scr, outs)
+
+
+def left_kernel(normed_ref, mask_ref, w_ref, *refs):
+    outs, (w_turned, side_scr) = refs[:GROUPS], refs[GROUPS:]
+    rows, cols = mask_ref.shape
+    turn(w_ref.at[:, : w_ref.shape[1] // 2], w_turned)
+    block = rows // 4
+    for step in range(4):
+        normed = normed_ref[step * block * cols : (step + 1) * block * cols, :]
+        project(normed, w_turned, mask_ref, side_scr, step * block)
+    cut(side_scr, outs)
+
+
+def lay_out(pieces, out_ref):
+    _, _, wide, core, _ = own_bits()
+    rows = pieces[0].shape[1]
+    for n, piece in enumerate(pieces):
+        block = 2 * (wide ^ ((n >> 1) & 1)) + (core ^ (n >> 2))
+        out_ref[n & 1, :, pl.ds(pl.multiple_of(block * rows, rows), rows), :] = piece[...]
+
+
+def gates_kernel(normed_ref, w_gate_ref, *refs):
+    pieces, (gain_hbm, bias_hbm, w_out_hbm) = refs[: 2 * GROUPS], refs[2 * GROUPS : 2 * GROUPS + 3]
+    gating_ref, gain_ref, bias_ref, w_out_ref, near_ref, sems = refs[2 * GROUPS + 3 :]
     waits = start_copies([(gain_hbm, gain_ref), (bias_hbm, bias_ref), (w_out_hbm, w_out_ref)], sems)
     rows, cols, channels = gating_ref.shape
     block = rows // 4
@@ -141,19 +168,17 @@
         gating_ref[step * block : (step + 1) * block] = (0.5 * jnp.tanh(0.5 * gates) + 0.5).reshape(
             block, cols, channels
         )
+    lay_out(pieces, near_ref)
     for wait in waits:
         wait()
 
 
-def pairs_kernel(*refs):
-    rights, lefts, out_ref, scr = refs[: 4 * GROUPS], refs[4 * GROUPS : 6 * GROUPS], refs[-2], refs[-1]
-    half, parity, wide, core, _ = own_bits()
+def pairs_kernel(near_ref, *refs):
+    pieces, lefts, (out_ref, far_scr) = refs[: 2 * GROUPS], refs[2 * GROUPS : 4 * GROUPS], refs[4 * GROUPS :]
+    half, parity, wide, _, _ = own_bits()
     share, rows, _ = lefts[0].shape
-    for n, piece in enumerate(rights):
-        other_core, other_half, other_wide, other_col = [(n >> bit) & 1 for bit in (3, 2, 1, 0)]
-        block = 4 * (half ^ other_half) + 2 * (wide ^ other_wide) + (core ^ other_core)
-        scr[other_col, :, pl.ds(pl.multiple_of(block * rows, rows), rows), :] = piece[...]
-    count = scr.shape[2]
+    lay_out(pieces, far_scr)
+    count = 2 * far_scr.shape[2]
     first = lax.broadcasted_iota(jnp.int32, (GROUPS, rows // 2, count), 2) < count // 2
     for pair in range(share // 2):
         packed = []
@@ -161,7 +186,9 @@
             left = jnp.concatenate(
                 [jnp.concatenate([lefts[2 * at + q][c] for at in range(GROUPS)], axis=0) for q in range(2)], axis=1
             )
-            right = jnp.concatenate([scr[q, c] for q in range(2)], axis=1)
+            right = jnp.concatenate(
+                [jnp.concatenate([near_ref[q, c], far_scr[q, c]], axis=0) for q in range(2)], axis=1
+            )
             summed = lax.dot_general(left, right, NT, preferred_element_type=F32)
             rolled = pltpu.roll(summed, count // 2, 1).reshape(GROUPS, 2, rows // 2, count)
             summed = summed.reshape(GROUPS, 2, rows // 2, count)
@@ -174,7 +201,8 @@
         for at in range(GROUPS):
             place = 4 * (parity ^ (at >> 1)) + 2 * (wide ^ (at & 1))
             for q in range(2):
-                out_ref[place + q, pair] = jnp.concatenate([packed[0][q][at], packed[1][q][at]], axis=0).astype(BF16)
+                sums = jnp.concatenate([packed[0][q][at], packed[1][q][at]], axis=0)
+                out_ref[place + (half ^ q), pair] = sums.astype(BF16)
 
 
 def output_kernel(summed_ref, gating_ref, gain_ref, bias_ref, w_ref, out_hbm, scr, out_scr, sems):
@@ -222,53 +250,73 @@
     params = pltpu.CompilerParams(vmem_limit_bytes=VMEM_LIMIT)
     inputs = (pair_map, pair_mask, in_gain.reshape(1, -1), in_bias.reshape(1, -1), w_proj)
     piece = jax.ShapeDtypeStruct((share, rows, cols), BF16)
-    *pieces, normed = pl.pallas_call(
-        sides_kernel,
+    laid_out = jax.ShapeDtypeStruct((2, share, 4 * rows, cols), BF16)
+    turned_shape = pltpu.VMEM((2 * hidden, channels), BF16)
+    side_shape = pltpu.VMEM((hidden * rows, cols), F32)
+    *rights, normed = pl.pallas_call(
+        right_kernel,
         in_specs=[HBM] * 5,
-        out_specs=[VMEM] * (2 * GROUPS + 1),
-        out_shape=[piece] * (2 * GROUPS) + [jax.ShapeDtypeStruct((rows * cols, channels), BF16)],
+        out_specs=[VMEM] * (GROUPS + 1),
+        out_shape=[piece] * GROUPS + [jax.ShapeDtypeStruct((rows * cols, channels), BF16)],
         scratch_shapes=[
             pltpu.VMEM((rows, cols, channels), F32),
             pltpu.VMEM((rows, cols), pair_mask.dtype),
             pltpu.VMEM((1, channels), F32),
             pltpu.VMEM((1, channels), F32),
-            pltpu.VMEM((channels, 4 * hidden), BF16),
-            pltpu.VMEM((4 * hidden, channels), BF16),
-            pltpu.VMEM((2, hidden * rows, cols), F32),
+            pltpu.VMEM((channels, 2 * hidden), BF16),
+            turned_shape,
+            side_shape,
             pltpu.SemaphoreType.DMA((5,)),
         ],
         compiler_params=params,
-        name="sides",
+        name="right",
     )(*[in_hbm(x) for x in inputs])
-    lefts, rights = pieces[:GROUPS], pieces[GROUPS:]
+    lefts = pl.pallas_call(
+        left_kernel,
+        in_specs=[VMEM] * 3,
+        out_specs=[VMEM] * GROUPS,
+        out_shape=[piece] * GROUPS,
+        scratch_shapes=[turned_shape, side_shape],
+        compiler_params=params,
+        name="left",
+    )(normed, pair_mask, w_proj)
     lefts = [swap(x, plane[n]) for n, x in enumerate(lefts)]
     lefts += [swap(x, parity) for x in lefts]
     rights = [swap(x, plane[n]) for n, x in enumerate(rights)]
     rights += [swap(x, half) for x in rights]
-    rights += [swap(x, core) for x in rights]
-    gating, gain, bias, w_last = pl.pallas_call(
+    across = [swap(x, core) for x in rights]
+    gating, gain, bias, w_last, near = pl.pallas_call(
         gates_kernel,
-        in_specs=[VMEM, VMEM, HBM, HBM, HBM],
-        out_specs=[VMEM] * 4,
+        in_specs=[VMEM] * (2 * GROUPS + 2) + [HBM] * 3,
+        out_specs=[VMEM] * 5,
         out_shape=[
             jax.ShapeDtypeStruct((rows, cols, channels), F32),
             jax.ShapeDtypeStruct((1, hidden), F32),
             jax.ShapeDtypeStruct((1, hidden), F32),
             jax.ShapeDtypeStruct(w_out.shape, BF16),
+            laid_out,
         ],
         scratch_shapes=[pltpu.SemaphoreType.DMA((3,))],
         compiler_params=params,
         name="gates",
-    )(normed, w_gate, in_hbm(out_gain.reshape(1, -1)), in_hbm(out_bias.reshape(1, -1)), in_hbm(w_out))
+    )(
+        normed,
+        w_gate,
+        *rights[:GROUPS],
+        *across[:GROUPS],
+        in_hbm(out_gain.reshape(1, -1)),
+        in_hbm(out_bias.reshape(1, -1)),
+        in_hbm(w_out),
+    )
     summed = pl.pallas_call(
         pairs_kernel,
-        in_specs=[VMEM] * (6 * GROUPS + 1),
+        in_specs=[VMEM] * (4 * GROUPS + 1),
         out_specs=VMEM,
         out_shape=jax.ShapeDtypeStruct((2 * GROUPS, share // 2, rows, cols), BF16),
-        scratch_shapes=[pltpu.VMEM((2, share, 8 * rows, cols), BF16)],
+        scratch_shapes=[pltpu.VMEM(laid_out.shape, BF16)],
         compiler_params=params,
         name="pairs",
-    )(*rights, *lefts, gain)
+    )(near, *rights[GROUPS:], *across[GROUPS:], *lefts)
     circles = [
         [own + other + offset for other in (0, parity) for offset in plane]
         for own in (0, core, half, half + core)

time: 66 us -> 59.9 us (0.908)
  the two profiles are of different devices: /device:TPU:16 before, /device:TPU:0 now
where the time goes in v3:
time: 59.9 us; the launch traced here: 59.7 us
  starting transfers between devices  22.2 us (37%)
  waiting for transfers between devices  16.9 us (28%)
  blocking collectives  13.4 us (22%)
  Pallas kernels  7 us (12%)
    ppermute x22, starting transfers between devices, swap(): lax.ppermute(array, ('row', 'col'), [(n, n ^ offset) for n in devices])  22.2 us
    ppermute x22, waiting for transfers between devices, swap(): lax.ppermute(array, ('row', 'col'), [(n, n ^ offset) for n in devices])  16.9 us
    all_to_all x1, blocking collectives, exchanged(): lax.all_to_all(summed, ('row', 'col'), 0, 0, tiled=True, axis_index_group...  13.4 us
    pallas_call x1, Pallas kernels, exchanged(): pl.pallas_call(right_kernel, in_specs=[HBM] * 5, out_specs=[VMEM] * (GROU...  2.53 us
    pallas_call x1, Pallas kernels, exchanged(): pl.pallas_call(output_kernel, in_specs=[VMEM] * 5, out_specs=HBM, out_sha...  1.65 us
  transfers between devices with their start and end apart: 22, of which 11 were waited for; matrix products, arithmetic and copies ran while one was open for 0% of the time, Pallas kernels for 3%

profile of v3, /device:TPU:0, one launch (start us, length us, event | category | flops | bytes accessed | tf_op | source)
XLA Modules:
  0.0 59.7 jit_solution(13129232947974222841)
XLA Ops:
  0.0 2.5 %right.1 = (bf16[32,16,128]{2,1,0:T(8,128)(2,1)S(1)}, bf16[32,16,128]{2,1,0:T(8,128)(2,1)S(1)}, bf16[32,16,128]{2,1,0:T(8,128)(2,1)S(1)}, bf16[32,16,128]{2,1,0:T(8,128)(2,1)S(1)}, bf16[2048,128]{1,0:T(8,128)(2,1)S(1)}) custom-call(f32[16,128,128]{2,1,0:T(8,128)} %map_hbm.1, s32[16,128]{1,0:T(8,128)} %mask_ref.1, f32[1,128]{1,0:T(1,128)} %bitcast.4, ...), custom_call_target="tpu_custom_call" | custom-call | tf_op jit(solution)/shard_map/right/pallas_call | solution.py:256
  2.5 0.0 copy-start.2
  2.6 3.1 %collective-permute-start = (bf16[32,16,128]{2,1,0:T(8,128)(2,1)S(1)}, bf16[32,16,128]{2,1,0:T(8,128)(2,1)S(1)}, u32[]{:S(2)}, u32[]{:S(2)}) collective-permute-start(bf16[32,16,128]{2,1,0:T(8,128)(2,1)S(1)} %get-tuple-element.21), channel_id=1, source_target_pairs={{0,1},{1,0},{2,3},{3,2},{4,5},{5,4},{6,7},{7,6},{8,9},{9,8},{10,11... | collective-permute-start | bytes 393224 | tf_op jit(solution)/shard_map/ppermute | solution.py:248
  5.6 1.5 %collective-permute-start.1 = (bf16[32,16,128]{2,1,0:T(8,128)(2,1)S(1)}, bf16[32,16,128]{2,1,0:T(8,128)(2,1)S(1)}, u32[]{:S(2)}, u32[]{:S(2)}) collective-permute-start(bf16[32,16,128]{2,1,0:T(8,128)(2,1)S(1)} %get-tuple-element.22), channel_id=1, source_target_pairs={{0,4},{1,5},{2,6},{3,7},{4,0},{5,1},{6,2},{7,3},{8,12},{9,13},{10,... | collective-permute-start | bytes 393224 | tf_op jit(solution)/shard_map/ppermute | solution.py:248
  7.1 0.1 collective-permute-start.2
  7.2 0.0 collective-permute-start.3
  7.2 0.0 copy-start.1
  7.2 0.7 %left.1 = (bf16[32,16,128]{2,1,0:T(8,128)(2,1)S(1)}, bf16[32,16,128]{2,1,0:T(8,128)(2,1)S(1)}, bf16[32,16,128]{2,1,0:T(8,128)(2,1)S(1)}, bf16[32,16,128]{2,1,0:T(8,128)(2,1)S(1)}) custom-call(bf16[2048,128]{1,0:T(8,128)(2,1)S(1)} %get-tuple-element.19.normed_ref, s32[16,128]{1,0:T(8,128)S(1)} %copy-done.2, bf16[128,512]{1,0:T(8,128)(2,1)S(1)} %copy-done), custom_call_target="tpu_custom_call" | custom-call | tf_op jit(solution)/shard_map/left/pallas_call | solution.py:274
  7.9 2.0 %collective-permute-start.15 = (bf16[32,16,128]{2,1,0:T(8,128)(2,1)S(1)}, bf16[32,16,128]{2,1,0:T(8,128)(2,1)S(1)}, u32[]{:S(2)}, u32[]{:S(2)}) collective-permute-start(bf16[32,16,128]{2,1,0:T(8,128)(2,1)S(1)} %get-tuple-element.26), channel_id=1, source_target_pairs={{0,1},{1,0},{2,3},{3,2},{4,5},{5,4},{6,7},{7,6},{8,9},{9,8},{10,11... | collective-permute-start | bytes 393224 | tf_op jit(solution)/shard_map/ppermute | solution.py:248
  9.9 0.0 collective-permute-done.refs_1_
  9.9 1.5 %collective-permute-start.16 = (bf16[32,16,128]{2,1,0:T(8,128)(2,1)S(1)}, bf16[32,16,128]{2,1,0:T(8,128)(2,1)S(1)}, u32[]{:S(2)}, u32[]{:S(2)}) collective-permute-start(bf16[32,16,128]{2,1,0:T(8,128)(2,1)S(1)} %get-tuple-element.27), channel_id=1, source_target_pairs={{0,4},{1,5},{2,6},{3,7},{4,0},{5,1},{6,2},{7,3},{8,12},{9,13},{10,... | collective-permute-start | bytes 393224 | tf_op jit(solution)/shard_map/ppermute | solution.py:248
  11.4 0.6 collective-permute-done.1.refs_2_
  12.0 1.4 %collective-permute-start.17 = (bf16[32,16,128]{2,1,0:T(8,128)(2,1)S(1)}, bf16[32,16,128]{2,1,0:T(8,128)(2,1)S(1)}, u32[]{:S(2)}, u32[]{:S(2)}) collective-permute-start(bf16[32,16,128]{2,1,0:T(8,128)(2,1)S(1)} %get-tuple-element.28), channel_id=1, source_target_pairs={{0,5},{1,4},{2,7},{3,6},{4,1},{5,0},{6,3},{7,2},{8,13},{9,12},{10,... | collective-permute-start | bytes 393224 | tf_op jit(solution)/shard_map/ppermute | solution.py:248
  13.4 0.4 collective-permute-done.2.refs_3_
  13.8 1.7 %collective-permute-start.18 = (bf16[32,16,128]{2,1,0:T(8,128)(2,1)S(1)}, bf16[32,16,128]{2,1,0:T(8,128)(2,1)S(1)}, u32[]{:S(2)}, u32[]{:S(2)}) collective-permute-start(bf16[32,16,128]{2,1,0:T(8,128)(2,1)S(1)} %get-tuple-element.25.refs_8_), channel_id=1, source_target_pairs={{0,8},{1,9},{2,10},{3,11},{4,12},{5,13},{6,14},{7,15},{8,0},{9,1},... | collective-permute-start | bytes 393224 | tf_op jit(solution)/shard_map/ppermute | solution.py:248
  15.6 0.0 collective-permute-done.3.refs_4_
  15.6 2.6 %collective-permute-start.7 = (bf16[32,16,128]{2,1,0:T(8,128)(2,1)S(1)}, bf16[32,16,128]{2,1,0:T(8,128)(2,1)S(1)}, u32[]{:S(2)}, u32[]{:S(2)}) collective-permute-start(bf16[32,16,128]{2,1,0:T(8,128)(2,1)S(1)} %get-tuple-element.20.refs_0_), channel_id=1, source_target_pairs={{0,16},{1,17},{2,18},{3,19},{4,20},{5,21},{6,22},{7,23},{8,24},{9,... | collective-permute-start | bytes 393224 | tf_op jit(solution)/shard_map/ppermute | solution.py:248
  18.2 0.0 collective-permute-done.15.refs_9_
  18.2 0.0 collective-permute-start.4
  18.2 0.0 collective-permute-done.16.refs_10_
  18.2 0.5 collective-permute-start.5
  18.7 0.1 collective-permute-done.17.refs_11_
  18.8 0.0 collective-permute-start.6
  18.8 1.2 %collective-permute-done.18.refs_12_ = bf16[32,16,128]{2,1,0:T(8,128)(2,1)S(1)} collective-permute-done((bf16[32,16,128]{2,1,0:T(8,128)(2,1)S(1)}, bf16[32,16,128]{2,1,0:T(8,128)(2,1)S(1)}, u32[]{:S(2)}, u32[]{:S(2)}) %collective-permute-start.18) | collective-permute-done | bytes 131104 | tf_op jit(solution)/shard_map/ppermute | solution.py:248
  20.0 1.7 %collective-permute-start.19 = (bf16[32,16,128]{2,1,0:T(8,128)(2,1)S(1)}, bf16[32,16,128]{2,1,0:T(8,128)(2,1)S(1)}, u32[]{:S(2)}, u32[]{:S(2)}) collective-permute-start(bf16[32,16,128]{2,1,0:T(8,128)(2,1)S(1)} %collective-permute-done.15.refs_9_), channel_id=1, source_target_pairs={{0,8},{1,9},{2,10},{3,11},{4,12},{5,13},{6,14},{7,15},{8,0},{9,1},... | collective-permute-start | bytes 393224 | tf_op jit(solution)/shard_map/ppermute | solution.py:248
  21.7 1.3 %collective-permute-done.7.refs_0_ = bf16[32,16,128]{2,1,0:T(8,128)(2,1)S(1)} collective-permute-done((bf16[32,16,128]{2,1,0:T(8,128)(2,1)S(1)}, bf16[32,16,128]{2,1,0:T(8,128)(2,1)S(1)}, u32[]{:S(2)}, u32[]{:S(2)}) %collective-permute-start.7) | collective-permute-done | bytes 131104 | tf_op jit(solution)/shard_map/ppermute | solution.py:248
  23.0 0.3 collective-permute-start.20
  23.3 0.0 collective-permute-done.4.refs_5_
  23.3 2.9 %collective-permute-start.8 = (bf16[32,16,128]{2,1,0:T(8,128)(2,1)S(1)}, bf16[32,16,128]{2,1,0:T(8,128)(2,1)S(1)}, u32[]{:S(2)}, u32[]{:S(2)}) collective-permute-start(bf16[32,16,128]{2,1,0:T(8,128)(2,1)S(1)} %collective-permute-done.refs_1_), channel_id=1, source_target_pairs={{0,16},{1,17},{2,18},{3,19},{4,20},{5,21},{6,22},{7,23},{8,24},{9,... | collective-permute-start | bytes 393224 | tf_op jit(solution)/shard_map/ppermute | solution.py:248
  26.3 0.0 collective-permute-done.5.refs_6_
  26.3 0.1 collective-permute-start.9
  26.3 2.9 %collective-permute-start.10 = (bf16[32,16,128]{2,1,0:T(8,128)(2,1)S(1)}, bf16[32,16,128]{2,1,0:T(8,128)(2,1)S(1)}, u32[]{:S(2)}, u32[]{:S(2)}) collective-permute-start(bf16[32,16,128]{2,1,0:T(8,128)(2,1)S(1)} %collective-permute-done.2.refs_3_), channel_id=1, source_target_pairs={{0,16},{1,17},{2,18},{3,19},{4,20},{5,21},{6,22},{7,23},{8,24},{9,... | collective-permute-start | bytes 393224 | tf_op jit(solution)/shard_map/ppermute | solution.py:248
  29.2 1.6 %collective-permute-done.19.refs_13_ = bf16[32,16,128]{2,1,0:T(8,128)(2,1)S(1)} collective-permute-done((bf16[32,16,128]{2,1,0:T(8,128)(2,1)S(1)}, bf16[32,16,128]{2,1,0:T(8,128)(2,1)S(1)}, u32[]{:S(2)}, u32[]{:S(2)}) %collective-permute-start.19) | collective-permute-done | bytes 131104 | tf_op jit(solution)/shard_map/ppermute | solution.py:248
  30.8 0.0 collective-permute-start.21
  30.8 2.7 %collective-permute-done.20.refs_14_ = bf16[32,16,128]{2,1,0:T(8,128)(2,1)S(1)} collective-permute-done((bf16[32,16,128]{2,1,0:T(8,128)(2,1)S(1)}, bf16[32,16,128]{2,1,0:T(8,128)(2,1)S(1)}, u32[]{:S(2)}, u32[]{:S(2)}) %collective-permute-start.20) | collective-permute-done | bytes 131104 | tf_op jit(solution)/shard_map/ppermute | solution.py:248
  33.5 5.6 %collective-permute-done.8.refs_1_ = bf16[32,16,128]{2,1,0:T(8,128)(2,1)S(1)} collective-permute-done((bf16[32,16,128]{2,1,0:T(8,128)(2,1)S(1)}, bf16[32,16,128]{2,1,0:T(8,128)(2,1)S(1)}, u32[]{:S(2)}, u32[]{:S(2)}) %collective-permute-start.8) | collective-permute-done | bytes 131104 | tf_op jit(solution)/shard_map/ppermute | solution.py:248
  39.0 0.0 collective-permute-start.12
  39.0 1.8 %collective-permute-done.9.refs_2_ = bf16[32,16,128]{2,1,0:T(8,128)(2,1)S(1)} collective-permute-done((bf16[32,16,128]{2,1,0:T(8,128)(2,1)S(1)}, bf16[32,16,128]{2,1,0:T(8,128)(2,1)S(1)}, u32[]{:S(2)}, u32[]{:S(2)}) %collective-permute-start.9) | collective-permute-done | bytes 131104 | tf_op jit(solution)/shard_map/ppermute | solution.py:248
  40.8 1.4 %collective-permute-done.10.refs_3_ = bf16[32,16,128]{2,1,0:T(8,128)(2,1)S(1)} collective-permute-done((bf16[32,16,128]{2,1,0:T(8,128)(2,1)S(1)}, bf16[32,16,128]{2,1,0:T(8,128)(2,1)S(1)}, u32[]{:S(2)}, u32[]{:S(2)}) %collective-permute-start.10) | collective-permute-done | bytes 131104 | tf_op jit(solution)/shard_map/ppermute | solution.py:248
  42.2 0.0 collective-permute-start.14
  42.2 1.0 %gates.1 = (f32[16,128,128]{2,1,0:T(8,128)S(1)}, f32[1,128]{1,0:T(1,128)S(1)}, f32[1,128]{1,0:T(1,128)S(1)}, bf16[128,128]{1,0:T(8,128)(2,1)S(1)}, bf16[2,32,64,128]{3,2,1,0:T(8,128)(2,1)S(1)}) custom-call(bf16[2048,128]{1,0:T(8,128)(2,1)S(1)} %get-tuple-element.19.normed_ref, bf16[128,128]{1,0:T(8,128)(2,1)S(1)} %copy-done.1, ...), custom_call_target="tpu_custom_call" | custom-call | tf_op jit(solution)/shard_map/gates/pallas_call | solution.py:288
  43.3 0.0 collective-permute-done.21.refs_15_
  43.3 0.0 collective-permute-done.12.refs_5_
  43.3 0.0 collective-permute-done.13.refs_6_
  43.3 0.3 collective-permute-done.14.refs_7_
  43.6 1.1 %pairs.1 = bf16[8,16,16,128]{3,2,1,0:T(8,128)(2,1)S(1)} custom-call(bf16[2,32,64,128]{3,2,1,0:T(8,128)(2,1)S(1)} %get-tuple-element.24.near_ref, bf16[32,16,128]{2,1,0:T(8,128)(2,1)S(1)} %collective-permute-done.7.refs_0_, bf16[32,16,128]{2,1,0:T(8,128)(2,1)S(1)} %collective-permute-done.8.refs_1_, bf16[32,16,128]{2,1,0:T(8,128)(2,1)S(1)} %collective-permute-done.9.refs_2_, ...), custom_call_target="tpu_custom_call" | custom-call | tf_op jit(solution)/shard_map/pairs/pallas_call | solution.py:311
  44.7 13.4 %all_to_all.5.summed_ref = bf16[8,16,16,128]{3,2,1,0:T(8,128)(2,1)S(1)} all-to-all(bf16[8,16,16,128]{3,2,1,0:T(8,128)(2,1)S(1)} %pairs.1), channel_id=1, replica_groups={{0,1,4,5,8,9,12,13},{2,3,6,7,10,11,14,15},{16,17,20,21,24,25,28,29},{18..., dimensions={0} | all-to-all | bytes 1048576 | tf_op jit(solution)/shard_map/all_to_all | solution.py:324
  58.0 1.7 %output.1 = f32[16,128,128]{2,1,0:T(8,128)} custom-call(bf16[8,16,16,128]{3,2,1,0:T(8,128)(2,1)S(1)} %all_to_all.5.summed_ref, f32[16,128,128]{2,1,0:T(8,128)S(1)} %get-tuple-element.29.gating_ref, f32[1,128]{1,0:T(1,128)S(1)} %get-tuple-element.30.gain_ref, f32[1,128]{1,0:T(1,128)S(1)} %get-tuple-element.31.bias_ref, ...), custom_call_target="tpu_custom_call" | custom-call | tf_op jit(solution)/shard_map/output/pallas_call | solution.py:325
  (8 shorter events, 0.0 us)
Async XLA Ops:
  0.0 7.2 %copy-start = (bf16[128,512]{1,0:T(8,128)(2,1)S(1)}, bf16[128,512]{1,0:T(8,128)(2,1)}, u32[]{:S(2)}) copy-start(bf16[128,512]{1,0:T(8,128)(2,1)} %w_ref.1) | copy-start | bytes 393220
  2.5 4.6 %copy-start.2 = (s32[16,128]{1,0:T(8,128)S(1)}, s32[16,128]{1,0:T(8,128)}, u32[]{:S(2)}) copy-start(s32[16,128]{1,0:T(8,128)} %mask_ref.1) | copy-start | bytes 24580
  2.6 7.4 %collective-permute-start = (bf16[32,16,128]{2,1,0:T(8,128)(2,1)S(1)}, bf16[32,16,128]{2,1,0:T(8,128)(2,1)S(1)}, u32[]{:S(2)}, u32[]{:S(2)}) collective-permute-start(bf16[32,16,128]{2,1,0:T(8,128)(2,1)S(1)} %get-tuple-element.21), channel_id=1, source_target_pairs={{0,1},{1,0},{2,3},{3,2},{4,5},{5,4},{6,7},{7,6},{8,9},{9,8},{10,11... | collective-permute-start | bytes 393224 | tf_op jit(solution)/shard_map/ppermute | solution.py:248
  5.6 6.4 %collective-permute-start.1 = (bf16[32,16,128]{2,1,0:T(8,128)(2,1)S(1)}, bf16[32,16,128]{2,1,0:T(8,128)(2,1)S(1)}, u32[]{:S(2)}, u32[]{:S(2)}) collective-permute-start(bf16[32,16,128]{2,1,0:T(8,128)(2,1)S(1)} %get-tuple-element.22), channel_id=1, source_target_pairs={{0,4},{1,5},{2,6},{3,7},{4,0},{5,1},{6,2},{7,3},{8,12},{9,13},{10,... | collective-permute-start | bytes 393224 | tf_op jit(solution)/shard_map/ppermute | solution.py:248
  7.1 6.7 %collective-permute-start.2 = (bf16[32,16,128]{2,1,0:T(8,128)(2,1)S(1)}, bf16[32,16,128]{2,1,0:T(8,128)(2,1)S(1)}, u32[]{:S(2)}, u32[]{:S(2)}) collective-permute-start(bf16[32,16,128]{2,1,0:T(8,128)(2,1)S(1)} %get-tuple-element.23), channel_id=1, source_target_pairs={{0,5},{1,4},{2,7},{3,6},{4,1},{5,0},{6,3},{7,2},{8,13},{9,12},{10,... | collective-permute-start | bytes 393224 | tf_op jit(solution)/shard_map/ppermute | solution.py:248
  7.2 8.4 %collective-permute-start.3 = (bf16[32,16,128]{2,1,0:T(8,128)(2,1)S(1)}, bf16[32,16,128]{2,1,0:T(8,128)(2,1)S(1)}, u32[]{:S(2)}, u32[]{:S(2)}) collective-permute-start(bf16[32,16,128]{2,1,0:T(8,128)(2,1)S(1)} %get-tuple-element.20.refs_0_), channel_id=1, source_target_pairs={{0,2},{1,3},{2,0},{3,1},{4,6},{5,7},{6,4},{7,5},{8,10},{9,11},{10,... | collective-permute-start | bytes 393224 | tf_op jit(solution)/shard_map/ppermute | solution.py:248
  7.2 35.1 %copy-start.1 = (bf16[128,128]{1,0:T(8,128)(2,1)S(1)}, bf16[128,128]{1,0:T(8,128)(2,1)}, u32[]{:S(2)}) copy-start(bf16[128,128]{1,0:T(8,128)(2,1)} %w_gate_ref.1) | copy-start | bytes 98308
  7.9 10.3 %collective-permute-start.15 = (bf16[32,16,128]{2,1,0:T(8,128)(2,1)S(1)}, bf16[32,16,128]{2,1,0:T(8,128)(2,1)S(1)}, u32[]{:S(2)}, u32[]{:S(2)}) collective-permute-start(bf16[32,16,128]{2,1,0:T(8,128)(2,1)S(1)} %get-tuple-element.26), channel_id=1, source_target_pairs={{0,1},{1,0},{2,3},{3,2},{4,5},{5,4},{6,7},{7,6},{8,9},{9,8},{10,11... | collective-permute-start | bytes 393224 | tf_op jit(solution)/shard_map/ppermute | solution.py:248
  9.9 8.2 %collective-permute-start.16 = (bf16[32,16,128]{2,1,0:T(8,128)(2,1)S(1)}, bf16[32,16,128]{2,1,0:T(8,128)(2,1)S(1)}, u32[]{:S(2)}, u32[]{:S(2)}) collective-permute-start(bf16[32,16,128]{2,1,0:T(8,128)(2,1)S(1)} %get-tuple-element.27), channel_id=1, source_target_pairs={{0,4},{1,5},{2,6},{3,7},{4,0},{5,1},{6,2},{7,3},{8,12},{9,13},{10,... | collective-permute-start | bytes 393224 | tf_op jit(solution)/shard_map/ppermute | solution.py:248
  12.0 6.8 %collective-permute-start.17 = (bf16[32,16,128]{2,1,0:T(8,128)(2,1)S(1)}, bf16[32,16,128]{2,1,0:T(8,128)(2,1)S(1)}, u32[]{:S(2)}, u32[]{:S(2)}) collective-permute-start(bf16[32,16,128]{2,1,0:T(8,128)(2,1)S(1)} %get-tuple-element.28), channel_id=1, source_target_pairs={{0,5},{1,4},{2,7},{3,6},{4,1},{5,0},{6,3},{7,2},{8,13},{9,12},{10,... | collective-permute-start | bytes 393224 | tf_op jit(solution)/shard_map/ppermute | solution.py:248
  13.8 6.2 %collective-permute-start.18 = (bf16[32,16,128]{2,1,0:T(8,128)(2,1)S(1)}, bf16[32,16,128]{2,1,0:T(8,128)(2,1)S(1)}, u32[]{:S(2)}, u32[]{:S(2)}) collective-permute-start(bf16[32,16,128]{2,1,0:T(8,128)(2,1)S(1)} %get-tuple-element.25.refs_8_), channel_id=1, source_target_pairs={{0,8},{1,9},{2,10},{3,11},{4,12},{5,13},{6,14},{7,15},{8,0},{9,1},... | collective-permute-start | bytes 393224 | tf_op jit(solution)/shard_map/ppermute | solution.py:248
  15.6 7.4 %collective-permute-start.7 = (bf16[32,16,128]{2,1,0:T(8,128)(2,1)S(1)}, bf16[32,16,128]{2,1,0:T(8,128)(2,1)S(1)}, u32[]{:S(2)}, u32[]{:S(2)}) collective-permute-start(bf16[32,16,128]{2,1,0:T(8,128)(2,1)S(1)} %get-tuple-element.20.refs_0_), channel_id=1, source_target_pairs={{0,16},{1,17},{2,18},{3,19},{4,20},{5,21},{6,22},{7,23},{8,24},{9,... | collective-permute-start | bytes 393224 | tf_op jit(solution)/shard_map/ppermute | solution.py:248
  18.2 5.2 %collective-permute-start.4 = (bf16[32,16,128]{2,1,0:T(8,128)(2,1)S(1)}, bf16[32,16,128]{2,1,0:T(8,128)(2,1)S(1)}, u32[]{:S(2)}, u32[]{:S(2)}) collective-permute-start(bf16[32,16,128]{2,1,0:T(8,128)(2,1)S(1)} %collective-permute-done.refs_1_), channel_id=1, source_target_pairs={{0,2},{1,3},{2,0},{3,1},{4,6},{5,7},{6,4},{7,5},{8,10},{9,11},{10,... | collective-permute-start | bytes 393224 | tf_op jit(solution)/shard_map/ppermute | solution.py:248
  18.2 8.1 %collective-permute-start.5 = (bf16[32,16,128]{2,1,0:T(8,128)(2,1)S(1)}, bf16[32,16,128]{2,1,0:T(8,128)(2,1)S(1)}, u32[]{:S(2)}, u32[]{:S(2)}) collective-permute-start(bf16[32,16,128]{2,1,0:T(8,128)(2,1)S(1)} %collective-permute-done.1.refs_2_), channel_id=1, source_target_pairs={{0,2},{1,3},{2,0},{3,1},{4,6},{5,7},{6,4},{7,5},{8,10},{9,11},{10,... | collective-permute-start | bytes 393224 | tf_op jit(solution)/shard_map/ppermute | solution.py:248
  18.8 7.5 %collective-permute-start.6 = (bf16[32,16,128]{2,1,0:T(8,128)(2,1)S(1)}, bf16[32,16,128]{2,1,0:T(8,128)(2,1)S(1)}, u32[]{:S(2)}, u32[]{:S(2)}) collective-permute-start(bf16[32,16,128]{2,1,0:T(8,128)(2,1)S(1)} %collective-permute-done.2.refs_3_), channel_id=1, source_target_pairs={{0,2},{1,3},{2,0},{3,1},{4,6},{5,7},{6,4},{7,5},{8,10},{9,11},{10,... | collective-permute-start | bytes 393224 | tf_op jit(solution)/shard_map/ppermute | solution.py:248
  20.0 10.8 %collective-permute-start.19 = (bf16[32,16,128]{2,1,0:T(8,128)(2,1)S(1)}, bf16[32,16,128]{2,1,0:T(8,128)(2,1)S(1)}, u32[]{:S(2)}, u32[]{:S(2)}) collective-permute-start(bf16[32,16,128]{2,1,0:T(8,128)(2,1)S(1)} %collective-permute-done.15.refs_9_), channel_id=1, source_target_pairs={{0,8},{1,9},{2,10},{3,11},{4,12},{5,13},{6,14},{7,15},{8,0},{9,1},... | collective-permute-start | bytes 393224 | tf_op jit(solution)/shard_map/ppermute | solution.py:248
  23.0 10.5 %collective-permute-start.20 = (bf16[32,16,128]{2,1,0:T(8,128)(2,1)S(1)}, bf16[32,16,128]{2,1,0:T(8,128)(2,1)S(1)}, u32[]{:S(2)}, u32[]{:S(2)}) collective-permute-start(bf16[32,16,128]{2,1,0:T(8,128)(2,1)S(1)} %collective-permute-done.16.refs_10_), channel_id=1, source_target_pairs={{0,8},{1,9},{2,10},{3,11},{4,12},{5,13},{6,14},{7,15},{8,0},{9,1},... | collective-permute-start | bytes 393224 | tf_op jit(solution)/shard_map/ppermute | solution.py:248
  23.3 15.7 %collective-permute-start.8 = (bf16[32,16,128]{2,1,0:T(8,128)(2,1)S(1)}, bf16[32,16,128]{2,1,0:T(8,128)(2,1)S(1)}, u32[]{:S(2)}, u32[]{:S(2)}) collective-permute-start(bf16[32,16,128]{2,1,0:T(8,128)(2,1)S(1)} %collective-permute-done.refs_1_), channel_id=1, source_target_pairs={{0,16},{1,17},{2,18},{3,19},{4,20},{5,21},{6,22},{7,23},{8,24},{9,... | collective-permute-start | bytes 393224 | tf_op jit(solution)/shard_map/ppermute | solution.py:248
  26.3 14.6 %collective-permute-start.9 = (bf16[32,16,128]{2,1,0:T(8,128)(2,1)S(1)}, bf16[32,16,128]{2,1,0:T(8,128)(2,1)S(1)}, u32[]{:S(2)}, u32[]{:S(2)}) collective-permute-start(bf16[32,16,128]{2,1,0:T(8,128)(2,1)S(1)} %collective-permute-done.1.refs_2_), channel_id=1, source_target_pairs={{0,16},{1,17},{2,18},{3,19},{4,20},{5,21},{6,22},{7,23},{8,24},{9,... | collective-permute-start | bytes 393224 | tf_op jit(solution)/shard_map/ppermute | solution.py:248
  26.3 15.9 %collective-permute-start.10 = (bf16[32,16,128]{2,1,0:T(8,128)(2,1)S(1)}, bf16[32,16,128]{2,1,0:T(8,128)(2,1)S(1)}, u32[]{:S(2)}, u32[]{:S(2)}) collective-permute-start(bf16[32,16,128]{2,1,0:T(8,128)(2,1)S(1)} %collective-permute-done.2.refs_3_), channel_id=1, source_target_pairs={{0,16},{1,17},{2,18},{3,19},{4,20},{5,21},{6,22},{7,23},{8,24},{9,... | collective-permute-start | bytes 393224 | tf_op jit(solution)/shard_map/ppermute | solution.py:248
  30.8 12.5 %collective-permute-start.21 = (bf16[32,16,128]{2,1,0:T(8,128)(2,1)S(1)}, bf16[32,16,128]{2,1,0:T(8,128)(2,1)S(1)}, u32[]{:S(2)}, u32[]{:S(2)}) collective-permute-start(bf16[32,16,128]{2,1,0:T(8,128)(2,1)S(1)} %collective-permute-done.17.refs_11_), channel_id=1, source_target_pairs={{0,8},{1,9},{2,10},{3,11},{4,12},{5,13},{6,14},{7,15},{8,0},{9,1},... | collective-permute-start | bytes 393224 | tf_op jit(solution)/shard_map/ppermute | solution.py:248
  33.5 9.8 %collective-permute-start.11 = (bf16[32,16,128]{2,1,0:T(8,128)(2,1)S(1)}, bf16[32,16,128]{2,1,0:T(8,128)(2,1)S(1)}, u32[]{:S(2)}, u32[]{:S(2)}) collective-permute-start(bf16[32,16,128]{2,1,0:T(8,128)(2,1)S(1)} %collective-permute-done.7.refs_0_), channel_id=1, source_target_pairs={{0,2},{1,3},{2,0},{3,1},{4,6},{5,7},{6,4},{7,5},{8,10},{9,11},{10,... | collective-permute-start | bytes 393224 | tf_op jit(solution)/shard_map/ppermute | solution.py:248
  39.0 4.3 %collective-permute-start.12 = (bf16[32,16,128]{2,1,0:T(8,128)(2,1)S(1)}, bf16[32,16,128]{2,1,0:T(8,128)(2,1)S(1)}, u32[]{:S(2)}, u32[]{:S(2)}) collective-permute-start(bf16[32,16,128]{2,1,0:T(8,128)(2,1)S(1)} %collective-permute-done.8.refs_1_), channel_id=1, source_target_pairs={{0,2},{1,3},{2,0},{3,1},{4,6},{5,7},{6,4},{7,5},{8,10},{9,11},{10,... | collective-permute-start | bytes 393224 | tf_op jit(solution)/shard_map/ppermute | solution.py:248
  40.8 2.5 %collective-permute-start.13 = (bf16[32,16,128]{2,1,0:T(8,128)(2,1)S(1)}, bf16[32,16,128]{2,1,0:T(8,128)(2,1)S(1)}, u32[]{:S(2)}, u32[]{:S(2)}) collective-permute-start(bf16[32,16,128]{2,1,0:T(8,128)(2,1)S(1)} %collective-permute-done.9.refs_2_), channel_id=1, source_target_pairs={{0,2},{1,3},{2,0},{3,1},{4,6},{5,7},{6,4},{7,5},{8,10},{9,11},{10,... | collective-permute-start | bytes 393224 | tf_op jit(solution)/shard_map/ppermute | solution.py:248
  42.2 1.3 %collective-permute-start.14 = (bf16[32,16,128]{2,1,0:T(8,128)(2,1)S(1)}, bf16[32,16,128]{2,1,0:T(8,128)(2,1)S(1)}, u32[]{:S(2)}, u32[]{:S(2)}) collective-permute-start(bf16[32,16,128]{2,1,0:T(8,128)(2,1)S(1)} %collective-permute-done.10.refs_3_), channel_id=1, source_target_pairs={{0,2},{1,3},{2,0},{3,1},{4,6},{5,7},{6,4},{7,5},{8,10},{9,11},{10,... | collective-permute-start | bytes 393224 | tf_op jit(solution)/shard_map/ppermute | solution.py:248

commit v4 on v3

--- a/solution.py
+++ b/solution.py
@@ -58,6 +58,7 @@
 
 ROW_BITS = 4
 GROUPS = 4
+BLOCKS = 4
 VMEM_LIMIT = 16 * 2**20
 HBM = pl.BlockSpec(memory_space=pltpu.MemorySpace.HBM)
 VMEM = pl.BlockSpec(memory_space=pltpu.MemorySpace.VMEM)
@@ -83,37 +84,37 @@
     return [copy.wait for copy in copies]
 
 
-def turn(w_ref, w_turned):
-    hidden = w_ref.shape[1] // 2
+def turn(w_ref, first, w_turned):
+    hidden = w_turned.shape[0] // 2
     for part, scale in enumerate((0.5, 1.0)):
-        columns = w_ref[:, part * hidden : (part + 1) * hidden].astype(F32)
+        columns = w_ref[:, first + part * hidden : first + (part + 1) * hidden].astype(F32)
         w_turned[part * hidden : (part + 1) * hidden, :] = (scale * columns).T.astype(BF16)
 
 
-def project(normed, w_turned, mask_ref, side_scr, first):
+def project(normed, w_turned, first, mask_ref, side_scr, row):
     rows, cols = mask_ref.shape
-    hidden = w_turned.shape[0] // 2
-    projected = lax.dot_general(w_turned[...], normed, NT, preferred_element_type=F32)
+    hidden, count = w_turned.shape[0] // 2, side_scr.shape[0] // rows
+    weights = [w_turned[pl.ds(pl.multiple_of(start + first, count), count), :] for start in (0, hidden)]
+    projected = lax.dot_general(jnp.concatenate(weights, axis=0), normed, NT, preferred_element_type=F32)
     for at in range(normed.shape[0] // cols):
-        row = first + at
         here = projected[:, at * cols : (at + 1) * cols]
-        half_masked = 0.5 * mask_ref[row : row + 1, :].astype(F32)
-        side_scr[pl.ds(row, hidden, stride=rows), :] = gated(here[:hidden], half_masked * here[hidden:])
-
-
-def cut(side_scr, outs):
-    _, _, wide, _, col = own_bits()
+        half_masked = 0.5 * mask_ref[row + at : row + at + 1, :].astype(F32)
+        side_scr[pl.ds(row + at, count, stride=rows), :] = gated(here[:count], half_masked * here[count:])
+
+
+def cut(side_scr, own, outs):
     share, rows, cols = outs[0].shape
     for offset, out_ref in enumerate(outs):
-        start = pl.multiple_of(((2 * wide + col) ^ offset) * (share * rows), share * rows)
+        start = pl.multiple_of((own ^ offset) * (share * rows), share * rows)
         out_ref[...] = side_scr[pl.ds(start, share * rows), :].astype(BF16).reshape(share, rows, cols)
 
 
 def right_kernel(map_hbm, mask_hbm, gain_hbm, bias_hbm, w_hbm, *refs):
-    outs, normed_ref = refs[:GROUPS], refs[GROUPS]
-    map_scr, mask_scr, gain_scr, bias_scr, w_scr, w_turned, side_scr, sems = refs[GROUPS + 1 :]
+    outs, normed_ref = refs[: GROUPS // 2], refs[GROUPS // 2]
+    map_scr, mask_scr, gain_scr, bias_scr, w_scr, w_turned, side_scr, sems = refs[GROUPS // 2 + 1 :]
     rows, cols, channels = map_scr.shape
     width = w_scr.shape[1]
+    _, _, wide, _, col = own_bits()
     wait_map, wait_w, wait_gain, wait_bias, wait_mask = start_copies(
         [
             (map_hbm, map_scr),
@@ -125,27 +126,34 @@
         sems,
     )
     wait_w()
-    turn(w_scr, w_turned)
+    turn(w_scr, 0, w_turned)
     wait_gain()
     wait_bias()
     wait_mask()
     wait_map()
-    values = map_scr[...].reshape(rows * cols, channels)
-    normed = layer_norm(values, gain_scr[...], bias_scr[...]).astype(BF16)
-    normed_ref[...] = normed
-    project(normed, w_turned, mask_scr, side_scr, 0)
-    cut(side_scr, outs)
+    block = rows // BLOCKS
+    for row in range(0, rows, block):
+        values = map_scr[row : row + block].reshape(block * cols, channels)
+        normed = layer_norm(values, gain_scr[...], bias_scr[...]).astype(BF16)
+        normed_ref[row * cols : (row + block) * cols, :] = normed
+        project(normed, w_turned, wide * (width // 4), mask_scr, side_scr, row)
+    cut(side_scr, col, outs)
 
 
 def left_kernel(normed_ref, mask_ref, w_ref, *refs):
-    outs, (w_turned, side_scr) = refs[:GROUPS], refs[GROUPS:]
+    rights, lefts = refs[: GROUPS // 2], refs[GROUPS // 2 : GROUPS // 2 + GROUPS]
+    w_turned, right_scr, left_scr = refs[GROUPS // 2 + GROUPS :]
     rows, cols = mask_ref.shape
-    turn(w_ref.at[:, : w_ref.shape[1] // 2], w_turned)
-    block = rows // 4
-    for step in range(4):
-        normed = normed_ref[step * block * cols : (step + 1) * block * cols, :]
-        project(normed, w_turned, mask_ref, side_scr, step * block)
-    cut(side_scr, outs)
+    width = w_ref.shape[1] // 2
+    _, _, wide, _, col = own_bits()
+    block = rows // BLOCKS
+    sides = ((0, left_scr, 0, 2 * wide + col, lefts), (width, right_scr, (wide ^ 1) * (width // 4), col, rights))
+    for start, side_scr, first, own, outs in sides:
+        turn(w_ref, start, w_turned)
+        for row in range(0, rows, block):
+            normed = normed_ref[row * cols : (row + block) * cols, :]
+            project(normed, w_turned, first, mask_ref, side_scr, row)
+        cut(side_scr, own, outs)
 
 
 def lay_out(pieces, out_ref):
@@ -252,12 +260,11 @@
     piece = jax.ShapeDtypeStruct((share, rows, cols), BF16)
     laid_out = jax.ShapeDtypeStruct((2, share, 4 * rows, cols), BF16)
     turned_shape = pltpu.VMEM((2 * hidden, channels), BF16)
-    side_shape = pltpu.VMEM((hidden * rows, cols), F32)
     *rights, normed = pl.pallas_call(
         right_kernel,
         in_specs=[HBM] * 5,
-        out_specs=[VMEM] * (GROUPS + 1),
-        out_shape=[piece] * GROUPS + [jax.ShapeDtypeStruct((rows * cols, channels), BF16)],
+        out_specs=[VMEM] * (GROUPS // 2 + 1),
+        out_shape=[piece] * (GROUPS // 2) + [jax.ShapeDtypeStruct((rows * cols, channels), BF16)],
         scratch_shapes=[
             pltpu.VMEM((rows, cols, channels), F32),
             pltpu.VMEM((rows, cols), pair_mask.dtype),
@@ -265,21 +272,26 @@
             pltpu.VMEM((1, channels), F32),
             pltpu.VMEM((channels, 2 * hidden), BF16),
             turned_shape,
-            side_shape,
+            pltpu.VMEM((hidden // 2 * rows, cols), F32),
             pltpu.SemaphoreType.DMA((5,)),
         ],
         compiler_params=params,
         name="right",
     )(*[in_hbm(x) for x in inputs])
-    lefts = pl.pallas_call(
+    pieces = pl.pallas_call(
         left_kernel,
         in_specs=[VMEM] * 3,
-        out_specs=[VMEM] * GROUPS,
-        out_shape=[piece] * GROUPS,
-        scratch_shapes=[turned_shape, side_shape],
+        out_specs=[VMEM] * (GROUPS // 2 + GROUPS),
+        out_shape=[piece] * (GROUPS // 2 + GROUPS),
+        scratch_shapes=[
+            turned_shape,
+            pltpu.VMEM((hidden // 2 * rows, cols), F32),
+            pltpu.VMEM((hidden * rows, cols), F32),
+        ],
         compiler_params=params,
         name="left",
     )(normed, pair_mask, w_proj)
+    rights, lefts = [*rights, *pieces[: GROUPS // 2]], pieces[GROUPS // 2 :]
     lefts = [swap(x, plane[n]) for n, x in enumerate(lefts)]
     lefts += [swap(x, parity) for x in lefts]
     rights = [swap(x, plane[n]) for n, x in enumerate(rights)]

time: 59.9 us -> 59.2 us (0.988)
  waiting for transfers between devices: 16.9 us -> 16.3 us
    ppermute x22, waiting for transfers between devices: 16.9 us -> 16.3 us  [swap(): lax.ppermute(array, ('row', 'col'), [(n, n ^ offset) for n in devices])]
  transfers between devices with their start and end apart: 22 -> 22, of which waited for: 11 -> 10; matrix products, arithmetic and copies ran while one was open for 0% -> 0% of each run, Pallas kernels for 3% -> 2%
where the time goes in v4:
time: 59.2 us; the launch traced here: 59 us
  starting transfers between devices  22.7 us (38%)
  waiting for transfers between devices  16.3 us (28%)
  blocking collectives  12.9 us (22%)
  Pallas kernels  7.04 us (12%)
    ppermute x22, starting transfers between devices, swap(): lax.ppermute(array, ('row', 'col'), [(n, n ^ offset) for n in devices])  22.7 us
    ppermute x22, waiting for transfers between devices, swap(): lax.ppermute(array, ('row', 'col'), [(n, n ^ offset) for n in devices])  16.3 us
    all_to_all x1, blocking collectives, exchanged(): lax.all_to_all(summed, ('row', 'col'), 0, 0, tiled=True, axis_index_group...  12.9 us
    pallas_call x1, Pallas kernels, exchanged(): pl.pallas_call(right_kernel, in_specs=[HBM] * 5, out_specs=[VMEM] * (GROU...  2.31 us
    pallas_call x1, Pallas kernels, exchanged(): pl.pallas_call(output_kernel, in_specs=[VMEM] * 5, out_specs=HBM, out_sha...  1.66 us
  transfers between devices with their start and end apart: 22, of which 10 were waited for; matrix products, arithmetic and copies ran while one was open for 0% of the time, Pallas kernels for 2%

profile of v4, /device:TPU:0, one launch (start us, length us, event | category | flops | bytes accessed | tf_op | source)
XLA Modules:
  0.0 59.0 jit_solution(12551134310459289367)
XLA Ops:
  0.0 2.3 %right.1 = (bf16[32,16,128]{2,1,0:T(8,128)(2,1)S(1)}, bf16[32,16,128]{2,1,0:T(8,128)(2,1)S(1)}, bf16[2048,128]{1,0:T(8,128)(2,1)S(1)}) custom-call(f32[16,128,128]{2,1,0:T(8,128)} %map_hbm.1, s32[16,128]{1,0:T(8,128)} %mask_ref.1, f32[1,128]{1,0:T(1,128)} %bitcast.4, f32[1,128]{1,0:T(1,128)} %bitcast.5, bf16[128,512]{1,0:T(8,128)(2,1)} %w_ref.1), custom_call_target="tpu_custom_call" | custom-call | tf_op jit(solution)/shard_map/right/pallas_call | solution.py:263
  2.3 0.0 copy-start.1
  2.4 1.0 %left.1 = (bf16[32,16,128]{2,1,0:T(8,128)(2,1)S(1)}, bf16[32,16,128]{2,1,0:T(8,128)(2,1)S(1)}, bf16[32,16,128]{2,1,0:T(8,128)(2,1)S(1)}, bf16[32,16,128]{2,1,0:T...) custom-call(bf16[2048,128]{1,0:T(8,128)(2,1)S(1)} %get-tuple-element.19.normed_ref, ...), custom_call_target="tpu_custom_call" | custom-call | tf_op jit(solution)/shard_map/left/pallas_call | solution.py:281
  3.3 3.0 %collective-permute-start.1 = (bf16[32,16,128]{2,1,0:T(8,128)(2,1)S(1)}, bf16[32,16,128]{2,1,0:T(8,128)(2,1)S(1)}, u32[]{:S(2)}, u32[]{:S(2)}) collective-permute-start(bf16[32,16,128]{2,1,0:T(8,128)(2,1)S(1)} %get-tuple-element.22), channel_id=1, source_target_pairs={{0,4},{1,5},{2,6},{3,7},{4,0},{5,1},{6,2},{7,3},{8,12},{9,13},{10,... | collective-permute-start | bytes 393224 | tf_op jit(solution)/shard_map/ppermute | solution.py:256
  6.4 1.5 %collective-permute-start.2 = (bf16[32,16,128]{2,1,0:T(8,128)(2,1)S(1)}, bf16[32,16,128]{2,1,0:T(8,128)(2,1)S(1)}, u32[]{:S(2)}, u32[]{:S(2)}) collective-permute-start(bf16[32,16,128]{2,1,0:T(8,128)(2,1)S(1)} %get-tuple-element.23), channel_id=1, source_target_pairs={{0,5},{1,4},{2,7},{3,6},{4,1},{5,0},{6,3},{7,2},{8,13},{9,12},{10,... | collective-permute-start | bytes 393224 | tf_op jit(solution)/shard_map/ppermute | solution.py:256
  7.9 0.0 collective-permute-start
  7.9 0.0 collective-permute-start.3
  7.9 2.0 %collective-permute-start.15 = (bf16[32,16,128]{2,1,0:T(8,128)(2,1)S(1)}, bf16[32,16,128]{2,1,0:T(8,128)(2,1)S(1)}, u32[]{:S(2)}, u32[]{:S(2)}) collective-permute-start(bf16[32,16,128]{2,1,0:T(8,128)(2,1)S(1)} %get-tuple-element.26), channel_id=1, source_target_pairs={{0,1},{1,0},{2,3},{3,2},{4,5},{5,4},{6,7},{7,6},{8,9},{9,8},{10,11... | collective-permute-start | bytes 393224 | tf_op jit(solution)/shard_map/ppermute | solution.py:256
  9.9 0.4 collective-permute-done.1.refs_2_
  10.3 2.5 %collective-permute-start.16 = (bf16[32,16,128]{2,1,0:T(8,128)(2,1)S(1)}, bf16[32,16,128]{2,1,0:T(8,128)(2,1)S(1)}, u32[]{:S(2)}, u32[]{:S(2)}) collective-permute-start(bf16[32,16,128]{2,1,0:T(8,128)(2,1)S(1)} %get-tuple-element.27), channel_id=1, source_target_pairs={{0,4},{1,5},{2,6},{3,7},{4,0},{5,1},{6,2},{7,3},{8,12},{9,13},{10,... | collective-permute-start | bytes 393224 | tf_op jit(solution)/shard_map/ppermute | solution.py:256
  12.7 2.3 %collective-permute-done.2.refs_3_ = bf16[32,16,128]{2,1,0:T(8,128)(2,1)S(1)} collective-permute-done((bf16[32,16,128]{2,1,0:T(8,128)(2,1)S(1)}, bf16[32,16,128]{2,1,0:T(8,128)(2,1)S(1)}, u32[]{:S(2)}, u32[]{:S(2)}) %collective-permute-start.2) | collective-permute-done | bytes 131104 | tf_op jit(solution)/shard_map/ppermute | solution.py:256
  15.0 0.6 %collective-permute-start.17 = (bf16[32,16,128]{2,1,0:T(8,128)(2,1)S(1)}, bf16[32,16,128]{2,1,0:T(8,128)(2,1)S(1)}, u32[]{:S(2)}, u32[]{:S(2)}) collective-permute-start(bf16[32,16,128]{2,1,0:T(8,128)(2,1)S(1)} %get-tuple-element.28), channel_id=1, source_target_pairs={{0,5},{1,4},{2,7},{3,6},{4,1},{5,0},{6,3},{7,2},{8,13},{9,12},{10,... | collective-permute-start | bytes 393224 | tf_op jit(solution)/shard_map/ppermute | solution.py:256
  15.6 0.7 %collective-permute-done.refs_1_ = bf16[32,16,128]{2,1,0:T(8,128)(2,1)S(1)} collective-permute-done((bf16[32,16,128]{2,1,0:T(8,128)(2,1)S(1)}, bf16[32,16,128]{2,1,0:T(8,128)(2,1)S(1)}, u32[]{:S(2)}, u32[]{:S(2)}) %collective-permute-start) | collective-permute-done | bytes 131104 | tf_op jit(solution)/shard_map/ppermute | solution.py:256
  16.3 1.6 %collective-permute-start.18 = (bf16[32,16,128]{2,1,0:T(8,128)(2,1)S(1)}, bf16[32,16,128]{2,1,0:T(8,128)(2,1)S(1)}, u32[]{:S(2)}, u32[]{:S(2)}) collective-permute-start(bf16[32,16,128]{2,1,0:T(8,128)(2,1)S(1)} %get-tuple-element.25.refs_8_), channel_id=1, source_target_pairs={{0,8},{1,9},{2,10},{3,11},{4,12},{5,13},{6,14},{7,15},{8,0},{9,1},... | collective-permute-start | bytes 393224 | tf_op jit(solution)/shard_map/ppermute | solution.py:256
  17.9 0.0 collective-permute-done.3.refs_4_
  17.9 2.6 %collective-permute-start.7 = (bf16[32,16,128]{2,1,0:T(8,128)(2,1)S(1)}, bf16[32,16,128]{2,1,0:T(8,128)(2,1)S(1)}, u32[]{:S(2)}, u32[]{:S(2)}) collective-permute-start(bf16[32,16,128]{2,1,0:T(8,128)(2,1)S(1)} %get-tuple-element.20.refs_0_), channel_id=1, source_target_pairs={{0,16},{1,17},{2,18},{3,19},{4,20},{5,21},{6,22},{7,23},{8,24},{9,... | collective-permute-start | bytes 393224 | tf_op jit(solution)/shard_map/ppermute | solution.py:256
  20.5 0.0 collective-permute-done.15.refs_9_
  20.5 0.0 collective-permute-start.5
  20.5 0.0 collective-permute-done.16.refs_10_
  20.5 0.5 collective-permute-start.6
  21.0 0.0 collective-permute-done.17.refs_11_
  21.0 0.1 collective-permute-start.4
  21.1 0.5 collective-permute-done.18.refs_12_
  21.6 2.8 %collective-permute-start.9 = (bf16[32,16,128]{2,1,0:T(8,128)(2,1)S(1)}, bf16[32,16,128]{2,1,0:T(8,128)(2,1)S(1)}, u32[]{:S(2)}, u32[]{:S(2)}) collective-permute-start(bf16[32,16,128]{2,1,0:T(8,128)(2,1)S(1)} %collective-permute-done.1.refs_2_), channel_id=1, source_target_pairs={{0,16},{1,17},{2,18},{3,19},{4,20},{5,21},{6,22},{7,23},{8,24},{9,... | collective-permute-start | bytes 393224 | tf_op jit(solution)/shard_map/ppermute | solution.py:256
  24.4 0.9 %collective-permute-done.7.refs_0_ = bf16[32,16,128]{2,1,0:T(8,128)(2,1)S(1)} collective-permute-done((bf16[32,16,128]{2,1,0:T(8,128)(2,1)S(1)}, bf16[32,16,128]{2,1,0:T(8,128)(2,1)S(1)}, u32[]{:S(2)}, u32[]{:S(2)}) %collective-permute-start.7) | collective-permute-done | bytes 131104 | tf_op jit(solution)/shard_map/ppermute | solution.py:256
  25.3 1.1 %collective-permute-start.10 = (bf16[32,16,128]{2,1,0:T(8,128)(2,1)S(1)}, bf16[32,16,128]{2,1,0:T(8,128)(2,1)S(1)}, u32[]{:S(2)}, u32[]{:S(2)}) collective-permute-start(bf16[32,16,128]{2,1,0:T(8,128)(2,1)S(1)} %collective-permute-done.2.refs_3_), channel_id=1, source_target_pairs={{0,16},{1,17},{2,18},{3,19},{4,20},{5,21},{6,22},{7,23},{8,24},{9,... | collective-permute-start | bytes 393224 | tf_op jit(solution)/shard_map/ppermute | solution.py:256
  26.4 0.0 collective-permute-done.5.refs_6_
  26.4 1.8 %collective-permute-start.19 = (bf16[32,16,128]{2,1,0:T(8,128)(2,1)S(1)}, bf16[32,16,128]{2,1,0:T(8,128)(2,1)S(1)}, u32[]{:S(2)}, u32[]{:S(2)}) collective-permute-start(bf16[32,16,128]{2,1,0:T(8,128)(2,1)S(1)} %collective-permute-done.15.refs_9_), channel_id=1, source_target_pairs={{0,8},{1,9},{2,10},{3,11},{4,12},{5,13},{6,14},{7,15},{8,0},{9,1},... | collective-permute-start | bytes 393224 | tf_op jit(solution)/shard_map/ppermute | solution.py:256
  28.2 0.0 collective-permute-done.6.refs_7_
  28.2 0.2 collective-permute-start.20
  28.5 1.8 %collective-permute-start.8 = (bf16[32,16,128]{2,1,0:T(8,128)(2,1)S(1)}, bf16[32,16,128]{2,1,0:T(8,128)(2,1)S(1)}, u32[]{:S(2)}, u32[]{:S(2)}) collective-permute-start(bf16[32,16,128]{2,1,0:T(8,128)(2,1)S(1)} %collective-permute-done.refs_1_), channel_id=1, source_target_pairs={{0,16},{1,17},{2,18},{3,19},{4,20},{5,21},{6,22},{7,23},{8,24},{9,... | collective-permute-start | bytes 393224 | tf_op jit(solution)/shard_map/ppermute | solution.py:256
  30.3 4.2 %collective-permute-done.9.refs_2_ = bf16[32,16,128]{2,1,0:T(8,128)(2,1)S(1)} collective-permute-done((bf16[32,16,128]{2,1,0:T(8,128)(2,1)S(1)}, bf16[32,16,128]{2,1,0:T(8,128)(2,1)S(1)}, u32[]{:S(2)}, u32[]{:S(2)}) %collective-permute-start.9) | collective-permute-done | bytes 131104 | tf_op jit(solution)/shard_map/ppermute | solution.py:256
  34.4 0.0 collective-permute-start.21
  34.4 3.9 %collective-permute-done.10.refs_3_ = bf16[32,16,128]{2,1,0:T(8,128)(2,1)S(1)} collective-permute-done((bf16[32,16,128]{2,1,0:T(8,128)(2,1)S(1)}, bf16[32,16,128]{2,1,0:T(8,128)(2,1)S(1)}, u32[]{:S(2)}, u32[]{:S(2)}) %collective-permute-start.10) | collective-permute-done | bytes 131104 | tf_op jit(solution)/shard_map/ppermute | solution.py:256
  38.4 0.0 collective-permute-done.19.refs_13_
  38.4 0.5 collective-permute-start.13
  38.9 0.7 %collective-permute-done.20.refs_14_ = bf16[32,16,128]{2,1,0:T(8,128)(2,1)S(1)} collective-permute-done((bf16[32,16,128]{2,1,0:T(8,128)(2,1)S(1)}, bf16[32,16,128]{2,1,0:T(8,128)(2,1)S(1)}, u32[]{:S(2)}, u32[]{:S(2)}) %collective-permute-start.20) | collective-permute-done | bytes 131104 | tf_op jit(solution)/shard_map/ppermute | solution.py:256
  39.5 0.0 collective-permute-start.14
  39.5 2.5 %collective-permute-done.8.refs_1_ = bf16[32,16,128]{2,1,0:T(8,128)(2,1)S(1)} collective-permute-done((bf16[32,16,128]{2,1,0:T(8,128)(2,1)S(1)}, bf16[32,16,128]{2,1,0:T(8,128)(2,1)S(1)}, u32[]{:S(2)}, u32[]{:S(2)}) %collective-permute-start.8) | collective-permute-done | bytes 131104 | tf_op jit(solution)/shard_map/ppermute | solution.py:256
  42.0 0.0 collective-permute-start.12
  42.0 1.0 %gates.1 = (f32[16,128,128]{2,1,0:T(8,128)S(1)}, f32[1,128]{1,0:T(1,128)S(1)}, f32[1,128]{1,0:T(1,128)S(1)}, bf16[128,128]{1,0:T(8,128)(2,1)S(1)}, bf16[2,32,64,128]{3,2,1,0:T(8,128)(2,1)S(1)}) custom-call(bf16[2048,128]{1,0:T(8,128)(2,1)S(1)} %get-tuple-element.19.normed_ref, bf16[128,128]{1,0:T(8,128)(2,1)S(1)} %copy-done.1, ...), custom_call_target="tpu_custom_call" | custom-call | tf_op jit(solution)/shard_map/gates/pallas_call | solution.py:300
  43.1 0.0 collective-permute-done.21.refs_15_
  43.1 0.0 collective-permute-done.13.refs_6_
  43.1 0.0 collective-permute-done.14.refs_7_
  43.1 0.3 collective-permute-done.12.refs_5_
  43.4 1.1 %pairs.1 = bf16[8,16,16,128]{3,2,1,0:T(8,128)(2,1)S(1)} custom-call(bf16[2,32,64,128]{3,2,1,0:T(8,128)(2,1)S(1)} %get-tuple-element.24.near_ref, bf16[32,16,128]{2,1,0:T(8,128)(2,1)S(1)} %collective-permute-done.7.refs_0_, bf16[32,16,128]{2,1,0:T(8,128)(2,1)S(1)} %collective-permute-done.8.refs_1_, bf16[32,16,128]{2,1,0:T(8,128)(2,1)S(1)} %collective-permute-done.9.refs_2_, ...), custom_call_target="tpu_custom_call" | custom-call | tf_op jit(solution)/shard_map/pairs/pallas_call | solution.py:323
  44.4 12.9 %all_to_all.5.summed_ref = bf16[8,16,16,128]{3,2,1,0:T(8,128)(2,1)S(1)} all-to-all(bf16[8,16,16,128]{3,2,1,0:T(8,128)(2,1)S(1)} %pairs.1), channel_id=1, replica_groups={{0,1,4,5,8,9,12,13},{2,3,6,7,10,11,14,15},{16,17,20,21,24,25,28,29},{18..., dimensions={0} | all-to-all | bytes 1048576 | tf_op jit(solution)/shard_map/all_to_all | solution.py:336
  57.3 1.7 %output.1 = f32[16,128,128]{2,1,0:T(8,128)} custom-call(bf16[8,16,16,128]{3,2,1,0:T(8,128)(2,1)S(1)} %all_to_all.5.summed_ref, f32[16,128,128]{2,1,0:T(8,128)S(1)} %get-tuple-element.29.gating_ref, f32[1,128]{1,0:T(1,128)S(1)} %get-tuple-element.30.gain_ref, f32[1,128]{1,0:T(1,128)S(1)} %get-tuple-element.31.bias_ref, ...), custom_call_target="tpu_custom_call" | custom-call | tf_op jit(solution)/shard_map/output/pallas_call | solution.py:337
  (8 shorter events, 0.0 us)
Async XLA Ops:
  0.0 2.3 %copy-start = (bf16[128,512]{1,0:T(8,128)(2,1)S(1)}, bf16[128,512]{1,0:T(8,128)(2,1)}, u32[]{:S(2)}) copy-start(bf16[128,512]{1,0:T(8,128)(2,1)} %w_ref.1) | copy-start | bytes 393220
  0.0 2.3 %copy-start.2 = (s32[16,128]{1,0:T(8,128)S(1)}, s32[16,128]{1,0:T(8,128)}, u32[]{:S(2)}) copy-start(s32[16,128]{1,0:T(8,128)} %mask_ref.1) | copy-start | bytes 24580
  2.3 39.7 %copy-start.1 = (bf16[128,128]{1,0:T(8,128)(2,1)S(1)}, bf16[128,128]{1,0:T(8,128)(2,1)}, u32[]{:S(2)}) copy-start(bf16[128,128]{1,0:T(8,128)(2,1)} %w_gate_ref.1) | copy-start | bytes 98308
  3.3 6.9 %collective-permute-start.1 = (bf16[32,16,128]{2,1,0:T(8,128)(2,1)S(1)}, bf16[32,16,128]{2,1,0:T(8,128)(2,1)S(1)}, u32[]{:S(2)}, u32[]{:S(2)}) collective-permute-start(bf16[32,16,128]{2,1,0:T(8,128)(2,1)S(1)} %get-tuple-element.22), channel_id=1, source_target_pairs={{0,4},{1,5},{2,6},{3,7},{4,0},{5,1},{6,2},{7,3},{8,12},{9,13},{10,... | collective-permute-start | bytes 393224 | tf_op jit(solution)/shard_map/ppermute | solution.py:256
  6.4 8.6 %collective-permute-start.2 = (bf16[32,16,128]{2,1,0:T(8,128)(2,1)S(1)}, bf16[32,16,128]{2,1,0:T(8,128)(2,1)S(1)}, u32[]{:S(2)}, u32[]{:S(2)}) collective-permute-start(bf16[32,16,128]{2,1,0:T(8,128)(2,1)S(1)} %get-tuple-element.23), channel_id=1, source_target_pairs={{0,5},{1,4},{2,7},{3,6},{4,1},{5,0},{6,3},{7,2},{8,13},{9,12},{10,... | collective-permute-start | bytes 393224 | tf_op jit(solution)/shard_map/ppermute | solution.py:256
  7.9 8.4 %collective-permute-start = (bf16[32,16,128]{2,1,0:T(8,128)(2,1)S(1)}, bf16[32,16,128]{2,1,0:T(8,128)(2,1)S(1)}, u32[]{:S(2)}, u32[]{:S(2)}) collective-permute-start(bf16[32,16,128]{2,1,0:T(8,128)(2,1)S(1)} %get-tuple-element.21), channel_id=1, source_target_pairs={{0,1},{1,0},{2,3},{3,2},{4,5},{5,4},{6,7},{7,6},{8,9},{9,8},{10,11... | collective-permute-start | bytes 393224 | tf_op jit(solution)/shard_map/ppermute | solution.py:256
  7.9 10.0 %collective-permute-start.3 = (bf16[32,16,128]{2,1,0:T(8,128)(2,1)S(1)}, bf16[32,16,128]{2,1,0:T(8,128)(2,1)S(1)}, u32[]{:S(2)}, u32[]{:S(2)}) collective-permute-start(bf16[32,16,128]{2,1,0:T(8,128)(2,1)S(1)} %get-tuple-element.20.refs_0_), channel_id=1, source_target_pairs={{0,2},{1,3},{2,0},{3,1},{4,6},{5,7},{6,4},{7,5},{8,10},{9,11},{10,... | collective-permute-start | bytes 393224 | tf_op jit(solution)/shard_map/ppermute | solution.py:256
  7.9 12.6 %collective-permute-start.15 = (bf16[32,16,128]{2,1,0:T(8,128)(2,1)S(1)}, bf16[32,16,128]{2,1,0:T(8,128)(2,1)S(1)}, u32[]{:S(2)}, u32[]{:S(2)}) collective-permute-start(bf16[32,16,128]{2,1,0:T(8,128)(2,1)S(1)} %get-tuple-element.26), channel_id=1, source_target_pairs={{0,1},{1,0},{2,3},{3,2},{4,5},{5,4},{6,7},{7,6},{8,9},{9,8},{10,11... | collective-permute-start | bytes 393224 | tf_op jit(solution)/shard_map/ppermute | solution.py:256
  10.3 10.2 %collective-permute-start.16 = (bf16[32,16,128]{2,1,0:T(8,128)(2,1)S(1)}, bf16[32,16,128]{2,1,0:T(8,128)(2,1)S(1)}, u32[]{:S(2)}, u32[]{:S(2)}) collective-permute-start(bf16[32,16,128]{2,1,0:T(8,128)(2,1)S(1)} %get-tuple-element.27), channel_id=1, source_target_pairs={{0,4},{1,5},{2,6},{3,7},{4,0},{5,1},{6,2},{7,3},{8,12},{9,13},{10,... | collective-permute-start | bytes 393224 | tf_op jit(solution)/shard_map/ppermute | solution.py:256
  15.0 6.0 %collective-permute-start.17 = (bf16[32,16,128]{2,1,0:T(8,128)(2,1)S(1)}, bf16[32,16,128]{2,1,0:T(8,128)(2,1)S(1)}, u32[]{:S(2)}, u32[]{:S(2)}) collective-permute-start(bf16[32,16,128]{2,1,0:T(8,128)(2,1)S(1)} %get-tuple-element.28), channel_id=1, source_target_pairs={{0,5},{1,4},{2,7},{3,6},{4,1},{5,0},{6,3},{7,2},{8,13},{9,12},{10,... | collective-permute-start | bytes 393224 | tf_op jit(solution)/shard_map/ppermute | solution.py:256
  16.3 5.3 %collective-permute-start.18 = (bf16[32,16,128]{2,1,0:T(8,128)(2,1)S(1)}, bf16[32,16,128]{2,1,0:T(8,128)(2,1)S(1)}, u32[]{:S(2)}, u32[]{:S(2)}) collective-permute-start(bf16[32,16,128]{2,1,0:T(8,128)(2,1)S(1)} %get-tuple-element.25.refs_8_), channel_id=1, source_target_pairs={{0,8},{1,9},{2,10},{3,11},{4,12},{5,13},{6,14},{7,15},{8,0},{9,1},... | collective-permute-start | bytes 393224 | tf_op jit(solution)/shard_map/ppermute | solution.py:256
  17.9 7.4 %collective-permute-start.7 = (bf16[32,16,128]{2,1,0:T(8,128)(2,1)S(1)}, bf16[32,16,128]{2,1,0:T(8,128)(2,1)S(1)}, u32[]{:S(2)}, u32[]{:S(2)}) collective-permute-start(bf16[32,16,128]{2,1,0:T(8,128)(2,1)S(1)} %get-tuple-element.20.refs_0_), channel_id=1, source_target_pairs={{0,16},{1,17},{2,18},{3,19},{4,20},{5,21},{6,22},{7,23},{8,24},{9,... | collective-permute-start | bytes 393224 | tf_op jit(solution)/shard_map/ppermute | solution.py:256
  20.5 6.0 %collective-permute-start.5 = (bf16[32,16,128]{2,1,0:T(8,128)(2,1)S(1)}, bf16[32,16,128]{2,1,0:T(8,128)(2,1)S(1)}, u32[]{:S(2)}, u32[]{:S(2)}) collective-permute-start(bf16[32,16,128]{2,1,0:T(8,128)(2,1)S(1)} %collective-permute-done.1.refs_2_), channel_id=1, source_target_pairs={{0,2},{1,3},{2,0},{3,1},{4,6},{5,7},{6,4},{7,5},{8,10},{9,11},{10,... | collective-permute-start | bytes 393224 | tf_op jit(solution)/shard_map/ppermute | solution.py:256
  20.5 7.8 %collective-permute-start.6 = (bf16[32,16,128]{2,1,0:T(8,128)(2,1)S(1)}, bf16[32,16,128]{2,1,0:T(8,128)(2,1)S(1)}, u32[]{:S(2)}, u32[]{:S(2)}) collective-permute-start(bf16[32,16,128]{2,1,0:T(8,128)(2,1)S(1)} %collective-permute-done.2.refs_3_), channel_id=1, source_target_pairs={{0,2},{1,3},{2,0},{3,1},{4,6},{5,7},{6,4},{7,5},{8,10},{9,11},{10,... | collective-permute-start | bytes 393224 | tf_op jit(solution)/shard_map/ppermute | solution.py:256
  21.0 7.5 %collective-permute-start.4 = (bf16[32,16,128]{2,1,0:T(8,128)(2,1)S(1)}, bf16[32,16,128]{2,1,0:T(8,128)(2,1)S(1)}, u32[]{:S(2)}, u32[]{:S(2)}) collective-permute-start(bf16[32,16,128]{2,1,0:T(8,128)(2,1)S(1)} %collective-permute-done.refs_1_), channel_id=1, source_target_pairs={{0,2},{1,3},{2,0},{3,1},{4,6},{5,7},{6,4},{7,5},{8,10},{9,11},{10,... | collective-permute-start | bytes 393224 | tf_op jit(solution)/shard_map/ppermute | solution.py:256
  21.6 12.9 %collective-permute-start.9 = (bf16[32,16,128]{2,1,0:T(8,128)(2,1)S(1)}, bf16[32,16,128]{2,1,0:T(8,128)(2,1)S(1)}, u32[]{:S(2)}, u32[]{:S(2)}) collective-permute-start(bf16[32,16,128]{2,1,0:T(8,128)(2,1)S(1)} %collective-permute-done.1.refs_2_), channel_id=1, source_target_pairs={{0,16},{1,17},{2,18},{3,19},{4,20},{5,21},{6,22},{7,23},{8,24},{9,... | collective-permute-start | bytes 393224 | tf_op jit(solution)/shard_map/ppermute | solution.py:256
  25.3 13.1 %collective-permute-start.10 = (bf16[32,16,128]{2,1,0:T(8,128)(2,1)S(1)}, bf16[32,16,128]{2,1,0:T(8,128)(2,1)S(1)}, u32[]{:S(2)}, u32[]{:S(2)}) collective-permute-start(bf16[32,16,128]{2,1,0:T(8,128)(2,1)S(1)} %collective-permute-done.2.refs_3_), channel_id=1, source_target_pairs={{0,16},{1,17},{2,18},{3,19},{4,20},{5,21},{6,22},{7,23},{8,24},{9,... | collective-permute-start | bytes 393224 | tf_op jit(solution)/shard_map/ppermute | solution.py:256
  26.4 11.9 %collective-permute-start.19 = (bf16[32,16,128]{2,1,0:T(8,128)(2,1)S(1)}, bf16[32,16,128]{2,1,0:T(8,128)(2,1)S(1)}, u32[]{:S(2)}, u32[]{:S(2)}) collective-permute-start(bf16[32,16,128]{2,1,0:T(8,128)(2,1)S(1)} %collective-permute-done.15.refs_9_), channel_id=1, source_target_pairs={{0,8},{1,9},{2,10},{3,11},{4,12},{5,13},{6,14},{7,15},{8,0},{9,1},... | collective-permute-start | bytes 393224 | tf_op jit(solution)/shard_map/ppermute | solution.py:256
  28.2 11.3 %collective-permute-start.20 = (bf16[32,16,128]{2,1,0:T(8,128)(2,1)S(1)}, bf16[32,16,128]{2,1,0:T(8,128)(2,1)S(1)}, u32[]{:S(2)}, u32[]{:S(2)}) collective-permute-start(bf16[32,16,128]{2,1,0:T(8,128)(2,1)S(1)} %collective-permute-done.16.refs_10_), channel_id=1, source_target_pairs={{0,8},{1,9},{2,10},{3,11},{4,12},{5,13},{6,14},{7,15},{8,0},{9,1},... | collective-permute-start | bytes 393224 | tf_op jit(solution)/shard_map/ppermute | solution.py:256
  28.5 13.5 %collective-permute-start.8 = (bf16[32,16,128]{2,1,0:T(8,128)(2,1)S(1)}, bf16[32,16,128]{2,1,0:T(8,128)(2,1)S(1)}, u32[]{:S(2)}, u32[]{:S(2)}) collective-permute-start(bf16[32,16,128]{2,1,0:T(8,128)(2,1)S(1)} %collective-permute-done.refs_1_), channel_id=1, source_target_pairs={{0,16},{1,17},{2,18},{3,19},{4,20},{5,21},{6,22},{7,23},{8,24},{9,... | collective-permute-start | bytes 393224 | tf_op jit(solution)/shard_map/ppermute | solution.py:256
  34.4 8.6 %collective-permute-start.21 = (bf16[32,16,128]{2,1,0:T(8,128)(2,1)S(1)}, bf16[32,16,128]{2,1,0:T(8,128)(2,1)S(1)}, u32[]{:S(2)}, u32[]{:S(2)}) collective-permute-start(bf16[32,16,128]{2,1,0:T(8,128)(2,1)S(1)} %collective-permute-done.17.refs_11_), channel_id=1, source_target_pairs={{0,8},{1,9},{2,10},{3,11},{4,12},{5,13},{6,14},{7,15},{8,0},{9,1},... | collective-permute-start | bytes 393224 | tf_op jit(solution)/shard_map/ppermute | solution.py:256
  38.4 4.7 %collective-permute-start.11 = (bf16[32,16,128]{2,1,0:T(8,128)(2,1)S(1)}, bf16[32,16,128]{2,1,0:T(8,128)(2,1)S(1)}, u32[]{:S(2)}, u32[]{:S(2)}) collective-permute-start(bf16[32,16,128]{2,1,0:T(8,128)(2,1)S(1)} %collective-permute-done.7.refs_0_), channel_id=1, source_target_pairs={{0,2},{1,3},{2,0},{3,1},{4,6},{5,7},{6,4},{7,5},{8,10},{9,11},{10,... | collective-permute-start | bytes 393224 | tf_op jit(solution)/shard_map/ppermute | solution.py:256
  38.4 4.7 %collective-permute-start.13 = (bf16[32,16,128]{2,1,0:T(8,128)(2,1)S(1)}, bf16[32,16,128]{2,1,0:T(8,128)(2,1)S(1)}, u32[]{:S(2)}, u32[]{:S(2)}) collective-permute-start(bf16[32,16,128]{2,1,0:T(8,128)(2,1)S(1)} %collective-permute-done.9.refs_2_), channel_id=1, source_target_pairs={{0,2},{1,3},{2,0},{3,1},{4,6},{5,7},{6,4},{7,5},{8,10},{9,11},{10,... | collective-permute-start | bytes 393224 | tf_op jit(solution)/shard_map/ppermute | solution.py:256
  39.5 3.5 %collective-permute-start.14 = (bf16[32,16,128]{2,1,0:T(8,128)(2,1)S(1)}, bf16[32,16,128]{2,1,0:T(8,128)(2,1)S(1)}, u32[]{:S(2)}, u32[]{:S(2)}) collective-permute-start(bf16[32,16,128]{2,1,0:T(8,128)(2,1)S(1)} %collective-permute-done.10.refs_3_), channel_id=1, source_target_pairs={{0,2},{1,3},{2,0},{3,1},{4,6},{5,7},{6,4},{7,5},{8,10},{9,11},{10,... | collective-permute-start | bytes 393224 | tf_op jit(solution)/shard_map/ppermute | solution.py:256
  42.0 1.3 %collective-permute-start.12 = (bf16[32,16,128]{2,1,0:T(8,128)(2,1)S(1)}, bf16[32,16,128]{2,1,0:T(8,128)(2,1)S(1)}, u32[]{:S(2)}, u32[]{:S(2)}) collective-permute-start(bf16[32,16,128]{2,1,0:T(8,128)(2,1)S(1)} %collective-permute-done.8.refs_1_), channel_id=1, source_target_pairs={{0,2},{1,3},{2,0},{3,1},{4,6},{5,7},{6,4},{7,5},{8,10},{9,11},{10,... | collective-permute-start | bytes 393224 | tf_op jit(solution)/shard_map/ppermute | solution.py:256

commit v5 on v3

--- a/solution.py
+++ b/solution.py
@@ -130,10 +130,12 @@
     wait_bias()
     wait_mask()
     wait_map()
-    values = map_scr[...].reshape(rows * cols, channels)
-    normed = layer_norm(values, gain_scr[...], bias_scr[...]).astype(BF16)
-    normed_ref[...] = normed
-    project(normed, w_turned, mask_scr, side_scr, 0)
+    block = rows // 4
+    for step in range(4):
+        values = map_scr[step * block : (step + 1) * block].reshape(block * cols, channels)
+        normed = layer_norm(values, gain_scr[...], bias_scr[...]).astype(BF16)
+        normed_ref[step * block * cols : (step + 1) * block * cols, :] = normed
+        project(normed, w_turned, mask_scr, side_scr, step * block)
     cut(side_scr, outs)
 
 

time: 59.9 us -> 59.9 us (level)
  no operation moved by 1% of the time
where the time goes in v5:
time: 59.9 us; the launch traced here: 59.7 us
  starting transfers between devices  22.3 us (37%)
  waiting for transfers between devices  16.9 us (28%)
  blocking collectives  13.4 us (22%)
  Pallas kernels  7.01 us (12%)
    ppermute x22, starting transfers between devices, swap(): lax.ppermute(array, ('row', 'col'), [(n, n ^ offset) for n in devices])  22.3 us
    ppermute x22, waiting for transfers between devices, swap(): lax.ppermute(array, ('row', 'col'), [(n, n ^ offset) for n in devices])  16.9 us
    all_to_all x1, blocking collectives, exchanged(): lax.all_to_all(summed, ('row', 'col'), 0, 0, tiled=True, axis_index_group...  13.4 us
    pallas_call x1, Pallas kernels, exchanged(): pl.pallas_call(right_kernel, in_specs=[HBM] * 5, out_specs=[VMEM] * (GROU...  2.52 us
    pallas_call x1, Pallas kernels, exchanged(): pl.pallas_call(output_kernel, in_specs=[VMEM] * 5, out_specs=HBM, out_sha...  1.65 us
  transfers between devices with their start and end apart: 22, of which 11 were waited for; matrix products, arithmetic and copies ran while one was open for 0% of the time, Pallas kernels for 3%

profile of v5, /device:TPU:0, one launch (start us, length us, event | category | flops | bytes accessed | tf_op | source)
XLA Modules:
  0.0 59.7 jit_solution(14549155963584902751)
XLA Ops:
  0.0 2.5 %right.1 = (bf16[32,16,128]{2,1,0:T(8,128)(2,1)S(1)}, bf16[32,16,128]{2,1,0:T(8,128)(2,1)S(1)}, bf16[32,16,128]{2,1,0:T(8,128)(2,1)S(1)}, bf16[32,16,128]{2,1,0:T(8,128)(2,1)S(1)}, bf16[2048,128]{1,0:T(8,128)(2,1)S(1)}) custom-call(f32[16,128,128]{2,1,0:T(8,128)} %map_hbm.1, s32[16,128]{1,0:T(8,128)} %mask_ref.1, f32[1,128]{1,0:T(1,128)} %bitcast.4, ...), custom_call_target="tpu_custom_call" | custom-call | tf_op jit(solution)/shard_map/right/pallas_call | solution.py:258
  2.5 0.0 copy-start.2
  2.5 3.1 %collective-permute-start = (bf16[32,16,128]{2,1,0:T(8,128)(2,1)S(1)}, bf16[32,16,128]{2,1,0:T(8,128)(2,1)S(1)}, u32[]{:S(2)}, u32[]{:S(2)}) collective-permute-start(bf16[32,16,128]{2,1,0:T(8,128)(2,1)S(1)} %get-tuple-element.21), channel_id=1, source_target_pairs={{0,1},{1,0},{2,3},{3,2},{4,5},{5,4},{6,7},{7,6},{8,9},{9,8},{10,11... | collective-permute-start | bytes 393224 | tf_op jit(solution)/shard_map/ppermute | solution.py:250
  5.6 1.5 %collective-permute-start.1 = (bf16[32,16,128]{2,1,0:T(8,128)(2,1)S(1)}, bf16[32,16,128]{2,1,0:T(8,128)(2,1)S(1)}, u32[]{:S(2)}, u32[]{:S(2)}) collective-permute-start(bf16[32,16,128]{2,1,0:T(8,128)(2,1)S(1)} %get-tuple-element.22), channel_id=1, source_target_pairs={{0,4},{1,5},{2,6},{3,7},{4,0},{5,1},{6,2},{7,3},{8,12},{9,13},{10,... | collective-permute-start | bytes 393224 | tf_op jit(solution)/shard_map/ppermute | solution.py:250
  7.1 0.1 collective-permute-start.2
  7.2 0.0 collective-permute-start.3
  7.2 0.0 copy-start.1
  7.2 0.7 %left.1 = (bf16[32,16,128]{2,1,0:T(8,128)(2,1)S(1)}, bf16[32,16,128]{2,1,0:T(8,128)(2,1)S(1)}, bf16[32,16,128]{2,1,0:T(8,128)(2,1)S(1)}, bf16[32,16,128]{2,1,0:T(8,128)(2,1)S(1)}) custom-call(bf16[2048,128]{1,0:T(8,128)(2,1)S(1)} %get-tuple-element.19.normed_ref, s32[16,128]{1,0:T(8,128)S(1)} %copy-done.2, bf16[128,512]{1,0:T(8,128)(2,1)S(1)} %copy-done), custom_call_target="tpu_custom_call" | custom-call | tf_op jit(solution)/shard_map/left/pallas_call | solution.py:276
  7.9 2.0 %collective-permute-start.15 = (bf16[32,16,128]{2,1,0:T(8,128)(2,1)S(1)}, bf16[32,16,128]{2,1,0:T(8,128)(2,1)S(1)}, u32[]{:S(2)}, u32[]{:S(2)}) collective-permute-start(bf16[32,16,128]{2,1,0:T(8,128)(2,1)S(1)} %get-tuple-element.26), channel_id=1, source_target_pairs={{0,1},{1,0},{2,3},{3,2},{4,5},{5,4},{6,7},{7,6},{8,9},{9,8},{10,11... | collective-permute-start | bytes 393224 | tf_op jit(solution)/shard_map/ppermute | solution.py:250
  9.9 0.0 collective-permute-done.refs_1_
  9.9 1.5 %collective-permute-start.16 = (bf16[32,16,128]{2,1,0:T(8,128)(2,1)S(1)}, bf16[32,16,128]{2,1,0:T(8,128)(2,1)S(1)}, u32[]{:S(2)}, u32[]{:S(2)}) collective-permute-start(bf16[32,16,128]{2,1,0:T(8,128)(2,1)S(1)} %get-tuple-element.27), channel_id=1, source_target_pairs={{0,4},{1,5},{2,6},{3,7},{4,0},{5,1},{6,2},{7,3},{8,12},{9,13},{10,... | collective-permute-start | bytes 393224 | tf_op jit(solution)/shard_map/ppermute | solution.py:250
  11.4 0.6 collective-permute-done.1.refs_2_
  12.0 1.4 %collective-permute-start.17 = (bf16[32,16,128]{2,1,0:T(8,128)(2,1)S(1)}, bf16[32,16,128]{2,1,0:T(8,128)(2,1)S(1)}, u32[]{:S(2)}, u32[]{:S(2)}) collective-permute-start(bf16[32,16,128]{2,1,0:T(8,128)(2,1)S(1)} %get-tuple-element.28), channel_id=1, source_target_pairs={{0,5},{1,4},{2,7},{3,6},{4,1},{5,0},{6,3},{7,2},{8,13},{9,12},{10,... | collective-permute-start | bytes 393224 | tf_op jit(solution)/shard_map/ppermute | solution.py:250
  13.4 0.4 collective-permute-done.2.refs_3_
  13.8 1.7 %collective-permute-start.18 = (bf16[32,16,128]{2,1,0:T(8,128)(2,1)S(1)}, bf16[32,16,128]{2,1,0:T(8,128)(2,1)S(1)}, u32[]{:S(2)}, u32[]{:S(2)}) collective-permute-start(bf16[32,16,128]{2,1,0:T(8,128)(2,1)S(1)} %get-tuple-element.25.refs_8_), channel_id=1, source_target_pairs={{0,8},{1,9},{2,10},{3,11},{4,12},{5,13},{6,14},{7,15},{8,0},{9,1},... | collective-permute-start | bytes 393224 | tf_op jit(solution)/shard_map/ppermute | solution.py:250
  15.6 0.0 collective-permute-done.3.refs_4_
  15.6 2.6 %collective-permute-start.7 = (bf16[32,16,128]{2,1,0:T(8,128)(2,1)S(1)}, bf16[32,16,128]{2,1,0:T(8,128)(2,1)S(1)}, u32[]{:S(2)}, u32[]{:S(2)}) collective-permute-start(bf16[32,16,128]{2,1,0:T(8,128)(2,1)S(1)} %get-tuple-element.20.refs_0_), channel_id=1, source_target_pairs={{0,16},{1,17},{2,18},{3,19},{4,20},{5,21},{6,22},{7,23},{8,24},{9,... | collective-permute-start | bytes 393224 | tf_op jit(solution)/shard_map/ppermute | solution.py:250
  18.2 0.0 collective-permute-done.15.refs_9_
  18.2 0.0 collective-permute-start.4
  18.2 0.0 collective-permute-done.16.refs_10_
  18.2 0.5 collective-permute-start.5
  18.7 0.1 collective-permute-done.17.refs_11_
  18.8 1.2 %collective-permute-done.18.refs_12_ = bf16[32,16,128]{2,1,0:T(8,128)(2,1)S(1)} collective-permute-done((bf16[32,16,128]{2,1,0:T(8,128)(2,1)S(1)}, bf16[32,16,128]{2,1,0:T(8,128)(2,1)S(1)}, u32[]{:S(2)}, u32[]{:S(2)}) %collective-permute-start.18) | collective-permute-done | bytes 131104 | tf_op jit(solution)/shard_map/ppermute | solution.py:250
  20.0 1.7 %collective-permute-start.19 = (bf16[32,16,128]{2,1,0:T(8,128)(2,1)S(1)}, bf16[32,16,128]{2,1,0:T(8,128)(2,1)S(1)}, u32[]{:S(2)}, u32[]{:S(2)}) collective-permute-start(bf16[32,16,128]{2,1,0:T(8,128)(2,1)S(1)} %collective-permute-done.15.refs_9_), channel_id=1, source_target_pairs={{0,8},{1,9},{2,10},{3,11},{4,12},{5,13},{6,14},{7,15},{8,0},{9,1},... | collective-permute-start | bytes 393224 | tf_op jit(solution)/shard_map/ppermute | solution.py:250
  21.7 1.3 %collective-permute-done.7.refs_0_ = bf16[32,16,128]{2,1,0:T(8,128)(2,1)S(1)} collective-permute-done((bf16[32,16,128]{2,1,0:T(8,128)(2,1)S(1)}, bf16[32,16,128]{2,1,0:T(8,128)(2,1)S(1)}, u32[]{:S(2)}, u32[]{:S(2)}) %collective-permute-start.7) | collective-permute-done | bytes 131104 | tf_op jit(solution)/shard_map/ppermute | solution.py:250
  23.0 0.3 collective-permute-start.20
  23.3 0.0 collective-permute-done.4.refs_5_
  23.3 2.9 %collective-permute-start.8 = (bf16[32,16,128]{2,1,0:T(8,128)(2,1)S(1)}, bf16[32,16,128]{2,1,0:T(8,128)(2,1)S(1)}, u32[]{:S(2)}, u32[]{:S(2)}) collective-permute-start(bf16[32,16,128]{2,1,0:T(8,128)(2,1)S(1)} %collective-permute-done.refs_1_), channel_id=1, source_target_pairs={{0,16},{1,17},{2,18},{3,19},{4,20},{5,21},{6,22},{7,23},{8,24},{9,... | collective-permute-start | bytes 393224 | tf_op jit(solution)/shard_map/ppermute | solution.py:250
  26.3 0.0 collective-permute-done.5.refs_6_
  26.3 0.1 collective-permute-start.9
  26.3 2.9 %collective-permute-start.10 = (bf16[32,16,128]{2,1,0:T(8,128)(2,1)S(1)}, bf16[32,16,128]{2,1,0:T(8,128)(2,1)S(1)}, u32[]{:S(2)}, u32[]{:S(2)}) collective-permute-start(bf16[32,16,128]{2,1,0:T(8,128)(2,1)S(1)} %collective-permute-done.2.refs_3_), channel_id=1, source_target_pairs={{0,16},{1,17},{2,18},{3,19},{4,20},{5,21},{6,22},{7,23},{8,24},{9,... | collective-permute-start | bytes 393224 | tf_op jit(solution)/shard_map/ppermute | solution.py:250
  29.2 1.6 %collective-permute-done.19.refs_13_ = bf16[32,16,128]{2,1,0:T(8,128)(2,1)S(1)} collective-permute-done((bf16[32,16,128]{2,1,0:T(8,128)(2,1)S(1)}, bf16[32,16,128]{2,1,0:T(8,128)(2,1)S(1)}, u32[]{:S(2)}, u32[]{:S(2)}) %collective-permute-start.19) | collective-permute-done | bytes 131104 | tf_op jit(solution)/shard_map/ppermute | solution.py:250
  30.8 2.7 %collective-permute-done.20.refs_14_ = bf16[32,16,128]{2,1,0:T(8,128)(2,1)S(1)} collective-permute-done((bf16[32,16,128]{2,1,0:T(8,128)(2,1)S(1)}, bf16[32,16,128]{2,1,0:T(8,128)(2,1)S(1)}, u32[]{:S(2)}, u32[]{:S(2)}) %collective-permute-start.20) | collective-permute-done | bytes 131104 | tf_op jit(solution)/shard_map/ppermute | solution.py:250
  33.5 0.0 collective-permute-start.11
  33.5 5.6 %collective-permute-done.8.refs_1_ = bf16[32,16,128]{2,1,0:T(8,128)(2,1)S(1)} collective-permute-done((bf16[32,16,128]{2,1,0:T(8,128)(2,1)S(1)}, bf16[32,16,128]{2,1,0:T(8,128)(2,1)S(1)}, u32[]{:S(2)}, u32[]{:S(2)}) %collective-permute-start.8) | collective-permute-done | bytes 131104 | tf_op jit(solution)/shard_map/ppermute | solution.py:250
  39.0 0.0 collective-permute-start.12
  39.0 1.8 %collective-permute-done.9.refs_2_ = bf16[32,16,128]{2,1,0:T(8,128)(2,1)S(1)} collective-permute-done((bf16[32,16,128]{2,1,0:T(8,128)(2,1)S(1)}, bf16[32,16,128]{2,1,0:T(8,128)(2,1)S(1)}, u32[]{:S(2)}, u32[]{:S(2)}) %collective-permute-start.9) | collective-permute-done | bytes 131104 | tf_op jit(solution)/shard_map/ppermute | solution.py:250
  40.8 0.0 collective-permute-start.13
  40.8 1.4 %collective-permute-done.10.refs_3_ = bf16[32,16,128]{2,1,0:T(8,128)(2,1)S(1)} collective-permute-done((bf16[32,16,128]{2,1,0:T(8,128)(2,1)S(1)}, bf16[32,16,128]{2,1,0:T(8,128)(2,1)S(1)}, u32[]{:S(2)}, u32[]{:S(2)}) %collective-permute-start.10) | collective-permute-done | bytes 131104 | tf_op jit(solution)/shard_map/ppermute | solution.py:250
  42.2 0.0 collective-permute-start.14
  42.2 1.0 %gates.1 = (f32[16,128,128]{2,1,0:T(8,128)S(1)}, f32[1,128]{1,0:T(1,128)S(1)}, f32[1,128]{1,0:T(1,128)S(1)}, bf16[128,128]{1,0:T(8,128)(2,1)S(1)}, bf16[2,32,64,128]{3,2,1,0:T(8,128)(2,1)S(1)}) custom-call(bf16[2048,128]{1,0:T(8,128)(2,1)S(1)} %get-tuple-element.19.normed_ref, bf16[128,128]{1,0:T(8,128)(2,1)S(1)} %copy-done.1, ...), custom_call_target="tpu_custom_call" | custom-call | tf_op jit(solution)/shard_map/gates/pallas_call | solution.py:290
  43.3 0.0 collective-permute-done.21.refs_15_
  43.3 0.0 collective-permute-done.11.refs_4_
  43.3 0.0 collective-permute-done.13.refs_6_
  43.3 0.2 collective-permute-done.14.refs_7_
  43.6 1.1 %pairs.1 = bf16[8,16,16,128]{3,2,1,0:T(8,128)(2,1)S(1)} custom-call(bf16[2,32,64,128]{3,2,1,0:T(8,128)(2,1)S(1)} %get-tuple-element.24.near_ref, bf16[32,16,128]{2,1,0:T(8,128)(2,1)S(1)} %collective-permute-done.7.refs_0_, bf16[32,16,128]{2,1,0:T(8,128)(2,1)S(1)} %collective-permute-done.8.refs_1_, bf16[32,16,128]{2,1,0:T(8,128)(2,1)S(1)} %collective-permute-done.9.refs_2_, ...), custom_call_target="tpu_custom_call" | custom-call | tf_op jit(solution)/shard_map/pairs/pallas_call | solution.py:313
  44.7 13.4 %all_to_all.5.summed_ref = bf16[8,16,16,128]{3,2,1,0:T(8,128)(2,1)S(1)} all-to-all(bf16[8,16,16,128]{3,2,1,0:T(8,128)(2,1)S(1)} %pairs.1), channel_id=1, replica_groups={{0,1,4,5,8,9,12,13},{2,3,6,7,10,11,14,15},{16,17,20,21,24,25,28,29},{18..., dimensions={0} | all-to-all | bytes 1048576 | tf_op jit(solution)/shard_map/all_to_all | solution.py:326
  58.0 1.7 %output.1 = f32[16,128,128]{2,1,0:T(8,128)} custom-call(bf16[8,16,16,128]{3,2,1,0:T(8,128)(2,1)S(1)} %all_to_all.5.summed_ref, f32[16,128,128]{2,1,0:T(8,128)S(1)} %get-tuple-element.29.gating_ref, f32[1,128]{1,0:T(1,128)S(1)} %get-tuple-element.30.gain_ref, f32[1,128]{1,0:T(1,128)S(1)} %get-tuple-element.31.bias_ref, ...), custom_call_target="tpu_custom_call" | custom-call | tf_op jit(solution)/shard_map/output/pallas_call | solution.py:327
  (8 shorter events, 0.0 us)
Async XLA Ops:
  0.0 7.2 %copy-start = (bf16[128,512]{1,0:T(8,128)(2,1)S(1)}, bf16[128,512]{1,0:T(8,128)(2,1)}, u32[]{:S(2)}) copy-start(bf16[128,512]{1,0:T(8,128)(2,1)} %w_ref.1) | copy-start | bytes 393220
  2.5 4.6 %copy-start.2 = (s32[16,128]{1,0:T(8,128)S(1)}, s32[16,128]{1,0:T(8,128)}, u32[]{:S(2)}) copy-start(s32[16,128]{1,0:T(8,128)} %mask_ref.1) | copy-start | bytes 24580
  2.5 7.4 %collective-permute-start = (bf16[32,16,128]{2,1,0:T(8,128)(2,1)S(1)}, bf16[32,16,128]{2,1,0:T(8,128)(2,1)S(1)}, u32[]{:S(2)}, u32[]{:S(2)}) collective-permute-start(bf16[32,16,128]{2,1,0:T(8,128)(2,1)S(1)} %get-tuple-element.21), channel_id=1, source_target_pairs={{0,1},{1,0},{2,3},{3,2},{4,5},{5,4},{6,7},{7,6},{8,9},{9,8},{10,11... | collective-permute-start | bytes 393224 | tf_op jit(solution)/shard_map/ppermute | solution.py:250
  5.6 6.4 %collective-permute-start.1 = (bf16[32,16,128]{2,1,0:T(8,128)(2,1)S(1)}, bf16[32,16,128]{2,1,0:T(8,128)(2,1)S(1)}, u32[]{:S(2)}, u32[]{:S(2)}) collective-permute-start(bf16[32,16,128]{2,1,0:T(8,128)(2,1)S(1)} %get-tuple-element.22), channel_id=1, source_target_pairs={{0,4},{1,5},{2,6},{3,7},{4,0},{5,1},{6,2},{7,3},{8,12},{9,13},{10,... | collective-permute-start | bytes 393224 | tf_op jit(solution)/shard_map/ppermute | solution.py:250
  7.1 6.7 %collective-permute-start.2 = (bf16[32,16,128]{2,1,0:T(8,128)(2,1)S(1)}, bf16[32,16,128]{2,1,0:T(8,128)(2,1)S(1)}, u32[]{:S(2)}, u32[]{:S(2)}) collective-permute-start(bf16[32,16,128]{2,1,0:T(8,128)(2,1)S(1)} %get-tuple-element.23), channel_id=1, source_target_pairs={{0,5},{1,4},{2,7},{3,6},{4,1},{5,0},{6,3},{7,2},{8,13},{9,12},{10,... | collective-permute-start | bytes 393224 | tf_op jit(solution)/shard_map/ppermute | solution.py:250
  7.2 8.4 %collective-permute-start.3 = (bf16[32,16,128]{2,1,0:T(8,128)(2,1)S(1)}, bf16[32,16,128]{2,1,0:T(8,128)(2,1)S(1)}, u32[]{:S(2)}, u32[]{:S(2)}) collective-permute-start(bf16[32,16,128]{2,1,0:T(8,128)(2,1)S(1)} %get-tuple-element.20.refs_0_), channel_id=1, source_target_pairs={{0,2},{1,3},{2,0},{3,1},{4,6},{5,7},{6,4},{7,5},{8,10},{9,11},{10,... | collective-permute-start | bytes 393224 | tf_op jit(solution)/shard_map/ppermute | solution.py:250
  7.2 35.1 %copy-start.1 = (bf16[128,128]{1,0:T(8,128)(2,1)S(1)}, bf16[128,128]{1,0:T(8,128)(2,1)}, u32[]{:S(2)}) copy-start(bf16[128,128]{1,0:T(8,128)(2,1)} %w_gate_ref.1) | copy-start | bytes 98308
  7.9 10.3 %collective-permute-start.15 = (bf16[32,16,128]{2,1,0:T(8,128)(2,1)S(1)}, bf16[32,16,128]{2,1,0:T(8,128)(2,1)S(1)}, u32[]{:S(2)}, u32[]{:S(2)}) collective-permute-start(bf16[32,16,128]{2,1,0:T(8,128)(2,1)S(1)} %get-tuple-element.26), channel_id=1, source_target_pairs={{0,1},{1,0},{2,3},{3,2},{4,5},{5,4},{6,7},{7,6},{8,9},{9,8},{10,11... | collective-permute-start | bytes 393224 | tf_op jit(solution)/shard_map/ppermute | solution.py:250
  9.9 8.3 %collective-permute-start.16 = (bf16[32,16,128]{2,1,0:T(8,128)(2,1)S(1)}, bf16[32,16,128]{2,1,0:T(8,128)(2,1)S(1)}, u32[]{:S(2)}, u32[]{:S(2)}) collective-permute-start(bf16[32,16,128]{2,1,0:T(8,128)(2,1)S(1)} %get-tuple-element.27), channel_id=1, source_target_pairs={{0,4},{1,5},{2,6},{3,7},{4,0},{5,1},{6,2},{7,3},{8,12},{9,13},{10,... | collective-permute-start | bytes 393224 | tf_op jit(solution)/shard_map/ppermute | solution.py:250
  12.0 6.8 %collective-permute-start.17 = (bf16[32,16,128]{2,1,0:T(8,128)(2,1)S(1)}, bf16[32,16,128]{2,1,0:T(8,128)(2,1)S(1)}, u32[]{:S(2)}, u32[]{:S(2)}) collective-permute-start(bf16[32,16,128]{2,1,0:T(8,128)(2,1)S(1)} %get-tuple-element.28), channel_id=1, source_target_pairs={{0,5},{1,4},{2,7},{3,6},{4,1},{5,0},{6,3},{7,2},{8,13},{9,12},{10,... | collective-permute-start | bytes 393224 | tf_op jit(solution)/shard_map/ppermute | solution.py:250
  13.8 6.2 %collective-permute-start.18 = (bf16[32,16,128]{2,1,0:T(8,128)(2,1)S(1)}, bf16[32,16,128]{2,1,0:T(8,128)(2,1)S(1)}, u32[]{:S(2)}, u32[]{:S(2)}) collective-permute-start(bf16[32,16,128]{2,1,0:T(8,128)(2,1)S(1)} %get-tuple-element.25.refs_8_), channel_id=1, source_target_pairs={{0,8},{1,9},{2,10},{3,11},{4,12},{5,13},{6,14},{7,15},{8,0},{9,1},... | collective-permute-start | bytes 393224 | tf_op jit(solution)/shard_map/ppermute | solution.py:250
  15.6 7.4 %collective-permute-start.7 = (bf16[32,16,128]{2,1,0:T(8,128)(2,1)S(1)}, bf16[32,16,128]{2,1,0:T(8,128)(2,1)S(1)}, u32[]{:S(2)}, u32[]{:S(2)}) collective-permute-start(bf16[32,16,128]{2,1,0:T(8,128)(2,1)S(1)} %get-tuple-element.20.refs_0_), channel_id=1, source_target_pairs={{0,16},{1,17},{2,18},{3,19},{4,20},{5,21},{6,22},{7,23},{8,24},{9,... | collective-permute-start | bytes 393224 | tf_op jit(solution)/shard_map/ppermute | solution.py:250
  18.2 5.2 %collective-permute-start.4 = (bf16[32,16,128]{2,1,0:T(8,128)(2,1)S(1)}, bf16[32,16,128]{2,1,0:T(8,128)(2,1)S(1)}, u32[]{:S(2)}, u32[]{:S(2)}) collective-permute-start(bf16[32,16,128]{2,1,0:T(8,128)(2,1)S(1)} %collective-permute-done.refs_1_), channel_id=1, source_target_pairs={{0,2},{1,3},{2,0},{3,1},{4,6},{5,7},{6,4},{7,5},{8,10},{9,11},{10,... | collective-permute-start | bytes 393224 | tf_op jit(solution)/shard_map/ppermute | solution.py:250
  18.2 8.1 %collective-permute-start.5 = (bf16[32,16,128]{2,1,0:T(8,128)(2,1)S(1)}, bf16[32,16,128]{2,1,0:T(8,128)(2,1)S(1)}, u32[]{:S(2)}, u32[]{:S(2)}) collective-permute-start(bf16[32,16,128]{2,1,0:T(8,128)(2,1)S(1)} %collective-permute-done.1.refs_2_), channel_id=1, source_target_pairs={{0,2},{1,3},{2,0},{3,1},{4,6},{5,7},{6,4},{7,5},{8,10},{9,11},{10,... | collective-permute-start | bytes 393224 | tf_op jit(solution)/shard_map/ppermute | solution.py:250
  18.8 7.5 %collective-permute-start.6 = (bf16[32,16,128]{2,1,0:T(8,128)(2,1)S(1)}, bf16[32,16,128]{2,1,0:T(8,128)(2,1)S(1)}, u32[]{:S(2)}, u32[]{:S(2)}) collective-permute-start(bf16[32,16,128]{2,1,0:T(8,128)(2,1)S(1)} %collective-permute-done.2.refs_3_), channel_id=1, source_target_pairs={{0,2},{1,3},{2,0},{3,1},{4,6},{5,7},{6,4},{7,5},{8,10},{9,11},{10,... | collective-permute-start | bytes 393224 | tf_op jit(solution)/shard_map/ppermute | solution.py:250
  20.0 10.8 %collective-permute-start.19 = (bf16[32,16,128]{2,1,0:T(8,128)(2,1)S(1)}, bf16[32,16,128]{2,1,0:T(8,128)(2,1)S(1)}, u32[]{:S(2)}, u32[]{:S(2)}) collective-permute-start(bf16[32,16,128]{2,1,0:T(8,128)(2,1)S(1)} %collective-permute-done.15.refs_9_), channel_id=1, source_target_pairs={{0,8},{1,9},{2,10},{3,11},{4,12},{5,13},{6,14},{7,15},{8,0},{9,1},... | collective-permute-start | bytes 393224 | tf_op jit(solution)/shard_map/ppermute | solution.py:250
  23.0 10.5 %collective-permute-start.20 = (bf16[32,16,128]{2,1,0:T(8,128)(2,1)S(1)}, bf16[32,16,128]{2,1,0:T(8,128)(2,1)S(1)}, u32[]{:S(2)}, u32[]{:S(2)}) collective-permute-start(bf16[32,16,128]{2,1,0:T(8,128)(2,1)S(1)} %collective-permute-done.16.refs_10_), channel_id=1, source_target_pairs={{0,8},{1,9},{2,10},{3,11},{4,12},{5,13},{6,14},{7,15},{8,0},{9,1},... | collective-permute-start | bytes 393224 | tf_op jit(solution)/shard_map/ppermute | solution.py:250
  23.3 15.7 %collective-permute-start.8 = (bf16[32,16,128]{2,1,0:T(8,128)(2,1)S(1)}, bf16[32,16,128]{2,1,0:T(8,128)(2,1)S(1)}, u32[]{:S(2)}, u32[]{:S(2)}) collective-permute-start(bf16[32,16,128]{2,1,0:T(8,128)(2,1)S(1)} %collective-permute-done.refs_1_), channel_id=1, source_target_pairs={{0,16},{1,17},{2,18},{3,19},{4,20},{5,21},{6,22},{7,23},{8,24},{9,... | collective-permute-start | bytes 393224 | tf_op jit(solution)/shard_map/ppermute | solution.py:250
  26.3 14.6 %collective-permute-start.9 = (bf16[32,16,128]{2,1,0:T(8,128)(2,1)S(1)}, bf16[32,16,128]{2,1,0:T(8,128)(2,1)S(1)}, u32[]{:S(2)}, u32[]{:S(2)}) collective-permute-start(bf16[32,16,128]{2,1,0:T(8,128)(2,1)S(1)} %collective-permute-done.1.refs_2_), channel_id=1, source_target_pairs={{0,16},{1,17},{2,18},{3,19},{4,20},{5,21},{6,22},{7,23},{8,24},{9,... | collective-permute-start | bytes 393224 | tf_op jit(solution)/shard_map/ppermute | solution.py:250
  26.3 15.9 %collective-permute-start.10 = (bf16[32,16,128]{2,1,0:T(8,128)(2,1)S(1)}, bf16[32,16,128]{2,1,0:T(8,128)(2,1)S(1)}, u32[]{:S(2)}, u32[]{:S(2)}) collective-permute-start(bf16[32,16,128]{2,1,0:T(8,128)(2,1)S(1)} %collective-permute-done.2.refs_3_), channel_id=1, source_target_pairs={{0,16},{1,17},{2,18},{3,19},{4,20},{5,21},{6,22},{7,23},{8,24},{9,... | collective-permute-start | bytes 393224 | tf_op jit(solution)/shard_map/ppermute | solution.py:250
  30.8 12.5 %collective-permute-start.21 = (bf16[32,16,128]{2,1,0:T(8,128)(2,1)S(1)}, bf16[32,16,128]{2,1,0:T(8,128)(2,1)S(1)}, u32[]{:S(2)}, u32[]{:S(2)}) collective-permute-start(bf16[32,16,128]{2,1,0:T(8,128)(2,1)S(1)} %collective-permute-done.17.refs_11_), channel_id=1, source_target_pairs={{0,8},{1,9},{2,10},{3,11},{4,12},{5,13},{6,14},{7,15},{8,0},{9,1},... | collective-permute-start | bytes 393224 | tf_op jit(solution)/shard_map/ppermute | solution.py:250
  33.5 9.8 %collective-permute-start.11 = (bf16[32,16,128]{2,1,0:T(8,128)(2,1)S(1)}, bf16[32,16,128]{2,1,0:T(8,128)(2,1)S(1)}, u32[]{:S(2)}, u32[]{:S(2)}) collective-permute-start(bf16[32,16,128]{2,1,0:T(8,128)(2,1)S(1)} %collective-permute-done.7.refs_0_), channel_id=1, source_target_pairs={{0,2},{1,3},{2,0},{3,1},{4,6},{5,7},{6,4},{7,5},{8,10},{9,11},{10,... | collective-permute-start | bytes 393224 | tf_op jit(solution)/shard_map/ppermute | solution.py:250
  39.0 4.3 %collective-permute-start.12 = (bf16[32,16,128]{2,1,0:T(8,128)(2,1)S(1)}, bf16[32,16,128]{2,1,0:T(8,128)(2,1)S(1)}, u32[]{:S(2)}, u32[]{:S(2)}) collective-permute-start(bf16[32,16,128]{2,1,0:T(8,128)(2,1)S(1)} %collective-permute-done.8.refs_1_), channel_id=1, source_target_pairs={{0,2},{1,3},{2,0},{3,1},{4,6},{5,7},{6,4},{7,5},{8,10},{9,11},{10,... | collective-permute-start | bytes 393224 | tf_op jit(solution)/shard_map/ppermute | solution.py:250
  40.8 2.5 %collective-permute-start.13 = (bf16[32,16,128]{2,1,0:T(8,128)(2,1)S(1)}, bf16[32,16,128]{2,1,0:T(8,128)(2,1)S(1)}, u32[]{:S(2)}, u32[]{:S(2)}) collective-permute-start(bf16[32,16,128]{2,1,0:T(8,128)(2,1)S(1)} %collective-permute-done.9.refs_2_), channel_id=1, source_target_pairs={{0,2},{1,3},{2,0},{3,1},{4,6},{5,7},{6,4},{7,5},{8,10},{9,11},{10,... | collective-permute-start | bytes 393224 | tf_op jit(solution)/shard_map/ppermute | solution.py:250
  42.2 1.3 %collective-permute-start.14 = (bf16[32,16,128]{2,1,0:T(8,128)(2,1)S(1)}, bf16[32,16,128]{2,1,0:T(8,128)(2,1)S(1)}, u32[]{:S(2)}, u32[]{:S(2)}) collective-permute-start(bf16[32,16,128]{2,1,0:T(8,128)(2,1)S(1)} %collective-permute-done.10.refs_3_), channel_id=1, source_target_pairs={{0,2},{1,3},{2,0},{3,1},{4,6},{5,7},{6,4},{7,5},{8,10},{9,11},{10,... | collective-permute-start | bytes 393224 | tf_op jit(solution)/shard_map/ppermute | solution.py:250

commit v6 on v5

--- a/solution.py
+++ b/solution.py
@@ -130,8 +130,8 @@
     wait_bias()
     wait_mask()
     wait_map()
-    block = rows // 4
-    for step in range(4):
+    block = rows // 8
+    for step in range(8):
         values = map_scr[step * block : (step + 1) * block].reshape(block * cols, channels)
         normed = layer_norm(values, gain_scr[...], bias_scr[...]).astype(BF16)
         normed_ref[step * block * cols : (step + 1) * block * cols, :] = normed
@@ -226,12 +226,9 @@
             for high in range(2):
                 at, where = row + high * low, slice(part * cols // 2, (part + 1) * cols // 2)
                 out_scr[at, where] = gating_ref[at, where] * result[high * cols // 2 : (high + 1) * cols // 2]
-        if row % 2:
-            for high in range(2):
-                ready = pl.ds(row - 1 + high * low, 2)
-                waits += start_copies(
-                    [(out_scr.at[ready], out_hbm.at[ready])], sems.at[pl.ds(row // 2 + high * low // 2, 1)]
-                )
+        for high in range(2):
+            ready = pl.ds(row + high * low, 1)
+            waits += start_copies([(out_scr.at[ready], out_hbm.at[ready])], sems.at[ready])
     for wait in waits:
         wait()
 
@@ -332,7 +329,7 @@
         scratch_shapes=[
             pltpu.VMEM((2, hidden * rows // 2, cols), F32),
             pltpu.VMEM((rows, cols, channels), F32),
-            pltpu.SemaphoreType.DMA((rows // 2,)),
+            pltpu.SemaphoreType.DMA((rows,)),
         ],
         compiler_params=params,
         name="output",

time: 59.9 us -> 59.9 us (level)
  no operation moved by 1% of the time
where the time goes in v6:
time: 59.9 us; the launch traced here: 59.7 us
  starting transfers between devices  22.3 us (37%)
  waiting for transfers between devices  16.9 us (28%)
  blocking collectives  13.4 us (22%)
  Pallas kernels  7.04 us (12%)
    ppermute x22, starting transfers between devices, swap(): lax.ppermute(array, ('row', 'col'), [(n, n ^ offset) for n in devices])  22.3 us
    ppermute x22, waiting for transfers between devices, swap(): lax.ppermute(array, ('row', 'col'), [(n, n ^ offset) for n in devices])  16.9 us
    all_to_all x1, blocking collectives, exchanged(): lax.all_to_all(summed, ('row', 'col'), 0, 0, tiled=True, axis_index_group...  13.4 us
    pallas_call x1, Pallas kernels, exchanged(): pl.pallas_call(right_kernel, in_specs=[HBM] * 5, out_specs=[VMEM] * (GROU...  2.52 us
    pallas_call x1, Pallas kernels, exchanged(): pl.pallas_call(output_kernel, in_specs=[VMEM] * 5, out_specs=HBM, out_sha...  1.68 us
  transfers between devices with their start and end apart: 22, of which 11 were waited for; matrix products, arithmetic and copies ran while one was open for 0% of the time, Pallas kernels for 3%

profile of v6, /device:TPU:0, one launch (start us, length us, event | category | flops | bytes accessed | tf_op | source)
XLA Modules:
  0.0 59.7 jit_solution(13975357654093980472)
XLA Ops:
  0.0 2.5 %right.1 = (bf16[32,16,128]{2,1,0:T(8,128)(2,1)S(1)}, bf16[32,16,128]{2,1,0:T(8,128)(2,1)S(1)}, bf16[32,16,128]{2,1,0:T(8,128)(2,1)S(1)}, bf16[32,16,128]{2,1,0:T(8,128)(2,1)S(1)}, bf16[2048,128]{1,0:T(8,128)(2,1)S(1)}) custom-call(f32[16,128,128]{2,1,0:T(8,128)} %map_hbm.1, s32[16,128]{1,0:T(8,128)} %mask_ref.1, f32[1,128]{1,0:T(1,128)} %bitcast.4, ...), custom_call_target="tpu_custom_call" | custom-call | tf_op jit(solution)/shard_map/right/pallas_call | solution.py:255
  2.5 0.0 copy-start.2
  2.5 3.1 %collective-permute-start = (bf16[32,16,128]{2,1,0:T(8,128)(2,1)S(1)}, bf16[32,16,128]{2,1,0:T(8,128)(2,1)S(1)}, u32[]{:S(2)}, u32[]{:S(2)}) collective-permute-start(bf16[32,16,128]{2,1,0:T(8,128)(2,1)S(1)} %get-tuple-element.21), channel_id=1, source_target_pairs={{0,1},{1,0},{2,3},{3,2},{4,5},{5,4},{6,7},{7,6},{8,9},{9,8},{10,11... | collective-permute-start | bytes 393224 | tf_op jit(solution)/shard_map/ppermute | solution.py:247
  5.6 1.5 %collective-permute-start.1 = (bf16[32,16,128]{2,1,0:T(8,128)(2,1)S(1)}, bf16[32,16,128]{2,1,0:T(8,128)(2,1)S(1)}, u32[]{:S(2)}, u32[]{:S(2)}) collective-permute-start(bf16[32,16,128]{2,1,0:T(8,128)(2,1)S(1)} %get-tuple-element.22), channel_id=1, source_target_pairs={{0,4},{1,5},{2,6},{3,7},{4,0},{5,1},{6,2},{7,3},{8,12},{9,13},{10,... | collective-permute-start | bytes 393224 | tf_op jit(solution)/shard_map/ppermute | solution.py:247
  7.1 0.1 collective-permute-start.2
  7.2 0.0 collective-permute-start.3
  7.2 0.0 copy-start.1
  7.2 0.7 %left.1 = (bf16[32,16,128]{2,1,0:T(8,128)(2,1)S(1)}, bf16[32,16,128]{2,1,0:T(8,128)(2,1)S(1)}, bf16[32,16,128]{2,1,0:T(8,128)(2,1)S(1)}, bf16[32,16,128]{2,1,0:T(8,128)(2,1)S(1)}) custom-call(bf16[2048,128]{1,0:T(8,128)(2,1)S(1)} %get-tuple-element.19.normed_ref, s32[16,128]{1,0:T(8,128)S(1)} %copy-done.2, bf16[128,512]{1,0:T(8,128)(2,1)S(1)} %copy-done), custom_call_target="tpu_custom_call" | custom-call | tf_op jit(solution)/shard_map/left/pallas_call | solution.py:273
  7.9 2.0 %collective-permute-start.15 = (bf16[32,16,128]{2,1,0:T(8,128)(2,1)S(1)}, bf16[32,16,128]{2,1,0:T(8,128)(2,1)S(1)}, u32[]{:S(2)}, u32[]{:S(2)}) collective-permute-start(bf16[32,16,128]{2,1,0:T(8,128)(2,1)S(1)} %get-tuple-element.26), channel_id=1, source_target_pairs={{0,1},{1,0},{2,3},{3,2},{4,5},{5,4},{6,7},{7,6},{8,9},{9,8},{10,11... | collective-permute-start | bytes 393224 | tf_op jit(solution)/shard_map/ppermute | solution.py:247
  9.9 0.0 collective-permute-done.refs_1_
  9.9 1.5 %collective-permute-start.16 = (bf16[32,16,128]{2,1,0:T(8,128)(2,1)S(1)}, bf16[32,16,128]{2,1,0:T(8,128)(2,1)S(1)}, u32[]{:S(2)}, u32[]{:S(2)}) collective-permute-start(bf16[32,16,128]{2,1,0:T(8,128)(2,1)S(1)} %get-tuple-element.27), channel_id=1, source_target_pairs={{0,4},{1,5},{2,6},{3,7},{4,0},{5,1},{6,2},{7,3},{8,12},{9,13},{10,... | collective-permute-start | bytes 393224 | tf_op jit(solution)/shard_map/ppermute | solution.py:247
  11.4 0.6 collective-permute-done.1.refs_2_
  12.0 1.4 %collective-permute-start.17 = (bf16[32,16,128]{2,1,0:T(8,128)(2,1)S(1)}, bf16[32,16,128]{2,1,0:T(8,128)(2,1)S(1)}, u32[]{:S(2)}, u32[]{:S(2)}) collective-permute-start(bf16[32,16,128]{2,1,0:T(8,128)(2,1)S(1)} %get-tuple-element.28), channel_id=1, source_target_pairs={{0,5},{1,4},{2,7},{3,6},{4,1},{5,0},{6,3},{7,2},{8,13},{9,12},{10,... | collective-permute-start | bytes 393224 | tf_op jit(solution)/shard_map/ppermute | solution.py:247
  13.4 0.4 collective-permute-done.2.refs_3_
  13.8 1.7 %collective-permute-start.18 = (bf16[32,16,128]{2,1,0:T(8,128)(2,1)S(1)}, bf16[32,16,128]{2,1,0:T(8,128)(2,1)S(1)}, u32[]{:S(2)}, u32[]{:S(2)}) collective-permute-start(bf16[32,16,128]{2,1,0:T(8,128)(2,1)S(1)} %get-tuple-element.25.refs_8_), channel_id=1, source_target_pairs={{0,8},{1,9},{2,10},{3,11},{4,12},{5,13},{6,14},{7,15},{8,0},{9,1},... | collective-permute-start | bytes 393224 | tf_op jit(solution)/shard_map/ppermute | solution.py:247
  15.6 0.0 collective-permute-done.3.refs_4_
  15.6 2.6 %collective-permute-start.7 = (bf16[32,16,128]{2,1,0:T(8,128)(2,1)S(1)}, bf16[32,16,128]{2,1,0:T(8,128)(2,1)S(1)}, u32[]{:S(2)}, u32[]{:S(2)}) collective-permute-start(bf16[32,16,128]{2,1,0:T(8,128)(2,1)S(1)} %get-tuple-element.20.refs_0_), channel_id=1, source_target_pairs={{0,16},{1,17},{2,18},{3,19},{4,20},{5,21},{6,22},{7,23},{8,24},{9,... | collective-permute-start | bytes 393224 | tf_op jit(solution)/shard_map/ppermute | solution.py:247
  18.2 0.0 collective-permute-done.15.refs_9_
  18.2 0.0 collective-permute-start.4
  18.2 0.0 collective-permute-done.16.refs_10_
  18.2 0.5 collective-permute-start.5
  18.7 0.1 collective-permute-done.17.refs_11_
  18.8 1.2 %collective-permute-done.18.refs_12_ = bf16[32,16,128]{2,1,0:T(8,128)(2,1)S(1)} collective-permute-done((bf16[32,16,128]{2,1,0:T(8,128)(2,1)S(1)}, bf16[32,16,128]{2,1,0:T(8,128)(2,1)S(1)}, u32[]{:S(2)}, u32[]{:S(2)}) %collective-permute-start.18) | collective-permute-done | bytes 131104 | tf_op jit(solution)/shard_map/ppermute | solution.py:247
  20.0 1.7 %collective-permute-start.19 = (bf16[32,16,128]{2,1,0:T(8,128)(2,1)S(1)}, bf16[32,16,128]{2,1,0:T(8,128)(2,1)S(1)}, u32[]{:S(2)}, u32[]{:S(2)}) collective-permute-start(bf16[32,16,128]{2,1,0:T(8,128)(2,1)S(1)} %collective-permute-done.15.refs_9_), channel_id=1, source_target_pairs={{0,8},{1,9},{2,10},{3,11},{4,12},{5,13},{6,14},{7,15},{8,0},{9,1},... | collective-permute-start | bytes 393224 | tf_op jit(solution)/shard_map/ppermute | solution.py:247
  21.7 1.3 %collective-permute-done.7.refs_0_ = bf16[32,16,128]{2,1,0:T(8,128)(2,1)S(1)} collective-permute-done((bf16[32,16,128]{2,1,0:T(8,128)(2,1)S(1)}, bf16[32,16,128]{2,1,0:T(8,128)(2,1)S(1)}, u32[]{:S(2)}, u32[]{:S(2)}) %collective-permute-start.7) | collective-permute-done | bytes 131104 | tf_op jit(solution)/shard_map/ppermute | solution.py:247
  23.0 0.3 collective-permute-start.20
  23.3 0.0 collective-permute-done.4.refs_5_
  23.3 2.9 %collective-permute-start.8 = (bf16[32,16,128]{2,1,0:T(8,128)(2,1)S(1)}, bf16[32,16,128]{2,1,0:T(8,128)(2,1)S(1)}, u32[]{:S(2)}, u32[]{:S(2)}) collective-permute-start(bf16[32,16,128]{2,1,0:T(8,128)(2,1)S(1)} %collective-permute-done.refs_1_), channel_id=1, source_target_pairs={{0,16},{1,17},{2,18},{3,19},{4,20},{5,21},{6,22},{7,23},{8,24},{9,... | collective-permute-start | bytes 393224 | tf_op jit(solution)/shard_map/ppermute | solution.py:247
  26.3 0.0 collective-permute-done.5.refs_6_
  26.3 0.1 collective-permute-start.9
  26.3 2.9 %collective-permute-start.10 = (bf16[32,16,128]{2,1,0:T(8,128)(2,1)S(1)}, bf16[32,16,128]{2,1,0:T(8,128)(2,1)S(1)}, u32[]{:S(2)}, u32[]{:S(2)}) collective-permute-start(bf16[32,16,128]{2,1,0:T(8,128)(2,1)S(1)} %collective-permute-done.2.refs_3_), channel_id=1, source_target_pairs={{0,16},{1,17},{2,18},{3,19},{4,20},{5,21},{6,22},{7,23},{8,24},{9,... | collective-permute-start | bytes 393224 | tf_op jit(solution)/shard_map/ppermute | solution.py:247
  29.2 1.6 %collective-permute-done.19.refs_13_ = bf16[32,16,128]{2,1,0:T(8,128)(2,1)S(1)} collective-permute-done((bf16[32,16,128]{2,1,0:T(8,128)(2,1)S(1)}, bf16[32,16,128]{2,1,0:T(8,128)(2,1)S(1)}, u32[]{:S(2)}, u32[]{:S(2)}) %collective-permute-start.19) | collective-permute-done | bytes 131104 | tf_op jit(solution)/shard_map/ppermute | solution.py:247
  30.8 2.7 %collective-permute-done.20.refs_14_ = bf16[32,16,128]{2,1,0:T(8,128)(2,1)S(1)} collective-permute-done((bf16[32,16,128]{2,1,0:T(8,128)(2,1)S(1)}, bf16[32,16,128]{2,1,0:T(8,128)(2,1)S(1)}, u32[]{:S(2)}, u32[]{:S(2)}) %collective-permute-start.20) | collective-permute-done | bytes 131104 | tf_op jit(solution)/shard_map/ppermute | solution.py:247
  33.5 0.0 collective-permute-start.11
  33.5 5.6 %collective-permute-done.8.refs_1_ = bf16[32,16,128]{2,1,0:T(8,128)(2,1)S(1)} collective-permute-done((bf16[32,16,128]{2,1,0:T(8,128)(2,1)S(1)}, bf16[32,16,128]{2,1,0:T(8,128)(2,1)S(1)}, u32[]{:S(2)}, u32[]{:S(2)}) %collective-permute-start.8) | collective-permute-done | bytes 131104 | tf_op jit(solution)/shard_map/ppermute | solution.py:247
  39.0 0.0 collective-permute-start.12
  39.0 1.8 %collective-permute-done.9.refs_2_ = bf16[32,16,128]{2,1,0:T(8,128)(2,1)S(1)} collective-permute-done((bf16[32,16,128]{2,1,0:T(8,128)(2,1)S(1)}, bf16[32,16,128]{2,1,0:T(8,128)(2,1)S(1)}, u32[]{:S(2)}, u32[]{:S(2)}) %collective-permute-start.9) | collective-permute-done | bytes 131104 | tf_op jit(solution)/shard_map/ppermute | solution.py:247
  40.8 0.0 collective-permute-start.13
  40.8 1.4 %collective-permute-done.10.refs_3_ = bf16[32,16,128]{2,1,0:T(8,128)(2,1)S(1)} collective-permute-done((bf16[32,16,128]{2,1,0:T(8,128)(2,1)S(1)}, bf16[32,16,128]{2,1,0:T(8,128)(2,1)S(1)}, u32[]{:S(2)}, u32[]{:S(2)}) %collective-permute-start.10) | collective-permute-done | bytes 131104 | tf_op jit(solution)/shard_map/ppermute | solution.py:247
  42.2 0.0 collective-permute-start.14
  42.2 1.0 %gates.1 = (f32[16,128,128]{2,1,0:T(8,128)S(1)}, f32[1,128]{1,0:T(1,128)S(1)}, f32[1,128]{1,0:T(1,128)S(1)}, bf16[128,128]{1,0:T(8,128)(2,1)S(1)}, bf16[2,32,64,128]{3,2,1,0:T(8,128)(2,1)S(1)}) custom-call(bf16[2048,128]{1,0:T(8,128)(2,1)S(1)} %get-tuple-element.19.normed_ref, bf16[128,128]{1,0:T(8,128)(2,1)S(1)} %copy-done.1, ...), custom_call_target="tpu_custom_call" | custom-call | tf_op jit(solution)/shard_map/gates/pallas_call | solution.py:287
  43.3 0.0 collective-permute-done.21.refs_15_
  43.3 0.0 collective-permute-done.11.refs_4_
  43.3 0.0 collective-permute-done.13.refs_6_
  43.3 0.2 collective-permute-done.14.refs_7_
  43.6 1.1 %pairs.1 = bf16[8,16,16,128]{3,2,1,0:T(8,128)(2,1)S(1)} custom-call(bf16[2,32,64,128]{3,2,1,0:T(8,128)(2,1)S(1)} %get-tuple-element.24.near_ref, bf16[32,16,128]{2,1,0:T(8,128)(2,1)S(1)} %collective-permute-done.7.refs_0_, bf16[32,16,128]{2,1,0:T(8,128)(2,1)S(1)} %collective-permute-done.8.refs_1_, bf16[32,16,128]{2,1,0:T(8,128)(2,1)S(1)} %collective-permute-done.9.refs_2_, ...), custom_call_target="tpu_custom_call" | custom-call | tf_op jit(solution)/shard_map/pairs/pallas_call | solution.py:310
  44.7 13.4 %all_to_all.5.summed_ref = bf16[8,16,16,128]{3,2,1,0:T(8,128)(2,1)S(1)} all-to-all(bf16[8,16,16,128]{3,2,1,0:T(8,128)(2,1)S(1)} %pairs.1), channel_id=1, replica_groups={{0,1,4,5,8,9,12,13},{2,3,6,7,10,11,14,15},{16,17,20,21,24,25,28,29},{18..., dimensions={0} | all-to-all | bytes 1048576 | tf_op jit(solution)/shard_map/all_to_all | solution.py:323
  58.0 1.7 %output.1 = f32[16,128,128]{2,1,0:T(8,128)} custom-call(bf16[8,16,16,128]{3,2,1,0:T(8,128)(2,1)S(1)} %all_to_all.5.summed_ref, f32[16,128,128]{2,1,0:T(8,128)S(1)} %get-tuple-element.29.gating_ref, f32[1,128]{1,0:T(1,128)S(1)} %get-tuple-element.30.gain_ref, f32[1,128]{1,0:T(1,128)S(1)} %get-tuple-element.31.bias_ref, ...), custom_call_target="tpu_custom_call" | custom-call | tf_op jit(solution)/shard_map/output/pallas_call | solution.py:324
  (8 shorter events, 0.0 us)
Async XLA Ops:
  0.0 7.2 %copy-start = (bf16[128,512]{1,0:T(8,128)(2,1)S(1)}, bf16[128,512]{1,0:T(8,128)(2,1)}, u32[]{:S(2)}) copy-start(bf16[128,512]{1,0:T(8,128)(2,1)} %w_ref.1) | copy-start | bytes 393220
  2.5 4.6 %copy-start.2 = (s32[16,128]{1,0:T(8,128)S(1)}, s32[16,128]{1,0:T(8,128)}, u32[]{:S(2)}) copy-start(s32[16,128]{1,0:T(8,128)} %mask_ref.1) | copy-start | bytes 24580
  2.5 7.4 %collective-permute-start = (bf16[32,16,128]{2,1,0:T(8,128)(2,1)S(1)}, bf16[32,16,128]{2,1,0:T(8,128)(2,1)S(1)}, u32[]{:S(2)}, u32[]{:S(2)}) collective-permute-start(bf16[32,16,128]{2,1,0:T(8,128)(2,1)S(1)} %get-tuple-element.21), channel_id=1, source_target_pairs={{0,1},{1,0},{2,3},{3,2},{4,5},{5,4},{6,7},{7,6},{8,9},{9,8},{10,11... | collective-permute-start | bytes 393224 | tf_op jit(solution)/shard_map/ppermute | solution.py:247
  5.6 6.4 %collective-permute-start.1 = (bf16[32,16,128]{2,1,0:T(8,128)(2,1)S(1)}, bf16[32,16,128]{2,1,0:T(8,128)(2,1)S(1)}, u32[]{:S(2)}, u32[]{:S(2)}) collective-permute-start(bf16[32,16,128]{2,1,0:T(8,128)(2,1)S(1)} %get-tuple-element.22), channel_id=1, source_target_pairs={{0,4},{1,5},{2,6},{3,7},{4,0},{5,1},{6,2},{7,3},{8,12},{9,13},{10,... | collective-permute-start | bytes 393224 | tf_op jit(solution)/shard_map/ppermute | solution.py:247
  7.1 6.7 %collective-permute-start.2 = (bf16[32,16,128]{2,1,0:T(8,128)(2,1)S(1)}, bf16[32,16,128]{2,1,0:T(8,128)(2,1)S(1)}, u32[]{:S(2)}, u32[]{:S(2)}) collective-permute-start(bf16[32,16,128]{2,1,0:T(8,128)(2,1)S(1)} %get-tuple-element.23), channel_id=1, source_target_pairs={{0,5},{1,4},{2,7},{3,6},{4,1},{5,0},{6,3},{7,2},{8,13},{9,12},{10,... | collective-permute-start | bytes 393224 | tf_op jit(solution)/shard_map/ppermute | solution.py:247
  7.2 8.4 %collective-permute-start.3 = (bf16[32,16,128]{2,1,0:T(8,128)(2,1)S(1)}, bf16[32,16,128]{2,1,0:T(8,128)(2,1)S(1)}, u32[]{:S(2)}, u32[]{:S(2)}) collective-permute-start(bf16[32,16,128]{2,1,0:T(8,128)(2,1)S(1)} %get-tuple-element.20.refs_0_), channel_id=1, source_target_pairs={{0,2},{1,3},{2,0},{3,1},{4,6},{5,7},{6,4},{7,5},{8,10},{9,11},{10,... | collective-permute-start | bytes 393224 | tf_op jit(solution)/shard_map/ppermute | solution.py:247
  7.2 35.1 %copy-start.1 = (bf16[128,128]{1,0:T(8,128)(2,1)S(1)}, bf16[128,128]{1,0:T(8,128)(2,1)}, u32[]{:S(2)}) copy-start(bf16[128,128]{1,0:T(8,128)(2,1)} %w_gate_ref.1) | copy-start | bytes 98308
  7.9 10.3 %collective-permute-start.15 = (bf16[32,16,128]{2,1,0:T(8,128)(2,1)S(1)}, bf16[32,16,128]{2,1,0:T(8,128)(2,1)S(1)}, u32[]{:S(2)}, u32[]{:S(2)}) collective-permute-start(bf16[32,16,128]{2,1,0:T(8,128)(2,1)S(1)} %get-tuple-element.26), channel_id=1, source_target_pairs={{0,1},{1,0},{2,3},{3,2},{4,5},{5,4},{6,7},{7,6},{8,9},{9,8},{10,11... | collective-permute-start | bytes 393224 | tf_op jit(solution)/shard_map/ppermute | solution.py:247
  9.9 8.3 %collective-permute-start.16 = (bf16[32,16,128]{2,1,0:T(8,128)(2,1)S(1)}, bf16[32,16,128]{2,1,0:T(8,128)(2,1)S(1)}, u32[]{:S(2)}, u32[]{:S(2)}) collective-permute-start(bf16[32,16,128]{2,1,0:T(8,128)(2,1)S(1)} %get-tuple-element.27), channel_id=1, source_target_pairs={{0,4},{1,5},{2,6},{3,7},{4,0},{5,1},{6,2},{7,3},{8,12},{9,13},{10,... | collective-permute-start | bytes 393224 | tf_op jit(solution)/shard_map/ppermute | solution.py:247
  12.0 6.8 %collective-permute-start.17 = (bf16[32,16,128]{2,1,0:T(8,128)(2,1)S(1)}, bf16[32,16,128]{2,1,0:T(8,128)(2,1)S(1)}, u32[]{:S(2)}, u32[]{:S(2)}) collective-permute-start(bf16[32,16,128]{2,1,0:T(8,128)(2,1)S(1)} %get-tuple-element.28), channel_id=1, source_target_pairs={{0,5},{1,4},{2,7},{3,6},{4,1},{5,0},{6,3},{7,2},{8,13},{9,12},{10,... | collective-permute-start | bytes 393224 | tf_op jit(solution)/shard_map/ppermute | solution.py:247
  13.8 6.2 %collective-permute-start.18 = (bf16[32,16,128]{2,1,0:T(8,128)(2,1)S(1)}, bf16[32,16,128]{2,1,0:T(8,128)(2,1)S(1)}, u32[]{:S(2)}, u32[]{:S(2)}) collective-permute-start(bf16[32,16,128]{2,1,0:T(8,128)(2,1)S(1)} %get-tuple-element.25.refs_8_), channel_id=1, source_target_pairs={{0,8},{1,9},{2,10},{3,11},{4,12},{5,13},{6,14},{7,15},{8,0},{9,1},... | collective-permute-start | bytes 393224 | tf_op jit(solution)/shard_map/ppermute | solution.py:247
  15.6 7.4 %collective-permute-start.7 = (bf16[32,16,128]{2,1,0:T(8,128)(2,1)S(1)}, bf16[32,16,128]{2,1,0:T(8,128)(2,1)S(1)}, u32[]{:S(2)}, u32[]{:S(2)}) collective-permute-start(bf16[32,16,128]{2,1,0:T(8,128)(2,1)S(1)} %get-tuple-element.20.refs_0_), channel_id=1, source_target_pairs={{0,16},{1,17},{2,18},{3,19},{4,20},{5,21},{6,22},{7,23},{8,24},{9,... | collective-permute-start | bytes 393224 | tf_op jit(solution)/shard_map/ppermute | solution.py:247
  18.2 5.2 %collective-permute-start.4 = (bf16[32,16,128]{2,1,0:T(8,128)(2,1)S(1)}, bf16[32,16,128]{2,1,0:T(8,128)(2,1)S(1)}, u32[]{:S(2)}, u32[]{:S(2)}) collective-permute-start(bf16[32,16,128]{2,1,0:T(8,128)(2,1)S(1)} %collective-permute-done.refs_1_), channel_id=1, source_target_pairs={{0,2},{1,3},{2,0},{3,1},{4,6},{5,7},{6,4},{7,5},{8,10},{9,11},{10,... | collective-permute-start | bytes 393224 | tf_op jit(solution)/shard_map/ppermute | solution.py:247
  18.2 8.1 %collective-permute-start.5 = (bf16[32,16,128]{2,1,0:T(8,128)(2,1)S(1)}, bf16[32,16,128]{2,1,0:T(8,128)(2,1)S(1)}, u32[]{:S(2)}, u32[]{:S(2)}) collective-permute-start(bf16[32,16,128]{2,1,0:T(8,128)(2,1)S(1)} %collective-permute-done.1.refs_2_), channel_id=1, source_target_pairs={{0,2},{1,3},{2,0},{3,1},{4,6},{5,7},{6,4},{7,5},{8,10},{9,11},{10,... | collective-permute-start | bytes 393224 | tf_op jit(solution)/shard_map/ppermute | solution.py:247
  18.8 7.5 %collective-permute-start.6 = (bf16[32,16,128]{2,1,0:T(8,128)(2,1)S(1)}, bf16[32,16,128]{2,1,0:T(8,128)(2,1)S(1)}, u32[]{:S(2)}, u32[]{:S(2)}) collective-permute-start(bf16[32,16,128]{2,1,0:T(8,128)(2,1)S(1)} %collective-permute-done.2.refs_3_), channel_id=1, source_target_pairs={{0,2},{1,3},{2,0},{3,1},{4,6},{5,7},{6,4},{7,5},{8,10},{9,11},{10,... | collective-permute-start | bytes 393224 | tf_op jit(solution)/shard_map/ppermute | solution.py:247
  20.0 10.8 %collective-permute-start.19 = (bf16[32,16,128]{2,1,0:T(8,128)(2,1)S(1)}, bf16[32,16,128]{2,1,0:T(8,128)(2,1)S(1)}, u32[]{:S(2)}, u32[]{:S(2)}) collective-permute-start(bf16[32,16,128]{2,1,0:T(8,128)(2,1)S(1)} %collective-permute-done.15.refs_9_), channel_id=1, source_target_pairs={{0,8},{1,9},{2,10},{3,11},{4,12},{5,13},{6,14},{7,15},{8,0},{9,1},... | collective-permute-start | bytes 393224 | tf_op jit(solution)/shard_map/ppermute | solution.py:247
  23.0 10.5 %collective-permute-start.20 = (bf16[32,16,128]{2,1,0:T(8,128)(2,1)S(1)}, bf16[32,16,128]{2,1,0:T(8,128)(2,1)S(1)}, u32[]{:S(2)}, u32[]{:S(2)}) collective-permute-start(bf16[32,16,128]{2,1,0:T(8,128)(2,1)S(1)} %collective-permute-done.16.refs_10_), channel_id=1, source_target_pairs={{0,8},{1,9},{2,10},{3,11},{4,12},{5,13},{6,14},{7,15},{8,0},{9,1},... | collective-permute-start | bytes 393224 | tf_op jit(solution)/shard_map/ppermute | solution.py:247
  23.3 15.7 %collective-permute-start.8 = (bf16[32,16,128]{2,1,0:T(8,128)(2,1)S(1)}, bf16[32,16,128]{2,1,0:T(8,128)(2,1)S(1)}, u32[]{:S(2)}, u32[]{:S(2)}) collective-permute-start(bf16[32,16,128]{2,1,0:T(8,128)(2,1)S(1)} %collective-permute-done.refs_1_), channel_id=1, source_target_pairs={{0,16},{1,17},{2,18},{3,19},{4,20},{5,21},{6,22},{7,23},{8,24},{9,... | collective-permute-start | bytes 393224 | tf_op jit(solution)/shard_map/ppermute | solution.py:247
  26.3 14.6 %collective-permute-start.9 = (bf16[32,16,128]{2,1,0:T(8,128)(2,1)S(1)}, bf16[32,16,128]{2,1,0:T(8,128)(2,1)S(1)}, u32[]{:S(2)}, u32[]{:S(2)}) collective-permute-start(bf16[32,16,128]{2,1,0:T(8,128)(2,1)S(1)} %collective-permute-done.1.refs_2_), channel_id=1, source_target_pairs={{0,16},{1,17},{2,18},{3,19},{4,20},{5,21},{6,22},{7,23},{8,24},{9,... | collective-permute-start | bytes 393224 | tf_op jit(solution)/shard_map/ppermute | solution.py:247
  26.3 15.9 %collective-permute-start.10 = (bf16[32,16,128]{2,1,0:T(8,128)(2,1)S(1)}, bf16[32,16,128]{2,1,0:T(8,128)(2,1)S(1)}, u32[]{:S(2)}, u32[]{:S(2)}) collective-permute-start(bf16[32,16,128]{2,1,0:T(8,128)(2,1)S(1)} %collective-permute-done.2.refs_3_), channel_id=1, source_target_pairs={{0,16},{1,17},{2,18},{3,19},{4,20},{5,21},{6,22},{7,23},{8,24},{9,... | collective-permute-start | bytes 393224 | tf_op jit(solution)/shard_map/ppermute | solution.py:247
  30.8 12.5 %collective-permute-start.21 = (bf16[32,16,128]{2,1,0:T(8,128)(2,1)S(1)}, bf16[32,16,128]{2,1,0:T(8,128)(2,1)S(1)}, u32[]{:S(2)}, u32[]{:S(2)}) collective-permute-start(bf16[32,16,128]{2,1,0:T(8,128)(2,1)S(1)} %collective-permute-done.17.refs_11_), channel_id=1, source_target_pairs={{0,8},{1,9},{2,10},{3,11},{4,12},{5,13},{6,14},{7,15},{8,0},{9,1},... | collective-permute-start | bytes 393224 | tf_op jit(solution)/shard_map/ppermute | solution.py:247
  33.5 9.8 %collective-permute-start.11 = (bf16[32,16,128]{2,1,0:T(8,128)(2,1)S(1)}, bf16[32,16,128]{2,1,0:T(8,128)(2,1)S(1)}, u32[]{:S(2)}, u32[]{:S(2)}) collective-permute-start(bf16[32,16,128]{2,1,0:T(8,128)(2,1)S(1)} %collective-permute-done.7.refs_0_), channel_id=1, source_target_pairs={{0,2},{1,3},{2,0},{3,1},{4,6},{5,7},{6,4},{7,5},{8,10},{9,11},{10,... | collective-permute-start | bytes 393224 | tf_op jit(solution)/shard_map/ppermute | solution.py:247
  39.0 4.3 %collective-permute-start.12 = (bf16[32,16,128]{2,1,0:T(8,128)(2,1)S(1)}, bf16[32,16,128]{2,1,0:T(8,128)(2,1)S(1)}, u32[]{:S(2)}, u32[]{:S(2)}) collective-permute-start(bf16[32,16,128]{2,1,0:T(8,128)(2,1)S(1)} %collective-permute-done.8.refs_1_), channel_id=1, source_target_pairs={{0,2},{1,3},{2,0},{3,1},{4,6},{5,7},{6,4},{7,5},{8,10},{9,11},{10,... | collective-permute-start | bytes 393224 | tf_op jit(solution)/shard_map/ppermute | solution.py:247
  40.8 2.5 %collective-permute-start.13 = (bf16[32,16,128]{2,1,0:T(8,128)(2,1)S(1)}, bf16[32,16,128]{2,1,0:T(8,128)(2,1)S(1)}, u32[]{:S(2)}, u32[]{:S(2)}) collective-permute-start(bf16[32,16,128]{2,1,0:T(8,128)(2,1)S(1)} %collective-permute-done.9.refs_2_), channel_id=1, source_target_pairs={{0,2},{1,3},{2,0},{3,1},{4,6},{5,7},{6,4},{7,5},{8,10},{9,11},{10,... | collective-permute-start | bytes 393224 | tf_op jit(solution)/shard_map/ppermute | solution.py:247
  42.2 1.3 %collective-permute-start.14 = (bf16[32,16,128]{2,1,0:T(8,128)(2,1)S(1)}, bf16[32,16,128]{2,1,0:T(8,128)(2,1)S(1)}, u32[]{:S(2)}, u32[]{:S(2)}) collective-permute-start(bf16[32,16,128]{2,1,0:T(8,128)(2,1)S(1)} %collective-permute-done.10.refs_3_), channel_id=1, source_target_pairs={{0,2},{1,3},{2,0},{3,1},{4,6},{5,7},{6,4},{7,5},{8,10},{9,11},{10,... | collective-permute-start | bytes 393224 | tf_op jit(solution)/shard_map/ppermute | solution.py:247
